TPU v7x, 128 devices: a whole 4x4x4 slice. The times are simulated.
128 devices in a mesh: walk: 8 (over y, x_lo), orb: 16 (over x_hi, z, core).
Axes of the slice: x: 4 (x_hi: 2, x_lo: 2; x = x_hi * 2 + x_lo), y: 4, z: 4, core: 2. Of those that a mesh axis runs over, the one named last changes fastest.
Arguments:
- coefficients: bfloat16 [4096, 4096], P(None, 'orb'), may hold values from -6 to 6
- inverse: bfloat16 [8, 1024, 1024], P('walk', 'orb'), may hold values from -0.005859375 to 0.005859375
- cell_index: int32 [8, 3, 1024], P('walk'), may hold values from 0 to 15
- fraction: float32 [8, 3, 1024], P('walk'), may hold values from 0 to 1
- energies: float32 [8], P('walk'), may hold values from -8 to 8
- weights: float32 [8], P('walk'), may hold values from 0.5 to 2
- occupied: int32 [1024], replicated, may hold values from 0 to 4095, as said below
Outputs:
- gradient: float32 [1024, 4096], P('walk', 'orb')
Inputs may be any that keep to these rules, and one draw needn't show every extreme that they name: `occupied`: 1024 distinct orbital indices; every block of 256 consecutive orbital indices holds at most 96 of them, and some block holds exactly 96.
All inputs are finite; a program needn't handle non-finite values.
Results may differ from a plain program's by a relative error of at most 0.019.
Values may be sent and summed in bfloat16 or wider, within the bound.
No kernel may reach another device: no remote copies, remote signals or barrier semaphores. Data moves between devices by JAX's collectives and lax.ppermute only.
A program may use at most 64 MiB of HBM per device.

v0:
```python
import functools

import jax
import jax.numpy as jnp
from jax import lax
from jax.experimental import pallas as pl
from jax.experimental.pallas import tpu as pltpu
from jax.sharding import Mesh
from jax.sharding import PartitionSpec as P


GRID = 16
PLANE = GRID * GRID
TILE = 256
BF16 = jnp.bfloat16
F32 = jnp.float32


def mm(left, right):
    return jnp.dot(left, right, preferred_element_type=F32)


def mm_nt(left, right):
    return lax.dot_general(left, right, (((1,), (1,)), ((), ())), preferred_element_type=F32)


def mm_tn(left, right):
    return lax.dot_general(left, right, (((0,), (0,)), ((), ())), preferred_element_type=F32)


def dense_rows(cell, frac):
    remain = 1.0 - frac
    square = frac * frac
    cubed = square * frac
    sixth = 1.0 / 6.0
    values = [
        remain * remain * remain * sixth,
        (3.0 * cubed - 6.0 * square + 4.0) * sixth,
        (-3.0 * cubed + 3.0 * square + 3.0 * frac + 1.0) * sixth,
        cubed * sixth,
    ]
    curves = [remain, 3.0 * frac - 2.0, 1.0 - 3.0 * frac, frac]
    line = lax.broadcasted_iota(jnp.int32, (GRID, cell.shape[1]), 0)
    tap = (line - cell + (GRID + 1)) & (GRID - 1)
    value = jnp.zeros((GRID, cell.shape[1]), F32)
    curve = jnp.zeros((GRID, cell.shape[1]), F32)
    for a in range(4):
        value = jnp.where(tap == a, values[a], value)
        curve = jnp.where(tap == a, curves[a], curve)
    return value, curve


def slot_tables(me, occ, shards, width, slots):
    owner = lax.broadcasted_iota(jnp.int32, (shards, occ.shape[1]), 0) == lax.div(occ, width)
    count = owner.astype(jnp.int32)
    lane = lax.broadcasted_iota(jnp.int32, count.shape, 1)
    step = 1
    while step < occ.shape[1]:
        count = count + jnp.where(lane >= step, pltpu.roll(count, step, 1), 0)
        step *= 2
    rank = jnp.sum(jnp.where(owner, count - 1, 0), axis=0, keepdims=True)
    slot = lax.div(occ, width) * slots + rank
    placed = lax.broadcasted_iota(jnp.int32, (slots, occ.shape[1]), 0) == slot - me * slots
    column = lax.broadcasted_iota(jnp.int32, (width, occ.shape[1]), 0) == occ - me * width
    picker = mm_nt(placed.astype(F32).astype(BF16), column.astype(F32).astype(BF16)).astype(BF16)
    return slot, picker


def expand(rows, weights):
    return jnp.concatenate([rows[g:g + 1, :] * weights for g in range(GRID)], axis=0)


def eval_kernel(*refs, shards, slots, first, electrons):
    if first == 0:
        me_ref, coef_ref, cell_ref, frac_ref, occ_ref, val_ref, lap_ref, lapt_ref, turned_ref, picker_ref, slot_ref, *weight_refs = refs
    else:
        turned_ref, picker_ref, cell_ref, frac_ref, val_ref, lap_ref, lapt_ref, *weight_refs = refs

    def build(t, value_ref, lap_ref):
        here = slice(first + t * TILE, first + (t + 1) * TILE)
        vx, cx = dense_rows(cell_ref[0, :, here], frac_ref[0, :, here])
        vy, cy = dense_rows(cell_ref[1, :, here], frac_ref[1, :, here])
        vz, cz = dense_rows(cell_ref[2, :, here], frac_ref[2, :, here])
        value = expand(vy, vz)
        curve = expand(cy, vz) + expand(vy, cz)
        for g in range(GRID):
            x_value, x_curve = vx[g:g + 1, :], cx[g:g + 1, :]
            value_ref[g * PLANE:(g + 1) * PLANE, :] = (x_value * value).astype(BF16)
            lap_ref[g * PLANE:(g + 1) * PLANE, :] = (x_curve * value + x_value * curve).astype(BF16)

    def product(t, value_w, lap_w):
        here = slice(t * TILE, (t + 1) * TILE)
        val_ref[:, here] = mm(turned_ref[...], value_w[...]).astype(BF16)
        lap = mm(turned_ref[...], lap_w[...]).astype(BF16)
        lap_ref[:, here] = lap
        lapt_ref[:, here] = mm(picker_ref[...], lap).astype(BF16)

    tiles = electrons // TILE
    build(0, weight_refs[0], weight_refs[1])
    if first == 0:
        slot, picker = slot_tables(me_ref[0], occ_ref[...], shards, coef_ref.shape[1], slots)
        slot_ref[...] = slot
        picker_ref[...] = picker
        for g in range(GRID):
            turned_ref[:, g * PLANE:(g + 1) * PLANE] = jnp.transpose(coef_ref[g * PLANE:(g + 1) * PLANE, :])
    for t in range(tiles):
        if t + 1 < tiles:
            build(t + 1, *weight_refs[2 * ((t + 1) % 2):][:2])
        product(t, *weight_refs[2 * (t % 2):][:2])


def owners(me_ref, z_count):
    me = me_ref[0]
    core = lax.rem(me, 2)
    z = lax.rem(lax.div(me, 2), z_count)
    plane = lax.div(me, 2 * z_count)
    chips = [(p * z_count + lax.rem(z + dz, z_count)) * 2
             for dz in (0, z_count - 1, 1, 2) for p in (plane, 1 - plane)]
    return [chip + core for chip in chips] + [chip + 1 - core for chip in chips]


def in_order(out_ref, value, blocks, size):
    for j, block in enumerate(blocks):
        start = pl.multiple_of(block * size, size)
        out_ref[pl.ds(start, size), :] = value[j * size:(j + 1) * size].astype(out_ref.dtype)


def inverse_times(inv_refs, right, out_ref, order, size):
    first = 0
    for ref in inv_refs:
        count = ref.shape[0] // size
        in_order(out_ref, mm_nt(ref[...], right), order[first:first + count], size)
        first += count


def ratio_kernel(me_ref, *refs, parts, z_count, slots, size):
    inv_refs, val_refs = refs[:parts], refs[parts:-3]
    slot_ref, rows_ref, ratio_ref = refs[-3:]
    order = owners(me_ref, z_count)
    val = jnp.concatenate([ref[...] for ref in val_refs], axis=1)
    inverse_times(inv_refs, val, ratio_ref, order, size)
    ratio = ratio_ref[...]
    slot = slot_ref[...]
    for j in range(0, len(order), 2):
        ids = lax.broadcasted_iota(jnp.int32, (slots, slot.shape[1]), 0)
        pick = jnp.concatenate([(ids + block * slots == slot).astype(F32) for block in order[j:j + 2]], axis=0)
        rows_ref[j * slots:(j + 2) * slots, :] = mm(pick.astype(BF16), ratio).astype(BF16)


def finish_kernel(me_ref, energy_ref, weight_ref, *refs, parts, halves, z_count, size):
    inv_refs, lapt_refs = refs[:parts], refs[parts:2 * parts]
    rows_ref = refs[2 * parts]
    val_refs, lap_refs = refs[2 * parts + 1:2 * parts + 1 + halves], refs[2 * parts + 1 + halves:2 * parts + 1 + 2 * halves]
    out_ref = refs[-1]
    total = None
    first = 0
    for ref in lapt_refs:
        term = mm_tn(rows_ref[first:first + ref.shape[0], :], ref[...])
        total = term if total is None else total + term
        first += ref.shape[0]
    val = jnp.concatenate([ref[...] for ref in val_refs], axis=1).astype(F32)
    lap = jnp.concatenate([ref[...] for ref in lap_refs], axis=1).astype(F32)
    mixed = (weight_ref[0] * (energy_ref[0] * val - 0.5 * (lap - total))).astype(BF16)
    inverse_times(inv_refs, mixed, out_ref, owners(me_ref, z_count), size)


VMEM = pl.BlockSpec(memory_space=pltpu.VMEM)
SMEM = pl.BlockSpec(memory_space=pltpu.SMEM)


def ring_swap(piece):
    return lax.ppermute(piece, "xh", [(0, 1), (1, 0)])


def ring_pass(piece, shift):
    count = lax.axis_size("z")
    return lax.ppermute(piece, "z", [(i, (i + shift) % count) for i in range(count)])


def core_swap(piece):
    return lax.ppermute(piece, "core", [(0, 1), (1, 0)])


def ring_parts(pair):
    half = pair.shape[0] // 2
    below = ring_pass(pair, 1)
    above = ring_pass(pair, -1)
    far_first = ring_pass(below[:half], 1)
    far_second = ring_pass(above[half:], -1)
    return [pair, below, above, far_first, far_second]


def gradient(coefficients, inverse, cell_index, fraction, energies, weights, occupied):
    cells, width = coefficients.shape
    _, rows, electrons = inverse.shape
    z_count = lax.axis_size("z")
    shards = 2 * z_count * 2
    slots = 3 * electrons // (2 * shards)
    xh, z, core = lax.axis_index("xh"), lax.axis_index("z"), lax.axis_index("core")
    me = ((xh * z_count + z) * 2 + core).astype(jnp.int32).reshape(1)

    out = lambda *shape_dtype: jax.ShapeDtypeStruct(*shape_dtype)
    halves = 2
    part = electrons // halves

    def evaluate(h, *operands):
        results = [out((width, part), BF16), out((width, part), BF16), out((slots, part), BF16)]
        if h == 0:
            results += [out((width, cells), BF16), out((slots, width), BF16), out((1, electrons), jnp.int32)]
        return pl.pallas_call(
            functools.partial(eval_kernel, shards=shards, slots=slots, first=h * part, electrons=part),
            out_shape=results,
            in_specs=[SMEM] + [VMEM] * 4 if h == 0 else [VMEM] * 4,
            out_specs=[VMEM] * len(results),
            scratch_shapes=[pltpu.VMEM((cells, TILE), BF16)] * 4,
            compiler_params=pltpu.CompilerParams(vmem_limit_bytes=32 * 1024 * 1024),
            cost_estimate=pl.CostEstimate(
                flops=4 * part * cells * width, bytes_accessed=4 * cells * width, transcendentals=0
            ),
            name="evaluate",
        )(*operands)

    cell_index, fraction = jnp.transpose(cell_index, (1, 0, 2)), jnp.transpose(fraction, (1, 0, 2))
    mine = inverse.reshape(rows, electrons)
    inv_far = ring_swap(mine)
    inv_pair = jnp.concatenate([mine, inv_far], axis=0)
    inv_ring = ring_parts(inv_pair)
    val_a, lap_a, lapt_a, turned, picker, slot = evaluate(
        0, me, coefficients, cell_index, fraction, occupied.reshape(1, electrons)
    )
    val_b, lap_b, lapt_b = evaluate(1, turned, picker, cell_index, fraction)
    vals, laps = [val_a, val_b], [lap_a, lap_b]
    lapt_mine = jnp.concatenate([lapt_a, lapt_b], axis=1)
    lapt_far = ring_swap(lapt_mine)
    lap_pair = jnp.concatenate([lapt_mine, lapt_far], axis=0)
    lap_ring = ring_parts(lap_pair)
    inv_all = inv_ring + [core_swap(piece) for piece in inv_ring]
    lap_all = lap_ring + [core_swap(piece) for piece in lap_ring]
    parts = len(inv_all)

    ratio_rows, _ = pl.pallas_call(
        functools.partial(ratio_kernel, parts=parts, z_count=z_count, slots=slots, size=rows),
        out_shape=[out((shards * slots, width), BF16), out((electrons, width), BF16)],
        in_specs=[SMEM] + [VMEM] * (parts + 3),
        out_specs=[VMEM] * 2,
        compiler_params=pltpu.CompilerParams(vmem_limit_bytes=24 * 1024 * 1024),
        cost_estimate=pl.CostEstimate(
            flops=5 * electrons * electrons * width, bytes_accessed=4 * electrons * electrons, transcendentals=0
        ),
        name="ratio",
    )(me, *inv_all, *vals, slot)

    partial = pl.pallas_call(
        functools.partial(finish_kernel, parts=parts, halves=halves, z_count=z_count, size=rows),
        out_shape=out((electrons, width), BF16),
        in_specs=[SMEM] * 3 + [VMEM] * (2 * parts + 1 + 2 * halves),
        out_specs=VMEM,
        compiler_params=pltpu.CompilerParams(vmem_limit_bytes=32 * 1024 * 1024),
        cost_estimate=pl.CostEstimate(
            flops=5 * electrons * electrons * width, bytes_accessed=8 * electrons * electrons, transcendentals=0
        ),
        name="finish",
    )(me, energies, weights, *inv_all, *lap_all, ratio_rows, *vals, *laps)

    walkers = ("y", "xl")
    count = lax.axis_size(walkers)
    blocks = lax.all_to_all(partial.reshape(count, electrons // count, width), walkers, 0, 0, tiled=True)
    return jnp.sum(blocks.astype(F32), axis=0)


def solution(mesh):
    fine = Mesh(mesh.devices.reshape(4, 2, 2, 4, 2), ("y", "xl", "xh", "z", "core"))
    walk, orb = ("y", "xl"), ("xh", "z", "core")
    in_specs = (
        P(None, orb),
        P(walk, orb, None),
        P(walk, None, None),
        P(walk, None, None),
        P(walk),
        P(walk),
        P(),
    )
    return jax.shard_map(gradient, mesh=fine, in_specs=in_specs, out_specs=P(walk, orb), check_vma=False)
```

profile of v0, /device:TPU:0, one launch (start us, length us, event | category | flops | bytes accessed | tf_op | source)
XLA Modules:
  0.0 70.6 jit_solution(13573748479426129758)
XLA Ops:
  0.0 3.1 %collective-permute-start = (bf16[64,1024]{1,0:T(8,128)(2,1)}, bf16[64,1024]{1,0:T(8,128)(2,1)S(1)}, u32[]{:S(2)}, u32[]{:S(2)}) collective-permute-start(bf16[64,1024]{1,0:T(8,128)(2,1)} %bitcast.12), channel_id=1, source_target_pairs={{0,8},{8,0},{1,9},{9,1},{2,10},{10,2},{3,11},{11,3},{4,12},{12,4},... | collective-permute-start | bytes 393224 | tf_op jit(solution)/shard_map/ppermute | solution.py:172
  3.1 1.6 %copy-done = bf16[4096,256]{1,0:T(8,128)(2,1)S(1)} copy-done((bf16[4096,256]{1,0:T(8,128)(2,1)S(1)}, bf16[4096,256]{1,0:T(8,128)(2,1)}, u32[]{:S(2)}) %copy-start) | copy-done | bytes 2097176
  4.7 0.7 copy-done.1
  5.4 0.7 copy-done.3
  6.1 0.7 copy-done.5
  6.8 3.8 %evaluate.2 = (bf16[256,512]{1,0:T(8,128)(2,1)S(1)}, bf16[256,512]{1,0:T(8,128)(2,1)S(1)}, bf16[96,512]{1,0:T(8,128)(2,1)S(1)}, bf16[256,4096]{1,0:T(8,128)(2,1)...) custom-call(s32[1]{0:T(128)} %bitcast.refs_0_.me_ref, bf16[4096,256]{1,0:T(8,128)(2,1)S(1)} %copy-done, ...), custom_call_target="tpu_custom_call" | custom-call | flops 2147483648 | bytes 4194304 | tf_op jit(solution)/shard_map/evaluate/pallas_call | solution.py:210
  10.7 2.9 %evaluate.3 = (bf16[256,512]{1,0:T(8,128)(2,1)S(1)}, bf16[256,512]{1,0:T(8,128)(2,1)S(1)}, bf16[96,512]{1,0:T(8,128)(2,1)S(1)}) custom-call(bf16[256,4096]{1,0:T(8,128)(2,1)S(1)} %get-tuple-element.16.refs_0_, bf16[96,256]{1,0:T(8,128)(2,1)S(1)} %get-tuple-element.17.refs_1_, s32[3,1,1024]{2,1,0:T(1,128)S(1)} %bitcast.8, f32[3,1,1024]{2,1,0:T(1,128)S(1)} %bitcast.10), custom_call_target="tpu_custom_call" | custom-call | flops 2147483648 | bytes 4194304 | tf_op jit(solution)/shard_map/evaluate/pallas_call | solution.py:210
  14.2 2.1 %collective-permute-start.1 = (bf16[128,1024]{1,0:T(8,128)(2,1)S(1)}, bf16[128,1024]{1,0:T(8,128)(2,1)S(1)}, u32[]{:S(2)}, u32[]{:S(2)}) collective-permute-start(bf16[128,1024]{1,0:T(8,128)(2,1)S(1)} %pad_maximum_fusion.1.refs_0_), channel_id=1, source_target_pairs={{0,2},{2,4},{4,6},{6,0},{1,3},{3,5},{5,7},{7,1},{8,10},{10,12},{12... | collective-permute-start | bytes 786440 | tf_op jit(solution)/shard_map/ppermute | solution.py:177
  16.3 2.2 %collective-permute-start.2 = (bf16[128,1024]{1,0:T(8,128)(2,1)S(1)}, bf16[128,1024]{1,0:T(8,128)(2,1)S(1)}, u32[]{:S(2)}, u32[]{:S(2)}) collective-permute-start(bf16[128,1024]{1,0:T(8,128)(2,1)S(1)} %pad_maximum_fusion.1.refs_0_), channel_id=1, source_target_pairs={{0,6},{2,0},{4,2},{6,4},{1,7},{3,1},{5,3},{7,5},{8,14},{10,8},{12,... | collective-permute-start | bytes 786440 | tf_op jit(solution)/shard_map/ppermute | solution.py:177
  18.5 3.1 %collective-permute-done.10 = bf16[96,1024]{1,0:T(8,128)(2,1)S(1)} collective-permute-done((bf16[96,1024]{1,0:T(8,128)(2,1)S(1)}, bf16[96,1024]{1,0:T(8,128)(2,1)S(1)}, u32[]{:S(2)}, u32[]{:S(2)}) %collective-permute-start.10) | collective-permute-done | bytes 196640 | tf_op jit(solution)/shard_map/ppermute | solution.py:172
  21.6 2.0 %collective-permute-start.11 = (bf16[192,1024]{1,0:T(8,128)(2,1)S(1)}, bf16[192,1024]{1,0:T(8,128)(2,1)S(1)}, u32[]{:S(2)}, u32[]{:S(2)}) collective-permute-start(bf16[192,1024]{1,0:T(8,128)(2,1)S(1)} %pad_maximum_fusion.refs_10_), channel_id=1, source_target_pairs={{0,2},{2,4},{4,6},{6,0},{1,3},{3,5},{5,7},{7,1},{8,10},{10,12},{12... | collective-permute-start | bytes 1179656 | tf_op jit(solution)/shard_map/ppermute | solution.py:177
  23.6 2.2 %collective-permute-start.12 = (bf16[192,1024]{1,0:T(8,128)(2,1)S(1)}, bf16[192,1024]{1,0:T(8,128)(2,1)S(1)}, u32[]{:S(2)}, u32[]{:S(2)}) collective-permute-start(bf16[192,1024]{1,0:T(8,128)(2,1)S(1)} %pad_maximum_fusion.refs_10_), channel_id=1, source_target_pairs={{0,6},{2,0},{4,2},{6,4},{1,7},{3,1},{5,3},{7,5},{8,14},{10,8},{12,... | collective-permute-start | bytes 1179656 | tf_op jit(solution)/shard_map/ppermute | solution.py:177
  26.0 3.3 %collective-permute-start.4 = (bf16[64,1024]{1,0:T(8,128)(2,1)S(1)}, bf16[64,1024]{1,0:T(8,128)(2,1)S(1)}, u32[]{:S(2)}, u32[]{:S(2)}) collective-permute-start(bf16[64,1024]{1,0:T(8,128)(2,1)S(1)} %slice.17), channel_id=1, source_target_pairs={{0,6},{2,0},{4,2},{6,4},{1,7},{3,1},{5,3},{7,5},{8,14},{10,8},{12,... | collective-permute-start | bytes 393224 | tf_op jit(solution)/shard_map/ppermute | solution.py:177
  29.2 7.3 %collective-permute-done.3.refs_3_ = bf16[64,1024]{1,0:T(8,128)(2,1)S(1)} collective-permute-done((bf16[64,1024]{1,0:T(8,128)(2,1)S(1)}, bf16[64,1024]{1,0:T(8,128)(2,1)S(1)}, u32[]{:S(2)}, u32[]{:S(2)}) %collective-permute-start.3) | collective-permute-done | bytes 131104 | tf_op jit(solution)/shard_map/ppermute | solution.py:177
  36.5 0.5 collective-permute-start.7
  37.8 0.9 %collective-permute-done.8.refs_8_ = bf16[64,1024]{1,0:T(8,128)(2,1)S(1)} collective-permute-done((bf16[64,1024]{1,0:T(8,128)(2,1)S(1)}, bf16[64,1024]{1,0:T(8,128)(2,1)S(1)}, u32[]{:S(2)}, u32[]{:S(2)}) %collective-permute-start.8) | collective-permute-done | bytes 131104 | tf_op jit(solution)/shard_map/ppermute | solution.py:181
  38.6 0.9 %collective-permute-start.13 = (bf16[96,1024]{1,0:T(8,128)(2,1)S(1)}, bf16[96,1024]{1,0:T(8,128)(2,1)S(1)}, u32[]{:S(2)}, u32[]{:S(2)}) collective-permute-start(bf16[96,1024]{1,0:T(8,128)(2,1)S(1)} %slice.18), channel_id=1, source_target_pairs={{0,2},{2,4},{4,6},{6,0},{1,3},{3,5},{5,7},{7,1},{8,10},{10,12},{12... | collective-permute-start | bytes 589832 | tf_op jit(solution)/shard_map/ppermute | solution.py:177
  39.5 2.3 %collective-permute-start.14 = (bf16[96,1024]{1,0:T(8,128)(2,1)S(1)}, bf16[96,1024]{1,0:T(8,128)(2,1)S(1)}, u32[]{:S(2)}, u32[]{:S(2)}) collective-permute-start(bf16[96,1024]{1,0:T(8,128)(2,1)S(1)} %slice.19), channel_id=1, source_target_pairs={{0,6},{2,0},{4,2},{6,4},{1,7},{3,1},{5,3},{7,5},{8,14},{10,8},{12,... | collective-permute-start | bytes 589832 | tf_op jit(solution)/shard_map/ppermute | solution.py:177
  42.4 4.4 %collective-permute-done.13.refs_13_ = bf16[96,1024]{1,0:T(8,128)(2,1)S(1)} collective-permute-done((bf16[96,1024]{1,0:T(8,128)(2,1)S(1)}, bf16[96,1024]{1,0:T(8,128)(2,1)S(1)}, u32[]{:S(2)}, u32[]{:S(2)}) %collective-permute-start.13) | collective-permute-done | bytes 196640 | tf_op jit(solution)/shard_map/ppermute | solution.py:177
  46.8 0.5 collective-permute-start.19
  48.6 3.4 %ratio.1 = (bf16[1536,256]{1,0:T(8,128)(2,1)S(1)}, bf16[1024,256]{1,0:T(8,128)(2,1)}) custom-call(s32[1]{0:T(128)} %bitcast.refs_0_.me_ref, bf16[128,1024]{1,0:T(8,128)(2,1)S(1)} %pad_maximum_fusion.1.refs_0_, bf16[128,1024]{1,0:T(8,128)(2,1)S(1)} %collective-permute-done.1.refs_1_, bf16[128,1024]{1,0:T(8,128)(2,1)S(1)} %collective-permute-done.2.refs_2_, ...), custom_call_target="tpu_custom_call" | custom-call | flops 1342177280 | bytes 4194304 | tf_op jit(solution)/shard_map/ratio/pallas_call | solution.py:241
  52.0 3.3 %finish.1 = bf16[1024,256]{1,0:T(8,128)(2,1)S(1)} custom-call(s32[1]{0:T(128)} %bitcast.refs_0_.me_ref, f32[1]{0:T(128)S(6)} %copy.9.energy_ref, f32[1]{0:T(128)S(6)} %copy.10.weight_ref, bf16[128,1024]{1,0:T(8,128)(2,1)S(1)} %pad_maximum_fusion.1.refs_0_, bf16[128,1024]{1,0:T(8,128)(2,1)S(1)} %collective-permute-done.1.refs_1_, ...), custom_call_target="tpu_custom_call" | custom-call | flops 1342177280 | bytes 8388608 | tf_op jit(solution)/shard_map/finish/pallas_call | solution.py:253
  55.3 14.6 %all_to_all.5 = bf16[8,128,256]{2,1,0:T(8,128)(2,1)S(1)} all-to-all(bf16[8,128,256]{2,1,0:T(8,128)(2,1)S(1)} %bitcast.6), channel_id=1, replica_groups=mesh['y'=4,'xl'=2,'xh'=2,'z'=4,'core'=2] {'y','xl'}, dimensions={0} | all-to-all | bytes 1048576 | tf_op jit(solution)/shard_map/all_to_all | solution.py:267
  69.8 0.7 %convert_reduce_fusion = f32[128,256]{1,0:T(8,128)} fusion(bf16[8,128,256]{2,1,0:T(8,128)(2,1)S(1)} %all_to_all.5), kind=kLoop, calls=%fused_computation | loop fusion | flops 491520 | bytes 655360 | tf_op jit(solution)/shard_map/reduce_sum | solution.py:268
  (44 shorter events, 1.9 us)
Async XLA Ops:
  0.0 14.1 %collective-permute-start = (bf16[64,1024]{1,0:T(8,128)(2,1)}, bf16[64,1024]{1,0:T(8,128)(2,1)S(1)}, u32[]{:S(2)}, u32[]{:S(2)}) collective-permute-start(bf16[64,1024]{1,0:T(8,128)(2,1)} %bitcast.12), channel_id=1, source_target_pairs={{0,8},{8,0},{1,9},{9,1},{2,10},{10,2},{3,11},{11,3},{4,12},{12,4},... | collective-permute-start | bytes 393224 | tf_op jit(solution)/shard_map/ppermute | solution.py:172
  3.1 1.6 %copy-start = (bf16[4096,256]{1,0:T(8,128)(2,1)S(1)}, bf16[4096,256]{1,0:T(8,128)(2,1)}, u32[]{:S(2)}) copy-start(bf16[4096,256]{1,0:T(8,128)(2,1)} %refs_1_.1) | copy-start | bytes 6291460
  6.8 3.8 %copy-start.2 = (s32[1,3,1024]{2,0,1:T(1,128)S(1)}, s32[1,3,1024]{2,0,1:T(1,128)}, u32[]{:S(2)}) copy-start(s32[1,3,1024]{2,0,1:T(1,128)} %param.9) | copy-start | bytes 36868
  6.8 3.8 %copy-start.4 = (f32[1,3,1024]{2,0,1:T(1,128)S(1)}, f32[1,3,1024]{2,0,1:T(1,128)}, u32[]{:S(2)}) copy-start(f32[1,3,1024]{2,0,1:T(1,128)} %param.10) | copy-start | bytes 36868
  10.7 3.5 %copy-start.6 = (bf16[1,64,1024]{2,1,0:T(8,128)(2,1)S(1)}, bf16[1,64,1024]{2,1,0:T(8,128)(2,1)}, u32[]{:S(2)}) copy-start(bf16[1,64,1024]{2,1,0:T(8,128)(2,1)} %param.8) | copy-start | bytes 393220
  13.7 7.9 %collective-permute-start.10 = (bf16[96,1024]{1,0:T(8,128)(2,1)S(1)}, bf16[96,1024]{1,0:T(8,128)(2,1)S(1)}, u32[]{:S(2)}, u32[]{:S(2)}) collective-permute-start(bf16[96,1024]{1,0:T(8,128)(2,1)S(1)} %constant_dynamic-update-slice_fusion), channel_id=1, source_target_pairs={{0,8},{8,0},{1,9},{9,1},{2,10},{10,2},{3,11},{11,3},{4,12},{12,4},... | collective-permute-start | bytes 589832 | tf_op jit(solution)/shard_map/ppermute | solution.py:172
  14.2 11.7 %collective-permute-start.1 = (bf16[128,1024]{1,0:T(8,128)(2,1)S(1)}, bf16[128,1024]{1,0:T(8,128)(2,1)S(1)}, u32[]{:S(2)}, u32[]{:S(2)}) collective-permute-start(bf16[128,1024]{1,0:T(8,128)(2,1)S(1)} %pad_maximum_fusion.1.refs_0_), channel_id=1, source_target_pairs={{0,2},{2,4},{4,6},{6,0},{1,3},{3,5},{5,7},{7,1},{8,10},{10,12},{12... | collective-permute-start | bytes 786440 | tf_op jit(solution)/shard_map/ppermute | solution.py:177
  16.3 9.7 %collective-permute-start.2 = (bf16[128,1024]{1,0:T(8,128)(2,1)S(1)}, bf16[128,1024]{1,0:T(8,128)(2,1)S(1)}, u32[]{:S(2)}, u32[]{:S(2)}) collective-permute-start(bf16[128,1024]{1,0:T(8,128)(2,1)S(1)} %pad_maximum_fusion.1.refs_0_), channel_id=1, source_target_pairs={{0,6},{2,0},{4,2},{6,4},{1,7},{3,1},{5,3},{7,5},{8,14},{10,8},{12,... | collective-permute-start | bytes 786440 | tf_op jit(solution)/shard_map/ppermute | solution.py:177
  21.6 15.4 %collective-permute-start.11 = (bf16[192,1024]{1,0:T(8,128)(2,1)S(1)}, bf16[192,1024]{1,0:T(8,128)(2,1)S(1)}, u32[]{:S(2)}, u32[]{:S(2)}) collective-permute-start(bf16[192,1024]{1,0:T(8,128)(2,1)S(1)} %pad_maximum_fusion.refs_10_), channel_id=1, source_target_pairs={{0,2},{2,4},{4,6},{6,0},{1,3},{3,5},{5,7},{7,1},{8,10},{10,12},{12... | collective-permute-start | bytes 1179656 | tf_op jit(solution)/shard_map/ppermute | solution.py:177
  23.6 13.5 %collective-permute-start.12 = (bf16[192,1024]{1,0:T(8,128)(2,1)S(1)}, bf16[192,1024]{1,0:T(8,128)(2,1)S(1)}, u32[]{:S(2)}, u32[]{:S(2)}) collective-permute-start(bf16[192,1024]{1,0:T(8,128)(2,1)S(1)} %pad_maximum_fusion.refs_10_), channel_id=1, source_target_pairs={{0,6},{2,0},{4,2},{6,4},{1,7},{3,1},{5,3},{7,5},{8,14},{10,8},{12,... | collective-permute-start | bytes 1179656 | tf_op jit(solution)/shard_map/ppermute | solution.py:177
  25.8 10.7 %collective-permute-start.3 = (bf16[64,1024]{1,0:T(8,128)(2,1)S(1)}, bf16[64,1024]{1,0:T(8,128)(2,1)S(1)}, u32[]{:S(2)}, u32[]{:S(2)}) collective-permute-start(bf16[64,1024]{1,0:T(8,128)(2,1)S(1)} %slice.16), channel_id=1, source_target_pairs={{0,2},{2,4},{4,6},{6,0},{1,3},{3,5},{5,7},{7,1},{8,10},{10,12},{12... | collective-permute-start | bytes 393224 | tf_op jit(solution)/shard_map/ppermute | solution.py:177
  26.0 10.6 %collective-permute-start.4 = (bf16[64,1024]{1,0:T(8,128)(2,1)S(1)}, bf16[64,1024]{1,0:T(8,128)(2,1)S(1)}, u32[]{:S(2)}, u32[]{:S(2)}) collective-permute-start(bf16[64,1024]{1,0:T(8,128)(2,1)S(1)} %slice.17), channel_id=1, source_target_pairs={{0,6},{2,0},{4,2},{6,4},{1,7},{3,1},{5,3},{7,5},{8,14},{10,8},{12,... | collective-permute-start | bytes 393224 | tf_op jit(solution)/shard_map/ppermute | solution.py:177
  29.2 8.4 %collective-permute-start.5 = (bf16[128,1024]{1,0:T(8,128)(2,1)S(1)}, bf16[128,1024]{1,0:T(8,128)(2,1)S(1)}, u32[]{:S(2)}, u32[]{:S(2)}) collective-permute-start(bf16[128,1024]{1,0:T(8,128)(2,1)S(1)} %pad_maximum_fusion.1.refs_0_), channel_id=1, source_target_pairs={{0,1},{1,0},{2,3},{3,2},{4,5},{5,4},{6,7},{7,6},{8,9},{9,8},{10,11... | collective-permute-start | bytes 786440 | tf_op jit(solution)/shard_map/ppermute | solution.py:181
  36.5 5.3 %collective-permute-start.6 = (bf16[128,1024]{1,0:T(8,128)(2,1)S(1)}, bf16[128,1024]{1,0:T(8,128)(2,1)S(1)}, u32[]{:S(2)}, u32[]{:S(2)}) collective-permute-start(bf16[128,1024]{1,0:T(8,128)(2,1)S(1)} %collective-permute-done.1.refs_1_), channel_id=1, source_target_pairs={{0,1},{1,0},{2,3},{3,2},{4,5},{5,4},{6,7},{7,6},{8,9},{9,8},{10,11... | collective-permute-start | bytes 786440 | tf_op jit(solution)/shard_map/ppermute | solution.py:181
  36.5 5.3 %collective-permute-start.7 = (bf16[128,1024]{1,0:T(8,128)(2,1)S(1)}, bf16[128,1024]{1,0:T(8,128)(2,1)S(1)}, u32[]{:S(2)}, u32[]{:S(2)}) collective-permute-start(bf16[128,1024]{1,0:T(8,128)(2,1)S(1)} %collective-permute-done.2.refs_2_), channel_id=1, source_target_pairs={{0,1},{1,0},{2,3},{3,2},{4,5},{5,4},{6,7},{7,6},{8,9},{9,8},{10,11... | collective-permute-start | bytes 786440 | tf_op jit(solution)/shard_map/ppermute | solution.py:181
  37.0 1.6 %collective-permute-start.8 = (bf16[64,1024]{1,0:T(8,128)(2,1)S(1)}, bf16[64,1024]{1,0:T(8,128)(2,1)S(1)}, u32[]{:S(2)}, u32[]{:S(2)}) collective-permute-start(bf16[64,1024]{1,0:T(8,128)(2,1)S(1)} %collective-permute-done.3.refs_3_), channel_id=1, source_target_pairs={{0,1},{1,0},{2,3},{3,2},{4,5},{5,4},{6,7},{7,6},{8,9},{9,8},{10,11... | collective-permute-start | bytes 393224 | tf_op jit(solution)/shard_map/ppermute | solution.py:181
  37.1 2.4 %collective-permute-start.9 = (bf16[64,1024]{1,0:T(8,128)(2,1)S(1)}, bf16[64,1024]{1,0:T(8,128)(2,1)S(1)}, u32[]{:S(2)}, u32[]{:S(2)}) collective-permute-start(bf16[64,1024]{1,0:T(8,128)(2,1)S(1)} %collective-permute-done.4.refs_4_), channel_id=1, source_target_pairs={{0,1},{1,0},{2,3},{3,2},{4,5},{5,4},{6,7},{7,6},{8,9},{9,8},{10,11... | collective-permute-start | bytes 393224 | tf_op jit(solution)/shard_map/ppermute | solution.py:181
  37.6 14.4 %collective-permute-start.15 = (bf16[192,1024]{1,0:T(8,128)(2,1)S(1)}, bf16[192,1024]{1,0:T(8,128)(2,1)S(1)}, u32[]{:S(2)}, u32[]{:S(2)}) collective-permute-start(bf16[192,1024]{1,0:T(8,128)(2,1)S(1)} %pad_maximum_fusion.refs_10_), channel_id=1, source_target_pairs={{0,1},{1,0},{2,3},{3,2},{4,5},{5,4},{6,7},{7,6},{8,9},{9,8},{10,11... | collective-permute-start | bytes 1179656 | tf_op jit(solution)/shard_map/ppermute | solution.py:181
  38.6 8.2 %collective-permute-start.13 = (bf16[96,1024]{1,0:T(8,128)(2,1)S(1)}, bf16[96,1024]{1,0:T(8,128)(2,1)S(1)}, u32[]{:S(2)}, u32[]{:S(2)}) collective-permute-start(bf16[96,1024]{1,0:T(8,128)(2,1)S(1)} %slice.18), channel_id=1, source_target_pairs={{0,2},{2,4},{4,6},{6,0},{1,3},{3,5},{5,7},{7,1},{8,10},{10,12},{12... | collective-permute-start | bytes 589832 | tf_op jit(solution)/shard_map/ppermute | solution.py:177
  39.5 7.3 %collective-permute-start.14 = (bf16[96,1024]{1,0:T(8,128)(2,1)S(1)}, bf16[96,1024]{1,0:T(8,128)(2,1)S(1)}, u32[]{:S(2)}, u32[]{:S(2)}) collective-permute-start(bf16[96,1024]{1,0:T(8,128)(2,1)S(1)} %slice.19), channel_id=1, source_target_pairs={{0,6},{2,0},{4,2},{6,4},{1,7},{3,1},{5,3},{7,5},{8,14},{10,8},{12,... | collective-permute-start | bytes 589832 | tf_op jit(solution)/shard_map/ppermute | solution.py:177
  41.9 10.1 %collective-permute-start.16 = (bf16[192,1024]{1,0:T(8,128)(2,1)S(1)}, bf16[192,1024]{1,0:T(8,128)(2,1)S(1)}, u32[]{:S(2)}, u32[]{:S(2)}) collective-permute-start(bf16[192,1024]{1,0:T(8,128)(2,1)S(1)} %collective-permute-done.11.refs_11_), channel_id=1, source_target_pairs={{0,1},{1,0},{2,3},{3,2},{4,5},{5,4},{6,7},{7,6},{8,9},{9,8},{10,11... | collective-permute-start | bytes 1179656 | tf_op jit(solution)/shard_map/ppermute | solution.py:181
  41.9 10.1 %collective-permute-start.17 = (bf16[192,1024]{1,0:T(8,128)(2,1)S(1)}, bf16[192,1024]{1,0:T(8,128)(2,1)S(1)}, u32[]{:S(2)}, u32[]{:S(2)}) collective-permute-start(bf16[192,1024]{1,0:T(8,128)(2,1)S(1)} %collective-permute-done.12.refs_12_), channel_id=1, source_target_pairs={{0,1},{1,0},{2,3},{3,2},{4,5},{5,4},{6,7},{7,6},{8,9},{9,8},{10,11... | collective-permute-start | bytes 1179656 | tf_op jit(solution)/shard_map/ppermute | solution.py:181
  46.8 5.2 %collective-permute-start.18 = (bf16[96,1024]{1,0:T(8,128)(2,1)S(1)}, bf16[96,1024]{1,0:T(8,128)(2,1)S(1)}, u32[]{:S(2)}, u32[]{:S(2)}) collective-permute-start(bf16[96,1024]{1,0:T(8,128)(2,1)S(1)} %collective-permute-done.13.refs_13_), channel_id=1, source_target_pairs={{0,1},{1,0},{2,3},{3,2},{4,5},{5,4},{6,7},{7,6},{8,9},{9,8},{10,11... | collective-permute-start | bytes 589832 | tf_op jit(solution)/shard_map/ppermute | solution.py:181
  46.8 5.2 %collective-permute-start.19 = (bf16[96,1024]{1,0:T(8,128)(2,1)S(1)}, bf16[96,1024]{1,0:T(8,128)(2,1)S(1)}, u32[]{:S(2)}, u32[]{:S(2)}) collective-permute-start(bf16[96,1024]{1,0:T(8,128)(2,1)S(1)} %collective-permute-done.14.refs_14_), channel_id=1, source_target_pairs={{0,1},{1,0},{2,3},{3,2},{4,5},{5,4},{6,7},{7,6},{8,9},{9,8},{10,11... | collective-permute-start | bytes 589832 | tf_op jit(solution)/shard_map/ppermute | solution.py:181
  (3 other events, 2.1 us)
where the time goes:
time: 70.9 us; the launch traced here: 70.6 us
  starting transfers between devices  20.9 us (29%)
  waiting for transfers between devices  15.7 us (22%)
  blocking collectives  14.6 us (21%)
  Pallas kernels  13.4 us (19%)
  local copies, waits for them, and re-layouts  3.77 us (5%)
  between operations  1.46 us (2%)
  other arithmetic  0.77 us (1%)
    ppermute x8, starting transfers between devices, ring_pass(): lax.ppermute(piece, 'z', [(i, (i + shift) % count) for i in range(count)])  15.1 us
    all_to_all x1, blocking collectives, gradient(): lax.all_to_all(partial.reshape(count, electrons // count, width), walkers...  14.6 us
    ppermute x8, waiting for transfers between devices, ring_pass(): lax.ppermute(piece, 'z', [(i, (i + shift) % count) for i in range(count)])  11.7 us
    pallas_call x2, Pallas kernels, evaluate(): pl.pallas_call(functools.partial(eval_kernel, shards=shards, slots=slots,...  6.75 us
    unnamed x15, local copies, waits for them, and re-layouts  3.71 us
    ppermute x2, starting transfers between devices, ring_swap(): return lax.ppermute(piece, 'xh', [(0, 1), (1, 0)])  3.61 us
    pallas_call x1, Pallas kernels, gradient(): pl.pallas_call(functools.partial(ratio_kernel, parts=parts, z_count=z_cou...  3.37 us
    pallas_call x1, Pallas kernels, gradient(): pl.pallas_call(functools.partial(finish_kernel, parts=parts, halves=halve...  3.25 us
  transfers between devices with their start and end apart: 20, of which 4 were waited for; matrix products, arithmetic and copies ran while one was open for 0% of the time, Pallas kernels for 14%

commit v1 on v0

v1 whole, which is shorter than its diff:
```python
import functools

import jax
import jax.numpy as jnp
from jax import lax
from jax.experimental import pallas as pl
from jax.experimental.pallas import tpu as pltpu
from jax.sharding import Mesh
from jax.sharding import PartitionSpec as P


GRID = 16
PLANE = GRID * GRID
TILE = 256
BF16 = jnp.bfloat16
F32 = jnp.float32


def mm(left, right):
    return jnp.dot(left, right, preferred_element_type=F32)


def mm_nt(left, right):
    return lax.dot_general(left, right, (((1,), (1,)), ((), ())), preferred_element_type=F32)


def mm_tn(left, right):
    return lax.dot_general(left, right, (((0,), (0,)), ((), ())), preferred_element_type=F32)


def dense_rows(cell, frac):
    remain = 1.0 - frac
    square = frac * frac
    cubed = square * frac
    sixth = 1.0 / 6.0
    values = [
        remain * remain * remain * sixth,
        (3.0 * cubed - 6.0 * square + 4.0) * sixth,
        (-3.0 * cubed + 3.0 * square + 3.0 * frac + 1.0) * sixth,
        cubed * sixth,
    ]
    curves = [remain, 3.0 * frac - 2.0, 1.0 - 3.0 * frac, frac]
    line = lax.broadcasted_iota(jnp.int32, (GRID, cell.shape[1]), 0)
    tap = (line - cell + (GRID + 1)) & (GRID - 1)
    value = jnp.zeros((GRID, cell.shape[1]), F32)
    curve = jnp.zeros((GRID, cell.shape[1]), F32)
    for a in range(4):
        value = jnp.where(tap == a, values[a], value)
        curve = jnp.where(tap == a, curves[a], curve)
    return value, curve


def slot_tables(me, occ, shards, width, slots):
    owner = lax.broadcasted_iota(jnp.int32, (shards, occ.shape[1]), 0) == lax.div(occ, width)
    count = owner.astype(jnp.int32)
    lane = lax.broadcasted_iota(jnp.int32, count.shape, 1)
    step = 1
    while step < occ.shape[1]:
        count = count + jnp.where(lane >= step, pltpu.roll(count, step, 1), 0)
        step *= 2
    rank = jnp.sum(jnp.where(owner, count - 1, 0), axis=0, keepdims=True)
    slot = lax.div(occ, width) * slots + rank
    placed = lax.broadcasted_iota(jnp.int32, (slots, occ.shape[1]), 0) == slot - me * slots
    column = lax.broadcasted_iota(jnp.int32, (width, occ.shape[1]), 0) == occ - me * width
    picker = mm_nt(placed.astype(F32).astype(BF16), column.astype(F32).astype(BF16)).astype(BF16)
    return slot, picker


def expand(rows, weights):
    return jnp.concatenate([rows[g:g + 1, :] * weights for g in range(GRID)], axis=0)


def turn_kernel(coef_hbm, turned_ref, coef_ref, sems):
    pieces = sems.shape[0]
    rows = coef_ref.shape[0] // pieces
    copies = [
        pltpu.make_async_copy(coef_hbm.at[pl.ds(k * rows, rows)], coef_ref.at[pl.ds(k * rows, rows)], sems.at[k])
        for k in range(pieces)
    ]
    for copy in copies:
        copy.start()
    for k, copy in enumerate(copies):
        copy.wait()
        for first in range(k * rows, (k + 1) * rows, PLANE):
            turned_ref[:, first:first + PLANE] = jnp.transpose(coef_ref[first:first + PLANE, :])


def eval_kernel(*refs, shards, slots, first, electrons):
    if first == 0:
        me_ref, turned_ref, cell_ref, frac_ref, occ_ref, val_ref, lap_ref, lapt_ref, picker_ref, slot_ref, *weight_refs = refs
    else:
        turned_ref, cell_ref, frac_ref, picker_ref, val_ref, lap_ref, lapt_ref, *weight_refs = refs

    def build(t, value_ref, lap_ref):
        here = slice(first + t * TILE, first + (t + 1) * TILE)
        vx, cx = dense_rows(cell_ref[0, :, here], frac_ref[0, :, here])
        vy, cy = dense_rows(cell_ref[1, :, here], frac_ref[1, :, here])
        vz, cz = dense_rows(cell_ref[2, :, here], frac_ref[2, :, here])
        value = expand(vy, vz)
        curve = expand(cy, vz) + expand(vy, cz)
        for g in range(GRID):
            x_value, x_curve = vx[g:g + 1, :], cx[g:g + 1, :]
            value_ref[g * PLANE:(g + 1) * PLANE, :] = (x_value * value).astype(BF16)
            lap_ref[g * PLANE:(g + 1) * PLANE, :] = (x_curve * value + x_value * curve).astype(BF16)

    def product(t, value_w, lap_w):
        here = slice(t * TILE, (t + 1) * TILE)
        val_ref[:, here] = mm(turned_ref[...], value_w[...]).astype(BF16)
        lap = mm(turned_ref[...], lap_w[...]).astype(BF16)
        lap_ref[:, here] = lap
        lapt_ref[:, here] = mm(picker_ref[...], lap).astype(BF16)

    tiles = electrons // TILE
    build(0, weight_refs[0], weight_refs[1])
    if first == 0:
        slot, picker = slot_tables(me_ref[0], occ_ref[...], shards, turned_ref.shape[0], slots)
        slot_ref[...] = slot
        picker_ref[...] = picker
    for t in range(tiles):
        if t + 1 < tiles:
            build(t + 1, *weight_refs[2 * ((t + 1) % 2):][:2])
        product(t, *weight_refs[2 * (t % 2):][:2])


def place(me_ref, z_count):
    me = me_ref[0]
    core = lax.rem(me, 2)
    z = lax.rem(lax.div(me, 2), z_count)
    plane = lax.div(me, 2 * z_count)
    along = [lax.rem(z + dz, z_count) for dz in (0, z_count - 1, 1, 2)]
    return plane, along, core


def inverse_times(me_ref, z_count, inv_refs, right, out_ref, size):
    plane, along, core = place(me_ref, z_count)
    blocks = [(p * z_count + z) * 2 + c for c in (core, 1 - core) for p in (plane, 1 - plane) for z in along]
    first = 0
    for ref in inv_refs:
        value = mm_nt(ref[...], right).astype(out_ref.dtype)
        count = ref.shape[0] // size
        for j, block in enumerate(blocks[first:first + count]):
            start = pl.multiple_of(block * size, size)
            out_ref[pl.ds(start, size), :] = value[j * size:(j + 1) * size]
        first += count


def ratio_kernel(me_ref, *refs, parts, z_count, slots, size):
    inv_refs, val_refs = refs[:parts], refs[parts:-3]
    slot_ref, rows_ref, ratio_ref = refs[-3:]
    val = jnp.concatenate([ref[...] for ref in val_refs], axis=1)
    inverse_times(me_ref, z_count, inv_refs, val, ratio_ref, size)
    ratio = ratio_ref[...]
    slot = slot_ref[...]
    plane, along, core = place(me_ref, z_count)
    blocks = [(p * z_count + z) * 2 + c for c in (core, 1 - core) for z in along for p in (plane, 1 - plane)]
    for j in range(0, len(blocks), 2):
        ids = lax.broadcasted_iota(jnp.int32, (slots, slot.shape[1]), 0)
        pick = jnp.concatenate([(ids + block * slots == slot).astype(F32) for block in blocks[j:j + 2]], axis=0)
        rows_ref[j * slots:(j + 2) * slots, :] = mm(pick.astype(BF16), ratio).astype(BF16)


def coupled(rows_ref, pieces):
    total = None
    for first, ref in pieces:
        term = mm_tn(rows_ref[first:first + ref.shape[0], :], ref[...])
        total = term if total is None else total + term
    return total


def couple_kernel(energy_ref, weight_ref, *refs, firsts):
    near_refs = refs[:len(firsts)]
    rows_ref, val_a, val_b, lap_a, lap_b, mixed_ref = refs[len(firsts):]
    total = coupled(rows_ref, list(zip(firsts, near_refs)))
    val = jnp.concatenate([val_a[...], val_b[...]], axis=1).astype(F32)
    lap = jnp.concatenate([lap_a[...], lap_b[...]], axis=1).astype(F32)
    mixed_ref[...] = weight_ref[0] * (energy_ref[0] * val - 0.5 * (lap - total))


def finish_kernel(me_ref, weight_ref, mixed_ref, rows_ref, *refs, firsts, z_count, size):
    far_refs, inv_refs, out_ref = refs[:len(firsts)], refs[len(firsts):-1], refs[-1]
    total = coupled(rows_ref, list(zip(firsts, far_refs)))
    mixed = (mixed_ref[...] + (0.5 * weight_ref[0]) * total).astype(BF16)
    inverse_times(me_ref, z_count, inv_refs, mixed, out_ref, size)


VMEM = pl.BlockSpec(memory_space=pltpu.VMEM)
SMEM = pl.BlockSpec(memory_space=pltpu.SMEM)
HBM = pl.BlockSpec(memory_space=pltpu.HBM)


def ring_swap(piece):
    return lax.ppermute(piece, "xh", [(0, 1), (1, 0)])


def ring_pass(piece, shift):
    count = lax.axis_size("z")
    return lax.ppermute(piece, "z", [(i, (i + shift) % count) for i in range(count)])


def core_swap(piece):
    return lax.ppermute(piece, "core", [(0, 1), (1, 0)])


def gradient(coefficients, inverse, cell_index, fraction, energies, weights, occupied):
    cells, width = coefficients.shape
    _, rows, electrons = inverse.shape
    z_count = lax.axis_size("z")
    shards = 2 * z_count * 2
    slots = 3 * electrons // (2 * shards)
    xh, z, core = lax.axis_index("xh"), lax.axis_index("z"), lax.axis_index("core")
    me = ((xh * z_count + z) * 2 + core).astype(jnp.int32).reshape(1)

    out = lambda *shape_dtype: jax.ShapeDtypeStruct(*shape_dtype)
    halves = 2
    part = electrons // halves

    def params(mib):
        return pltpu.CompilerParams(vmem_limit_bytes=mib * 1024 * 1024)

    def cost(products):
        return pl.CostEstimate(flops=2 * products, bytes_accessed=2 * cells * width, transcendentals=0)

    def evaluate(h, *operands):
        results = [out((width, part), BF16), out((width, part), BF16), out((slots, part), BF16)]
        if h == 0:
            results += [out((slots, width), BF16), out((1, electrons), jnp.int32)]
        return pl.pallas_call(
            functools.partial(eval_kernel, shards=shards, slots=slots, first=h * part, electrons=part),
            out_shape=results,
            in_specs=[SMEM] + [VMEM] * 4 if h == 0 else [VMEM] * 4,
            out_specs=[VMEM] * len(results),
            scratch_shapes=[pltpu.VMEM((cells, TILE), BF16)] * 4,
            compiler_params=params(32),
            cost_estimate=cost(2 * part * cells * width),
            name="evaluate",
        )(*operands)

    cell_index, fraction = jnp.transpose(cell_index, (1, 0, 2)), jnp.transpose(fraction, (1, 0, 2))
    mine = inverse.reshape(rows, electrons)
    half = rows // 2

    inv_below = ring_pass(mine, 1)
    inv_above = ring_pass(mine, -1)
    inv_far_mine = ring_swap(mine)
    inv_first = ring_pass(inv_below[:half], 1)
    inv_second = ring_pass(inv_above[half:], -1)
    inv_plane = jnp.concatenate([mine, inv_below, inv_above, inv_first, inv_second], axis=0)
    inv_far_rest = ring_swap(inv_plane[rows:])
    inv_own = [inv_plane, inv_far_mine, inv_far_rest]
    inv_others = [core_swap(inv_plane), core_swap(inv_far_mine)]
    inv_others.append(core_swap(inv_far_rest))
    inv_all = inv_own + inv_others

    turned = pl.pallas_call(
        turn_kernel,
        out_shape=out((width, cells), BF16),
        in_specs=[HBM],
        out_specs=VMEM,
        scratch_shapes=[pltpu.VMEM((cells, width), BF16), pltpu.SemaphoreType.DMA((4,))],
        compiler_params=params(50),
        cost_estimate=cost(cells * width * 64),
        name="turn",
    )(coefficients)
    val_a, lap_a, lapt_a, picker, slot = evaluate(0, me, turned, cell_index, fraction, occupied.reshape(1, electrons))
    val_b, lap_b, lapt_b = evaluate(1, turned, cell_index, fraction, picker)

    lapt_mine = jnp.concatenate([lapt_a, lapt_b], axis=1)
    lapt_far = ring_swap(lapt_mine)
    lap_pair = jnp.concatenate([lapt_mine, lapt_far], axis=0)
    lap_below = ring_pass(lap_pair, 1)
    lap_above = ring_pass(lap_pair, -1)
    lap_first = ring_pass(lap_below[:slots], 1)
    lap_second = ring_pass(lap_above[slots:], -1)
    near = [lap_pair, lap_below, lap_above]
    far = [lap_first, lap_second]
    near += [core_swap(piece) for piece in near]
    far += [core_swap(piece) for piece in far]
    total = shards * slots
    near_firsts = [0, 2 * slots, 4 * slots]
    near_firsts += [first + total // 2 for first in near_firsts]
    far_firsts = [6 * slots, 7 * slots]
    far_firsts += [first + total // 2 for first in far_firsts]

    ratio_rows, _ = pl.pallas_call(
        functools.partial(ratio_kernel, parts=len(inv_all), z_count=z_count, slots=slots, size=rows),
        out_shape=[out((total, width), BF16), out((electrons, width), BF16)],
        in_specs=[SMEM] + [VMEM] * (len(inv_all) + 3),
        out_specs=[VMEM] * 2,
        compiler_params=params(24),
        cost_estimate=cost(3 * electrons * electrons * width),
        name="ratio",
    )(me, *inv_all, val_a, val_b, slot)

    mixed = pl.pallas_call(
        functools.partial(couple_kernel, firsts=near_firsts),
        out_shape=out((width, electrons), F32),
        in_specs=[SMEM] * 2 + [VMEM] * (len(near) + 5),
        out_specs=VMEM,
        compiler_params=params(24),
        cost_estimate=cost(electrons * electrons * width),
        name="couple",
    )(energies, weights, *near, ratio_rows, val_a, val_b, lap_a, lap_b)

    partial = pl.pallas_call(
        functools.partial(finish_kernel, firsts=far_firsts, z_count=z_count, size=rows),
        out_shape=out((electrons, width), BF16),
        in_specs=[SMEM] * 2 + [VMEM] * (2 + len(far) + len(inv_all)),
        out_specs=VMEM,
        compiler_params=params(24),
        cost_estimate=cost(electrons * electrons * width),
        name="finish",
    )(me, weights, mixed, ratio_rows, *far, *inv_all)

    walkers = ("y", "xl")
    count = lax.axis_size(walkers)
    blocks = lax.all_to_all(partial.reshape(count, electrons // count, width), walkers, 0, 0, tiled=True)
    return jnp.sum(blocks.astype(F32), axis=0)


def solution(mesh):
    fine = Mesh(mesh.devices.reshape(4, 2, 2, 4, 2), ("y", "xl", "xh", "z", "core"))
    walk, orb = ("y", "xl"), ("xh", "z", "core")
    in_specs = (
        P(None, orb),
        P(walk, orb, None),
        P(walk, None, None),
        P(walk, None, None),
        P(walk),
        P(walk),
        P(),
    )
    return jax.shard_map(gradient, mesh=fine, in_specs=in_specs, out_specs=P(walk, orb), check_vma=False)
```

time: 70.9 us -> 67.5 us (0.952)
  local copies, waits for them, and re-layouts: 3.77 us -> 0.12 us
  blocking collectives: 14.6 us -> 15.6 us
  starting transfers between devices: 20.9 us -> 20 us
    unnamed x15 -> x13, local copies, waits for them, and re-layouts: 3.71 us -> 0.06 us
    ppermute x2 -> x3, starting transfers between devices: 3.61 us -> 6.71 us  [ring_swap(): return lax.ppermute(piece, 'xh', [(0, 1), (1, 0)])]
    ppermute x8, starting transfers between devices: 15.1 us -> 12.1 us  [ring_pass(): lax.ppermute(piece, 'z', [(i, (i + shift) % count) for i in range(count)])]
    all_to_all x1, blocking collectives: 14.6 us -> 15.6 us  [gradient(): lax.all_to_all(partial.reshape(count, electrons // count, width), walkers...]
    ppermute x10 -> x8, starting transfers between devices: 2.21 us -> 1.18 us  [core_swap(): return lax.ppermute(piece, 'core', [(0, 1), (1, 0)])]
    pallas_call x2 -> x4, Pallas kernels: 6.62 us -> 7.37 us  [the longest x1 2.73 us: gradient(): pl.pallas_call(functools.partial(ratio_kernel, parts=len(inv_all), z_coun...]
    ppermute x2 -> x3, waiting for transfers between devices: 3.15 us -> 2.73 us  [ring_swap(): return lax.ppermute(piece, 'xh', [(0, 1), (1, 0)])]
  transfers between devices with their start and end apart: 20 -> 19, of which waited for: 4 -> 7; matrix products, arithmetic and copies ran while one was open for 0% -> 0% of each run, Pallas kernels for 14% -> 18%
where the time goes in v1:
time: 67.5 us; the launch traced here: 67.3 us
  starting transfers between devices  20 us (30%)
  blocking collectives  15.6 us (23%)
  waiting for transfers between devices  15.5 us (23%)
  Pallas kernels  13.7 us (20%)
  between operations  1.52 us (2%)
  other arithmetic  0.78 us (1%)
    all_to_all x1, blocking collectives, gradient(): lax.all_to_all(partial.reshape(count, electrons // count, width), walkers...  15.6 us
    ppermute x8, starting transfers between devices, ring_pass(): lax.ppermute(piece, 'z', [(i, (i + shift) % count) for i in range(count)])  12.1 us
    ppermute x8, waiting for transfers between devices, ring_pass(): lax.ppermute(piece, 'z', [(i, (i + shift) % count) for i in range(count)])  11.4 us
    ppermute x3, starting transfers between devices, ring_swap(): return lax.ppermute(piece, 'xh', [(0, 1), (1, 0)])  6.71 us
    pallas_call x2, Pallas kernels, evaluate(): pl.pallas_call(functools.partial(eval_kernel, shards=shards, slots=slots,...  6.36 us
    ppermute x3, waiting for transfers between devices, ring_swap(): return lax.ppermute(piece, 'xh', [(0, 1), (1, 0)])  2.73 us
    pallas_call x1, Pallas kernels, gradient(): pl.pallas_call(functools.partial(ratio_kernel, parts=len(inv_all), z_coun...  2.73 us
    pallas_call x1, Pallas kernels, gradient(): pl.pallas_call(turn_kernel, out_shape=out((width, cells), BF16), in_specs...  1.91 us
  transfers between devices with their start and end apart: 19, of which 7 were waited for; matrix products, arithmetic and copies ran while one was open for 0% of the time, Pallas kernels for 18%

profile of v1, /device:TPU:0, one launch (start us, length us, event | category | flops | bytes accessed | tf_op | source)
XLA Modules:
  0.0 67.3 jit_solution(15553419190184980809)
XLA Ops:
  0.0 2.0 %collective-permute-start.6 = (bf16[64,1024]{1,0:T(8,128)(2,1)}, bf16[64,1024]{1,0:T(8,128)(2,1)S(1)}, u32[]{:S(2)}, u32[]{:S(2)}) collective-permute-start(bf16[64,1024]{1,0:T(8,128)(2,1)} %bitcast.13), channel_id=1, source_target_pairs={{0,2},{2,4},{4,6},{6,0},{1,3},{3,5},{5,7},{7,1},{8,10},{10,12},{12... | collective-permute-start | bytes 393224 | tf_op jit(solution)/shard_map/ppermute | solution.py:197
  2.0 2.1 %collective-permute-start.7 = (bf16[64,1024]{1,0:T(8,128)(2,1)}, bf16[64,1024]{1,0:T(8,128)(2,1)S(1)}, u32[]{:S(2)}, u32[]{:S(2)}) collective-permute-start(bf16[64,1024]{1,0:T(8,128)(2,1)} %bitcast.14), channel_id=1, source_target_pairs={{0,6},{2,0},{4,2},{6,4},{1,7},{3,1},{5,3},{7,5},{8,14},{10,8},{12,... | collective-permute-start | bytes 393224 | tf_op jit(solution)/shard_map/ppermute | solution.py:197
  4.2 1.9 %turn.1.refs_1_.refs_0_ = bf16[256,4096]{1,0:T(8,128)(2,1)S(1)} custom-call(bf16[4096,256]{1,0:T(8,128)(2,1)} %coef_hbm.1), custom_call_target="tpu_custom_call" | custom-call | flops 134217728 | bytes 2097152 | tf_op jit(solution)/shard_map/turn/pallas_call | solution.py:254
  6.1 3.6 %evaluate.2 = (bf16[256,512]{1,0:T(8,128)(2,1)S(1)}, bf16[256,512]{1,0:T(8,128)(2,1)S(1)}, bf16[96,512]{1,0:T(8,128)(2,1)S(1)}, bf16[96,256]{1,0:T(8,128)(2,1)S(1)}, s32[1,1024]{1,0:T(1,128)S(1)}) custom-call(s32[1]{0:T(128)} %bitcast.refs_0_.me_ref, bf16[256,4096]{1,0:T(8,128)(2,1)S(1)} %turn.1.refs_1_.refs_0_, s32[3,1,1024]{2,1,0:T(1,128)S(1)} %bitcast.8, ...), custom_call_target="tpu_custom_call" | custom-call | flops 2147483648 | bytes 2097152 | tf_op jit(solution)/shard_map/evaluate/pallas_call | solution.py:227
  9.7 2.8 %evaluate.3 = (bf16[256,512]{1,0:T(8,128)(2,1)S(1)}, bf16[256,512]{1,0:T(8,128)(2,1)S(1)}, bf16[96,512]{1,0:T(8,128)(2,1)S(1)}) custom-call(bf16[256,4096]{1,0:T(8,128)(2,1)S(1)} %turn.1.refs_1_.refs_0_, s32[3,1,1024]{2,1,0:T(1,128)S(1)} %bitcast.9, f32[3,1,1024]{2,1,0:T(1,128)S(1)} %bitcast.11, bf16[96,256]{1,0:T(8,128)(2,1)S(1)} %get-tuple-element.15.refs_3_), custom_call_target="tpu_custom_call" | custom-call | flops 2147483648 | bytes 2097152 | tf_op jit(solution)/shard_map/evaluate/pallas_call | solution.py:227
  12.5 3.1 %collective-permute-start = (bf16[96,1024]{1,0:T(8,128)(2,1)S(1)}, bf16[96,1024]{1,0:T(8,128)(2,1)S(1)}, u32[]{:S(2)}, u32[]{:S(2)}) collective-permute-start(bf16[96,1024]{1,0:T(8,128)(2,1)S(1)} %constant_dynamic-update-slice_fusion), channel_id=1, source_target_pairs={{0,8},{8,0},{1,9},{9,1},{2,10},{10,2},{3,11},{11,3},{4,12},{12,4},... | collective-permute-start | bytes 589832 | tf_op jit(solution)/shard_map/ppermute | solution.py:192
  15.8 3.3 %collective-permute-start.9 = (bf16[32,1024]{1,0:T(8,128)(2,1)S(1)}, bf16[32,1024]{1,0:T(8,128)(2,1)S(1)}, u32[]{:S(2)}, u32[]{:S(2)}) collective-permute-start(bf16[32,1024]{1,0:T(8,128)(2,1)S(1)} %slice.19), channel_id=1, source_target_pairs={{0,6},{2,0},{4,2},{6,4},{1,7},{3,1},{5,3},{7,5},{8,14},{10,8},{12,... | collective-permute-start | bytes 196616 | tf_op jit(solution)/shard_map/ppermute | solution.py:197
  19.1 2.1 %collective-permute-done.8 = bf16[32,1024]{1,0:T(8,128)(2,1)S(1)} collective-permute-done((bf16[32,1024]{1,0:T(8,128)(2,1)S(1)}, bf16[32,1024]{1,0:T(8,128)(2,1)S(1)}, u32[]{:S(2)}, u32[]{:S(2)}) %collective-permute-start.8) | collective-permute-done | bytes 65568 | tf_op jit(solution)/shard_map/ppermute | solution.py:197
  21.3 0.6 collective-permute-start.11
  21.9 0.8 %collective-permute-start.1 = (bf16[192,1024]{1,0:T(8,128)(2,1)S(1)}, bf16[192,1024]{1,0:T(8,128)(2,1)S(1)}, u32[]{:S(2)}, u32[]{:S(2)}) collective-permute-start(bf16[192,1024]{1,0:T(8,128)(2,1)S(1)} %pad_maximum_fusion.refs_0_), channel_id=1, source_target_pairs={{0,2},{2,4},{4,6},{6,0},{1,3},{3,5},{5,7},{7,1},{8,10},{10,12},{12... | collective-permute-start | bytes 1179656 | tf_op jit(solution)/shard_map/ppermute | solution.py:197
  22.7 2.8 %collective-permute-start.2 = (bf16[192,1024]{1,0:T(8,128)(2,1)S(1)}, bf16[192,1024]{1,0:T(8,128)(2,1)S(1)}, u32[]{:S(2)}, u32[]{:S(2)}) collective-permute-start(bf16[192,1024]{1,0:T(8,128)(2,1)S(1)} %pad_maximum_fusion.refs_0_), channel_id=1, source_target_pairs={{0,6},{2,0},{4,2},{6,4},{1,7},{3,1},{5,3},{7,5},{8,14},{10,8},{12,... | collective-permute-start | bytes 1179656 | tf_op jit(solution)/shard_map/ppermute | solution.py:197
  25.5 3.0 %collective-permute-start.10 = (bf16[64,1024]{1,0:T(8,128)(2,1)S(1)}, bf16[64,1024]{1,0:T(8,128)(2,1)S(1)}, u32[]{:S(2)}, u32[]{:S(2)}) collective-permute-start(bf16[64,1024]{1,0:T(8,128)(2,1)S(1)} %bitcast.15), channel_id=1, source_target_pairs={{0,8},{8,0},{1,9},{9,1},{2,10},{10,2},{3,11},{11,3},{4,12},{12,4},... | collective-permute-start | bytes 393224 | tf_op jit(solution)/shard_map/ppermute | solution.py:192
  28.5 3.8 %collective-permute-done.1.refs_1_ = bf16[192,1024]{1,0:T(8,128)(2,1)S(1)} collective-permute-done((bf16[192,1024]{1,0:T(8,128)(2,1)S(1)}, bf16[192,1024]{1,0:T(8,128)(2,1)S(1)}, u32[]{:S(2)}, u32[]{:S(2)}) %collective-permute-start.1) | collective-permute-done | bytes 393248 | tf_op jit(solution)/shard_map/ppermute | solution.py:197
  32.4 1.3 %collective-permute-done.11.refs_2_.refs_6_ = bf16[192,1024]{1,0:T(8,128)(2,1)S(1)} collective-permute-done((bf16[192,1024]{1,0:T(8,128)(2,1)S(1)}, bf16[192,1024]{1,0:T(8,128)(2,1)S(1)}, u32[]{:S(2)}, u32[]{:S(2)}) %collective-permute-start.11) | collective-permute-done | bytes 393248 | tf_op jit(solution)/shard_map/ppermute | solution.py:192
  33.7 1.4 %collective-permute-done.10.refs_1_.refs_5_ = bf16[64,1024]{1,0:T(8,128)(2,1)S(1)} collective-permute-done((bf16[64,1024]{1,0:T(8,128)(2,1)S(1)}, bf16[64,1024]{1,0:T(8,128)(2,1)S(1)}, u32[]{:S(2)}, u32[]{:S(2)}) %collective-permute-start.10) | collective-permute-done | bytes 131104 | tf_op jit(solution)/shard_map/ppermute | solution.py:192
  35.1 1.3 %collective-permute-done.13.refs_4_.refs_8_ = bf16[64,1024]{1,0:T(8,128)(2,1)S(1)} collective-permute-done((bf16[64,1024]{1,0:T(8,128)(2,1)S(1)}, bf16[64,1024]{1,0:T(8,128)(2,1)S(1)}, u32[]{:S(2)}, u32[]{:S(2)}) %collective-permute-start.13) | collective-permute-done | bytes 131104 | tf_op jit(solution)/shard_map/ppermute | solution.py:201
  37.1 2.1 %collective-permute-done.15.refs_0_ = bf16[96,1024]{1,0:T(8,128)(2,1)S(1)} collective-permute-done((bf16[96,1024]{1,0:T(8,128)(2,1)S(1)}, bf16[96,1024]{1,0:T(8,128)(2,1)S(1)}, u32[]{:S(2)}, u32[]{:S(2)}) %collective-permute-start.15) | collective-permute-done | bytes 196640 | tf_op jit(solution)/shard_map/ppermute | solution.py:197
  39.2 1.0 %collective-permute-start.16 = (bf16[96,1024]{1,0:T(8,128)(2,1)S(1)}, bf16[96,1024]{1,0:T(8,128)(2,1)S(1)}, u32[]{:S(2)}, u32[]{:S(2)}) collective-permute-start(bf16[96,1024]{1,0:T(8,128)(2,1)S(1)} %slice.21), channel_id=1, source_target_pairs={{0,6},{2,0},{4,2},{6,4},{1,7},{3,1},{5,3},{7,5},{8,14},{10,8},{12,... | collective-permute-start | bytes 589832 | tf_op jit(solution)/shard_map/ppermute | solution.py:197
  41.5 3.4 %collective-permute-done.16.refs_1_ = bf16[96,1024]{1,0:T(8,128)(2,1)S(1)} collective-permute-done((bf16[96,1024]{1,0:T(8,128)(2,1)S(1)}, bf16[96,1024]{1,0:T(8,128)(2,1)S(1)}, u32[]{:S(2)}, u32[]{:S(2)}) %collective-permute-start.16) | collective-permute-done | bytes 196640 | tf_op jit(solution)/shard_map/ppermute | solution.py:197
  45.4 2.7 %ratio.1 = (bf16[1536,256]{1,0:T(8,128)(2,1)S(1)}, bf16[1024,256]{1,0:T(8,128)(2,1)}) custom-call(s32[1]{0:T(128)} %bitcast.refs_0_.me_ref, bf16[256,1024]{1,0:T(8,128)(2,1)S(1)} %constant_dynamic-update-slice_fusion.2.refs_0_.refs_4_, bf16[64,1024]{1,0:T(8,128)(2,1)S(1)} %collective-permute-done.10.refs_1_.refs_5_, ...), custom_call_target="tpu_custom_call" | custom-call | flops 1610612736 | bytes 2097152 | tf_op jit(solution)/shard_map/ratio/pallas_call | solution.py:284
  48.2 1.1 %couple.1.mixed_ref = f32[256,1024]{1,0:T(8,128)S(1)} custom-call(f32[1]{0:T(128)S(6)} %copy.13.energy_ref, f32[1]{0:T(128)S(6)} %copy.14.weight_ref, bf16[192,1024]{1,0:T(8,128)(2,1)S(1)} %pad_maximum_fusion.refs_0_, bf16[192,1024]{1,0:T(8,128)(2,1)S(1)} %collective-permute-done.1.refs_1_, bf16[192,1024]{1,0:T(8,128)(2,1)S(1)} %collective-permute-done.2.refs_2_, ...), custom_call_target="tpu_custom_call" | custom-call | flops 536870912 | bytes 2097152 | tf_op jit(solution)/shard_map/couple/pallas_call | solution.py:294
  49.3 1.7 %finish.1 = bf16[1024,256]{1,0:T(8,128)(2,1)S(1)} custom-call(s32[1]{0:T(128)} %bitcast.refs_0_.me_ref, f32[1]{0:T(128)S(6)} %copy.14.weight_ref, f32[256,1024]{1,0:T(8,128)S(1)} %couple.1.mixed_ref, bf16[1536,256]{1,0:T(8,128)(2,1)S(1)} %get-tuple-element.20.refs_6_.rows_ref, bf16[96,1024]{1,0:T(8,128)(2,1)S(1)} %collective-permute-done.15.refs_0_, ...), custom_call_target="tpu_custom_call" | custom-call | flops 536870912 | bytes 2097152 | tf_op jit(solution)/shard_map/finish/pallas_call | solution.py:304
  50.9 15.6 %all_to_all.5 = bf16[8,128,256]{2,1,0:T(8,128)(2,1)S(1)} all-to-all(bf16[8,128,256]{2,1,0:T(8,128)(2,1)S(1)} %bitcast.7), channel_id=1, replica_groups=mesh['y'=4,'xl'=2,'xh'=2,'z'=4,'core'=2] {'y','xl'}, dimensions={0} | all-to-all | bytes 1048576 | tf_op jit(solution)/shard_map/all_to_all | solution.py:316
  66.6 0.7 %convert_reduce_fusion = f32[128,256]{1,0:T(8,128)} fusion(bf16[8,128,256]{2,1,0:T(8,128)(2,1)S(1)} %all_to_all.5), kind=kLoop, calls=%fused_computation | loop fusion | flops 491520 | bytes 655360 | tf_op jit(solution)/shard_map/reduce_sum | solution.py:317
  (43 shorter events, 1.5 us)
Async XLA Ops:
  0.0 15.7 %collective-permute-start.6 = (bf16[64,1024]{1,0:T(8,128)(2,1)}, bf16[64,1024]{1,0:T(8,128)(2,1)S(1)}, u32[]{:S(2)}, u32[]{:S(2)}) collective-permute-start(bf16[64,1024]{1,0:T(8,128)(2,1)} %bitcast.13), channel_id=1, source_target_pairs={{0,2},{2,4},{4,6},{6,0},{1,3},{3,5},{5,7},{7,1},{8,10},{10,12},{12... | collective-permute-start | bytes 393224 | tf_op jit(solution)/shard_map/ppermute | solution.py:197
  2.0 13.7 %collective-permute-start.7 = (bf16[64,1024]{1,0:T(8,128)(2,1)}, bf16[64,1024]{1,0:T(8,128)(2,1)S(1)}, u32[]{:S(2)}, u32[]{:S(2)}) collective-permute-start(bf16[64,1024]{1,0:T(8,128)(2,1)} %bitcast.14), channel_id=1, source_target_pairs={{0,6},{2,0},{4,2},{6,4},{1,7},{3,1},{5,3},{7,5},{8,14},{10,8},{12,... | collective-permute-start | bytes 393224 | tf_op jit(solution)/shard_map/ppermute | solution.py:197
  4.2 1.9 %copy-start = (s32[1,3,1024]{2,0,1:T(1,128)S(1)}, s32[1,3,1024]{2,0,1:T(1,128)}, u32[]{:S(2)}) copy-start(s32[1,3,1024]{2,0,1:T(1,128)} %param.9) | copy-start | bytes 36868
  4.2 2.0 %copy-start.1 = (f32[1,3,1024]{2,0,1:T(1,128)S(1)}, f32[1,3,1024]{2,0,1:T(1,128)}, u32[]{:S(2)}) copy-start(f32[1,3,1024]{2,0,1:T(1,128)} %param.10) | copy-start | bytes 36868
  4.2 2.0 %copy-start.2 = (s32[1024]{0:T(1024)S(1)}, s32[1024]{0:T(1024)}, u32[]{:S(2)}) copy-start(s32[1024]{0:T(1024)} %param.13) | copy-start | bytes 12292
  9.7 6.0 %copy-start.3 = (bf16[1,64,1024]{2,1,0:T(8,128)(2,1)S(1)}, bf16[1,64,1024]{2,1,0:T(8,128)(2,1)}, u32[]{:S(2)}) copy-start(bf16[1,64,1024]{2,1,0:T(8,128)(2,1)} %param.8) | copy-start | bytes 393220
  12.5 9.3 %collective-permute-start = (bf16[96,1024]{1,0:T(8,128)(2,1)S(1)}, bf16[96,1024]{1,0:T(8,128)(2,1)S(1)}, u32[]{:S(2)}, u32[]{:S(2)}) collective-permute-start(bf16[96,1024]{1,0:T(8,128)(2,1)S(1)} %constant_dynamic-update-slice_fusion), channel_id=1, source_target_pairs={{0,8},{8,0},{1,9},{9,1},{2,10},{10,2},{3,11},{11,3},{4,12},{12,4},... | collective-permute-start | bytes 589832 | tf_op jit(solution)/shard_map/ppermute | solution.py:192
  15.7 5.5 %collective-permute-start.8 = (bf16[32,1024]{1,0:T(8,128)(2,1)S(1)}, bf16[32,1024]{1,0:T(8,128)(2,1)S(1)}, u32[]{:S(2)}, u32[]{:S(2)}) collective-permute-start(bf16[32,1024]{1,0:T(8,128)(2,1)S(1)} %slice.18), channel_id=1, source_target_pairs={{0,2},{2,4},{4,6},{6,0},{1,3},{3,5},{5,7},{7,1},{8,10},{10,12},{12... | collective-permute-start | bytes 196616 | tf_op jit(solution)/shard_map/ppermute | solution.py:197
  15.8 5.4 %collective-permute-start.9 = (bf16[32,1024]{1,0:T(8,128)(2,1)S(1)}, bf16[32,1024]{1,0:T(8,128)(2,1)S(1)}, u32[]{:S(2)}, u32[]{:S(2)}) collective-permute-start(bf16[32,1024]{1,0:T(8,128)(2,1)S(1)} %slice.19), channel_id=1, source_target_pairs={{0,6},{2,0},{4,2},{6,4},{1,7},{3,1},{5,3},{7,5},{8,14},{10,8},{12,... | collective-permute-start | bytes 196616 | tf_op jit(solution)/shard_map/ppermute | solution.py:197
  21.3 12.4 %collective-permute-start.11 = (bf16[192,1024]{1,0:T(8,128)(2,1)S(1)}, bf16[192,1024]{1,0:T(8,128)(2,1)S(1)}, u32[]{:S(2)}, u32[]{:S(2)}) collective-permute-start(bf16[192,1024]{1,0:T(8,128)(2,1)S(1)} %pad_maximum_fusion.1), channel_id=1, source_target_pairs={{0,8},{8,0},{1,9},{9,1},{2,10},{10,2},{3,11},{11,3},{4,12},{12,4},... | collective-permute-start | bytes 1179656 | tf_op jit(solution)/shard_map/ppermute | solution.py:192
  21.9 10.4 %collective-permute-start.1 = (bf16[192,1024]{1,0:T(8,128)(2,1)S(1)}, bf16[192,1024]{1,0:T(8,128)(2,1)S(1)}, u32[]{:S(2)}, u32[]{:S(2)}) collective-permute-start(bf16[192,1024]{1,0:T(8,128)(2,1)S(1)} %pad_maximum_fusion.refs_0_), channel_id=1, source_target_pairs={{0,2},{2,4},{4,6},{6,0},{1,3},{3,5},{5,7},{7,1},{8,10},{10,12},{12... | collective-permute-start | bytes 1179656 | tf_op jit(solution)/shard_map/ppermute | solution.py:197
  22.7 14.3 %collective-permute-start.12 = (bf16[256,1024]{1,0:T(8,128)(2,1)S(1)}, bf16[256,1024]{1,0:T(8,128)(2,1)S(1)}, u32[]{:S(2)}, u32[]{:S(2)}) collective-permute-start(bf16[256,1024]{1,0:T(8,128)(2,1)S(1)} %constant_dynamic-update-slice_fusion.2.refs_0_.refs_4_), channel_id=1, source_target_pairs={{0,1},{1,0},{2,3},{3,2},{4,5},{5,4},{6,7},{7,6},{8,9},{9,8},{10,11... | collective-permute-start | bytes 1572872 | tf_op jit(solution)/shard_map/ppermute | solution.py:201
  22.7 13.9 %collective-permute-start.2 = (bf16[192,1024]{1,0:T(8,128)(2,1)S(1)}, bf16[192,1024]{1,0:T(8,128)(2,1)S(1)}, u32[]{:S(2)}, u32[]{:S(2)}) collective-permute-start(bf16[192,1024]{1,0:T(8,128)(2,1)S(1)} %pad_maximum_fusion.refs_0_), channel_id=1, source_target_pairs={{0,6},{2,0},{4,2},{6,4},{1,7},{3,1},{5,3},{7,5},{8,14},{10,8},{12,... | collective-permute-start | bytes 1179656 | tf_op jit(solution)/shard_map/ppermute | solution.py:197
  25.5 9.6 %collective-permute-start.10 = (bf16[64,1024]{1,0:T(8,128)(2,1)S(1)}, bf16[64,1024]{1,0:T(8,128)(2,1)S(1)}, u32[]{:S(2)}, u32[]{:S(2)}) collective-permute-start(bf16[64,1024]{1,0:T(8,128)(2,1)S(1)} %bitcast.15), channel_id=1, source_target_pairs={{0,8},{8,0},{1,9},{9,1},{2,10},{10,2},{3,11},{11,3},{4,12},{12,4},... | collective-permute-start | bytes 393224 | tf_op jit(solution)/shard_map/ppermute | solution.py:192
  32.3 7.0 %collective-permute-start.15 = (bf16[96,1024]{1,0:T(8,128)(2,1)S(1)}, bf16[96,1024]{1,0:T(8,128)(2,1)S(1)}, u32[]{:S(2)}, u32[]{:S(2)}) collective-permute-start(bf16[96,1024]{1,0:T(8,128)(2,1)S(1)} %slice.20), channel_id=1, source_target_pairs={{0,2},{2,4},{4,6},{6,0},{1,3},{3,5},{5,7},{7,1},{8,10},{10,12},{12... | collective-permute-start | bytes 589832 | tf_op jit(solution)/shard_map/ppermute | solution.py:197
  33.7 11.2 %collective-permute-start.14 = (bf16[192,1024]{1,0:T(8,128)(2,1)S(1)}, bf16[192,1024]{1,0:T(8,128)(2,1)S(1)}, u32[]{:S(2)}, u32[]{:S(2)}) collective-permute-start(bf16[192,1024]{1,0:T(8,128)(2,1)S(1)} %collective-permute-done.11.refs_2_.refs_6_), channel_id=1, source_target_pairs={{0,1},{1,0},{2,3},{3,2},{4,5},{5,4},{6,7},{7,6},{8,9},{9,8},{10,11... | collective-permute-start | bytes 1179656 | tf_op jit(solution)/shard_map/ppermute | solution.py:201
  35.1 1.3 %collective-permute-start.13 = (bf16[64,1024]{1,0:T(8,128)(2,1)S(1)}, bf16[64,1024]{1,0:T(8,128)(2,1)S(1)}, u32[]{:S(2)}, u32[]{:S(2)}) collective-permute-start(bf16[64,1024]{1,0:T(8,128)(2,1)S(1)} %collective-permute-done.10.refs_1_.refs_5_), channel_id=1, source_target_pairs={{0,1},{1,0},{2,3},{3,2},{4,5},{5,4},{6,7},{7,6},{8,9},{9,8},{10,11... | collective-permute-start | bytes 393224 | tf_op jit(solution)/shard_map/ppermute | solution.py:201
  36.5 11.7 %collective-permute-start.3 = (bf16[192,1024]{1,0:T(8,128)(2,1)S(1)}, bf16[192,1024]{1,0:T(8,128)(2,1)S(1)}, u32[]{:S(2)}, u32[]{:S(2)}) collective-permute-start(bf16[192,1024]{1,0:T(8,128)(2,1)S(1)} %pad_maximum_fusion.refs_0_), channel_id=1, source_target_pairs={{0,1},{1,0},{2,3},{3,2},{4,5},{5,4},{6,7},{7,6},{8,9},{9,8},{10,11... | collective-permute-start | bytes 1179656 | tf_op jit(solution)/shard_map/ppermute | solution.py:201
  36.6 11.6 %collective-permute-start.4 = (bf16[192,1024]{1,0:T(8,128)(2,1)S(1)}, bf16[192,1024]{1,0:T(8,128)(2,1)S(1)}, u32[]{:S(2)}, u32[]{:S(2)}) collective-permute-start(bf16[192,1024]{1,0:T(8,128)(2,1)S(1)} %collective-permute-done.1.refs_1_), channel_id=1, source_target_pairs={{0,1},{1,0},{2,3},{3,2},{4,5},{5,4},{6,7},{7,6},{8,9},{9,8},{10,11... | collective-permute-start | bytes 1179656 | tf_op jit(solution)/shard_map/ppermute | solution.py:201
  37.0 11.2 %collective-permute-start.5 = (bf16[192,1024]{1,0:T(8,128)(2,1)S(1)}, bf16[192,1024]{1,0:T(8,128)(2,1)S(1)}, u32[]{:S(2)}, u32[]{:S(2)}) collective-permute-start(bf16[192,1024]{1,0:T(8,128)(2,1)S(1)} %collective-permute-done.2.refs_2_), channel_id=1, source_target_pairs={{0,1},{1,0},{2,3},{3,2},{4,5},{5,4},{6,7},{7,6},{8,9},{9,8},{10,11... | collective-permute-start | bytes 1179656 | tf_op jit(solution)/shard_map/ppermute | solution.py:201
  39.2 5.7 %collective-permute-start.16 = (bf16[96,1024]{1,0:T(8,128)(2,1)S(1)}, bf16[96,1024]{1,0:T(8,128)(2,1)S(1)}, u32[]{:S(2)}, u32[]{:S(2)}) collective-permute-start(bf16[96,1024]{1,0:T(8,128)(2,1)S(1)} %slice.21), channel_id=1, source_target_pairs={{0,6},{2,0},{4,2},{6,4},{1,7},{3,1},{5,3},{7,5},{8,14},{10,8},{12,... | collective-permute-start | bytes 589832 | tf_op jit(solution)/shard_map/ppermute | solution.py:197
  44.9 4.3 %collective-permute-start.17 = (bf16[96,1024]{1,0:T(8,128)(2,1)S(1)}, bf16[96,1024]{1,0:T(8,128)(2,1)S(1)}, u32[]{:S(2)}, u32[]{:S(2)}) collective-permute-start(bf16[96,1024]{1,0:T(8,128)(2,1)S(1)} %collective-permute-done.15.refs_0_), channel_id=1, source_target_pairs={{0,1},{1,0},{2,3},{3,2},{4,5},{5,4},{6,7},{7,6},{8,9},{9,8},{10,11... | collective-permute-start | bytes 589832 | tf_op jit(solution)/shard_map/ppermute | solution.py:201
  44.9 4.3 %collective-permute-start.18 = (bf16[96,1024]{1,0:T(8,128)(2,1)S(1)}, bf16[96,1024]{1,0:T(8,128)(2,1)S(1)}, u32[]{:S(2)}, u32[]{:S(2)}) collective-permute-start(bf16[96,1024]{1,0:T(8,128)(2,1)S(1)} %collective-permute-done.16.refs_1_), channel_id=1, source_target_pairs={{0,1},{1,0},{2,3},{3,2},{4,5},{5,4},{6,7},{7,6},{8,9},{9,8},{10,11... | collective-permute-start | bytes 589832 | tf_op jit(solution)/shard_map/ppermute | solution.py:201

commit v2 on v1

--- a/solution.py
+++ b/solution.py
@@ -85,41 +85,52 @@
             turned_ref[:, first:first + PLANE] = jnp.transpose(coef_ref[first:first + PLANE, :])
 
 
-def eval_kernel(*refs, shards, slots, first, electrons):
-    if first == 0:
-        me_ref, turned_ref, cell_ref, frac_ref, occ_ref, val_ref, lap_ref, lapt_ref, picker_ref, slot_ref, *weight_refs = refs
-    else:
-        turned_ref, cell_ref, frac_ref, picker_ref, val_ref, lap_ref, lapt_ref, *weight_refs = refs
-
-    def build(t, value_ref, lap_ref):
-        here = slice(first + t * TILE, first + (t + 1) * TILE)
-        vx, cx = dense_rows(cell_ref[0, :, here], frac_ref[0, :, here])
-        vy, cy = dense_rows(cell_ref[1, :, here], frac_ref[1, :, here])
-        vz, cz = dense_rows(cell_ref[2, :, here], frac_ref[2, :, here])
-        value = expand(vy, vz)
-        curve = expand(cy, vz) + expand(vy, cz)
-        for g in range(GRID):
-            x_value, x_curve = vx[g:g + 1, :], cx[g:g + 1, :]
-            value_ref[g * PLANE:(g + 1) * PLANE, :] = (x_value * value).astype(BF16)
-            lap_ref[g * PLANE:(g + 1) * PLANE, :] = (x_curve * value + x_value * curve).astype(BF16)
-
-    def product(t, value_w, lap_w):
+def weight_tables(cell_ref, frac_ref, here):
+    tables = [dense_rows(cell_ref[k, :, here], frac_ref[k, :, here]) for k in range(3)]
+    (vx, cx), (vy, cy), (vz, cz) = tables
+    return vx, cx, expand(vy, vz), expand(cy, vz) + expand(vy, cz)
+
+
+def build_laplacian(tables, w_ref):
+    vx, cx, value, curve = tables
+    for g in range(GRID):
+        w_ref[g * PLANE:(g + 1) * PLANE, :] = (cx[g:g + 1, :] * value + vx[g:g + 1, :] * curve).astype(BF16)
+
+
+def build_value(tables, w_ref):
+    vx, _, value, _ = tables
+    for g in range(GRID):
+        w_ref[g * PLANE:(g + 1) * PLANE, :] = (vx[g:g + 1, :] * value).astype(BF16)
+
+
+def early_kernel(me_ref, turned_ref, cell_ref, frac_ref, occ_ref, lapt_ref, slot_ref, *w_refs, shards):
+    slots, electrons = lapt_ref.shape
+    slot, picker = slot_tables(me_ref[0], occ_ref[...], shards, turned_ref.shape[0], slots)
+    slot_ref[...] = slot
+    chosen = mm(picker, turned_ref[...]).astype(BF16)
+    tiles = [slice(first, first + TILE) for first in range(0, electrons, TILE)]
+    build_laplacian(weight_tables(cell_ref, frac_ref, tiles[0]), w_refs[0])
+    for t, here in enumerate(tiles):
+        if t + 1 < len(tiles):
+            build_laplacian(weight_tables(cell_ref, frac_ref, tiles[t + 1]), w_refs[(t + 1) % 2])
+        lapt_ref[:, here] = mm(chosen, w_refs[t % 2][...]).astype(BF16)
+
+
+def eval_kernel(turned_ref, cell_ref, frac_ref, val_ref, lap_ref, *w_refs, first):
+    electrons = val_ref.shape[1]
+
+    def build(t):
+        tables = weight_tables(cell_ref, frac_ref, slice(first + t * TILE, first + (t + 1) * TILE))
+        build_value(tables, w_refs[2 * (t % 2)])
+        build_laplacian(tables, w_refs[2 * (t % 2) + 1])
+
+    build(0)
+    for t in range(electrons // TILE):
+        if (t + 1) * TILE < electrons:
+            build(t + 1)
         here = slice(t * TILE, (t + 1) * TILE)
-        val_ref[:, here] = mm(turned_ref[...], value_w[...]).astype(BF16)
-        lap = mm(turned_ref[...], lap_w[...]).astype(BF16)
-        lap_ref[:, here] = lap
-        lapt_ref[:, here] = mm(picker_ref[...], lap).astype(BF16)
-
-    tiles = electrons // TILE
-    build(0, weight_refs[0], weight_refs[1])
-    if first == 0:
-        slot, picker = slot_tables(me_ref[0], occ_ref[...], shards, turned_ref.shape[0], slots)
-        slot_ref[...] = slot
-        picker_ref[...] = picker
-    for t in range(tiles):
-        if t + 1 < tiles:
-            build(t + 1, *weight_refs[2 * ((t + 1) % 2):][:2])
-        product(t, *weight_refs[2 * (t % 2):][:2])
+        val_ref[:, here] = mm(turned_ref[...], w_refs[2 * (t % 2)][...]).astype(BF16)
+        lap_ref[:, here] = mm(turned_ref[...], w_refs[2 * (t % 2) + 1][...]).astype(BF16)
 
 
 def place(me_ref, z_count):
@@ -220,20 +231,17 @@
     def cost(products):
         return pl.CostEstimate(flops=2 * products, bytes_accessed=2 * cells * width, transcendentals=0)
 
-    def evaluate(h, *operands):
-        results = [out((width, part), BF16), out((width, part), BF16), out((slots, part), BF16)]
-        if h == 0:
-            results += [out((slots, width), BF16), out((1, electrons), jnp.int32)]
+    def evaluate(h):
         return pl.pallas_call(
-            functools.partial(eval_kernel, shards=shards, slots=slots, first=h * part, electrons=part),
-            out_shape=results,
-            in_specs=[SMEM] + [VMEM] * 4 if h == 0 else [VMEM] * 4,
-            out_specs=[VMEM] * len(results),
+            functools.partial(eval_kernel, first=h * part),
+            out_shape=[out((width, part), BF16)] * 2,
+            in_specs=[VMEM] * 3,
+            out_specs=[VMEM] * 2,
             scratch_shapes=[pltpu.VMEM((cells, TILE), BF16)] * 4,
             compiler_params=params(32),
             cost_estimate=cost(2 * part * cells * width),
             name="evaluate",
-        )(*operands)
+        )(turned, cell_index, fraction)
 
     cell_index, fraction = jnp.transpose(cell_index, (1, 0, 2)), jnp.transpose(fraction, (1, 0, 2))
     mine = inverse.reshape(rows, electrons)
@@ -244,12 +252,11 @@
     inv_far_mine = ring_swap(mine)
     inv_first = ring_pass(inv_below[:half], 1)
     inv_second = ring_pass(inv_above[half:], -1)
-    inv_plane = jnp.concatenate([mine, inv_below, inv_above, inv_first, inv_second], axis=0)
-    inv_far_rest = ring_swap(inv_plane[rows:])
-    inv_own = [inv_plane, inv_far_mine, inv_far_rest]
-    inv_others = [core_swap(inv_plane), core_swap(inv_far_mine)]
+    inv_rest = jnp.concatenate([inv_below, inv_above, inv_first, inv_second], axis=0)
+    inv_far_rest = ring_swap(inv_rest)
+    inv_others = [core_swap(mine), core_swap(inv_rest), core_swap(inv_far_mine)]
     inv_others.append(core_swap(inv_far_rest))
-    inv_all = inv_own + inv_others
+    inv_all = [mine, inv_rest, inv_far_mine, inv_far_rest] + inv_others
 
     turned = pl.pallas_call(
         turn_kernel,
@@ -261,10 +268,19 @@
         cost_estimate=cost(cells * width * 64),
         name="turn",
     )(coefficients)
-    val_a, lap_a, lapt_a, picker, slot = evaluate(0, me, turned, cell_index, fraction, occupied.reshape(1, electrons))
-    val_b, lap_b, lapt_b = evaluate(1, turned, cell_index, fraction, picker)
-
-    lapt_mine = jnp.concatenate([lapt_a, lapt_b], axis=1)
+    lapt_mine, slot = pl.pallas_call(
+        functools.partial(early_kernel, shards=shards),
+        out_shape=[out((slots, electrons), BF16), out((1, electrons), jnp.int32)],
+        in_specs=[SMEM] + [VMEM] * 4,
+        out_specs=[VMEM] * 2,
+        scratch_shapes=[pltpu.VMEM((cells, TILE), BF16)] * 2,
+        compiler_params=params(32),
+        cost_estimate=cost(slots * cells * electrons),
+        name="early",
+    )(me, turned, cell_index, fraction, occupied.reshape(1, electrons))
+    val_a, lap_a = evaluate(0)
+    val_b, lap_b = evaluate(1)
+
     lapt_far = ring_swap(lapt_mine)
     lap_pair = jnp.concatenate([lapt_mine, lapt_far], axis=0)
     lap_below = ring_pass(lap_pair, 1)

time: 67.5 us -> 71.6 us (1.061)
  Pallas kernels: 13.7 us -> 17.1 us
  starting transfers between devices: 20 us -> 21.6 us
    ppermute x3, waiting for transfers between devices: 2.73 us -> 8.38 us  [ring_swap(): return lax.ppermute(piece, 'xh', [(0, 1), (1, 0)])]
    ppermute x8, waiting for transfers between devices: 11.4 us -> 6.01 us  [ring_pass(): lax.ppermute(piece, 'z', [(i, (i + shift) % count) for i in range(count)])]
    pallas_call x2 -> x3, Pallas kernels: 6.36 us -> 9.04 us  [the longest x2 5.03 us: evaluate(): pl.pallas_call(functools.partial(eval_kernel, first=h * part), out_shape=...]
    ppermute x8 -> x9, starting transfers between devices: 1.18 us -> 2.04 us  [core_swap(): return lax.ppermute(piece, 'core', [(0, 1), (1, 0)])]
  transfers between devices with their start and end apart: 19 -> 20, of which waited for: 7 -> 6; matrix products, arithmetic and copies ran while one was open for 0% -> 0% of each run, Pallas kernels for 18% -> 21%
where the time goes in v2:
time: 71.6 us; the launch traced here: 71.4 us
  starting transfers between devices  21.6 us (30%)
  Pallas kernels  17.1 us (24%)
  waiting for transfers between devices  15.2 us (21%)
  blocking collectives  15.1 us (21%)
  between operations  1.52 us (2%)
  other arithmetic  0.72 us (1%)
    all_to_all x1, blocking collectives, gradient(): lax.all_to_all(partial.reshape(count, electrons // count, width), walkers...  15.1 us
    ppermute x8, starting transfers between devices, ring_pass(): lax.ppermute(piece, 'z', [(i, (i + shift) % count) for i in range(count)])  12.8 us
    ppermute x3, waiting for transfers between devices, ring_swap(): return lax.ppermute(piece, 'xh', [(0, 1), (1, 0)])  8.38 us
    ppermute x3, starting transfers between devices, ring_swap(): return lax.ppermute(piece, 'xh', [(0, 1), (1, 0)])  6.72 us
    ppermute x8, waiting for transfers between devices, ring_pass(): lax.ppermute(piece, 'z', [(i, (i + shift) % count) for i in range(count)])  6.01 us
    pallas_call x2, Pallas kernels, evaluate(): pl.pallas_call(functools.partial(eval_kernel, first=h * part), out_shape=...  5.03 us
    pallas_call x1, Pallas kernels, gradient(): pl.pallas_call(functools.partial(early_kernel, shards=shards), out_shape=...  4.02 us
    pallas_call x1, Pallas kernels, gradient(): pl.pallas_call(functools.partial(ratio_kernel, parts=len(inv_all), z_coun...  3.07 us
  transfers between devices with their start and end apart: 20, of which 6 were waited for; matrix products, arithmetic and copies ran while one was open for 0% of the time, Pallas kernels for 21%

profile of v2, /device:TPU:0, one launch (start us, length us, event | category | flops | bytes accessed | tf_op | source)
XLA Modules:
  0.0 71.4 jit_solution(17225248612336617448)
XLA Ops:
  0.0 2.0 %collective-permute-start.6 = (bf16[64,1024]{1,0:T(8,128)(2,1)}, bf16[64,1024]{1,0:T(8,128)(2,1)S(1)}, u32[]{:S(2)}, u32[]{:S(2)}) collective-permute-start(bf16[64,1024]{1,0:T(8,128)(2,1)} %bitcast.7), channel_id=1, source_target_pairs={{0,2},{2,4},{4,6},{6,0},{1,3},{3,5},{5,7},{7,1},{8,10},{10,12},{12... | collective-permute-start | bytes 393224 | tf_op jit(solution)/shard_map/ppermute | solution.py:208
  2.0 2.1 %collective-permute-start.7 = (bf16[64,1024]{1,0:T(8,128)(2,1)}, bf16[64,1024]{1,0:T(8,128)(2,1)S(1)}, u32[]{:S(2)}, u32[]{:S(2)}) collective-permute-start(bf16[64,1024]{1,0:T(8,128)(2,1)} %bitcast.8), channel_id=1, source_target_pairs={{0,6},{2,0},{4,2},{6,4},{1,7},{3,1},{5,3},{7,5},{8,14},{10,8},{12,... | collective-permute-start | bytes 393224 | tf_op jit(solution)/shard_map/ppermute | solution.py:208
  4.2 1.9 %turn.1.turned_ref = bf16[256,4096]{1,0:T(8,128)(2,1)S(1)} custom-call(bf16[4096,256]{1,0:T(8,128)(2,1)} %coef_hbm.1), custom_call_target="tpu_custom_call" | custom-call | flops 134217728 | bytes 2097152 | tf_op jit(solution)/shard_map/turn/pallas_call | solution.py:261
  6.1 4.0 %early.1 = (bf16[96,1024]{1,0:T(8,128)(2,1)S(1)}, s32[1,1024]{1,0:T(1,128)S(1)}) custom-call(s32[1]{0:T(128)} %bitcast.me_ref, bf16[256,4096]{1,0:T(8,128)(2,1)S(1)} %turn.1.turned_ref, s32[3,1,1024]{2,1,0:T(1,128)S(1)} %bitcast.13, f32[3,1,1024]{2,1,0:T(1,128)S(1)} %bitcast.16, s32[1,1024]{1,0:T(1,128)S(1)} %bitcast.19), custom_call_target="tpu_custom_call" | custom-call | flops 805306368 | bytes 2097152 | tf_op jit(solution)/shard_map/early/pallas_call | solution.py:271
  10.2 3.1 %collective-permute-start = (bf16[96,1024]{1,0:T(8,128)(2,1)S(1)}, bf16[96,1024]{1,0:T(8,128)(2,1)S(1)}, u32[]{:S(2)}, u32[]{:S(2)}) collective-permute-start(bf16[96,1024]{1,0:T(8,128)(2,1)S(1)} %get-tuple-element.12), channel_id=1, source_target_pairs={{0,8},{8,0},{1,9},{9,1},{2,10},{10,2},{3,11},{11,3},{4,12},{12,4},... | collective-permute-start | bytes 589832 | tf_op jit(solution)/shard_map/ppermute | solution.py:203
  13.4 3.3 %collective-permute-start.9 = (bf16[32,1024]{1,0:T(8,128)(2,1)S(1)}, bf16[32,1024]{1,0:T(8,128)(2,1)S(1)}, u32[]{:S(2)}, u32[]{:S(2)}) collective-permute-start(bf16[32,1024]{1,0:T(8,128)(2,1)S(1)} %slice.17), channel_id=1, source_target_pairs={{0,6},{2,0},{4,2},{6,4},{1,7},{3,1},{5,3},{7,5},{8,14},{10,8},{12,... | collective-permute-start | bytes 196616 | tf_op jit(solution)/shard_map/ppermute | solution.py:208
  16.7 1.4 %collective-permute-done = bf16[96,1024]{1,0:T(8,128)(2,1)S(1)} collective-permute-done((bf16[96,1024]{1,0:T(8,128)(2,1)S(1)}, bf16[96,1024]{1,0:T(8,128)(2,1)S(1)}, u32[]{:S(2)}, u32[]{:S(2)}) %collective-permute-start) | collective-permute-done | bytes 196640 | tf_op jit(solution)/shard_map/ppermute | solution.py:203
  18.2 0.6 collective-permute-done.8
  18.9 2.5 %collective-permute-start.11 = (bf16[192,1024]{1,0:T(8,128)(2,1)S(1)}, bf16[192,1024]{1,0:T(8,128)(2,1)S(1)}, u32[]{:S(2)}, u32[]{:S(2)}) collective-permute-start(bf16[192,1024]{1,0:T(8,128)(2,1)S(1)} %constant_dynamic-update-slice_fusion.2.refs_1_.refs_5_), channel_id=1, source_target_pairs={{0,8},{8,0},{1,9},{9,1},{2,10},{10,2},{3,11},{11,3},{4,12},{12,4},... | collective-permute-start | bytes 1179656 | tf_op jit(solution)/shard_map/ppermute | solution.py:203
  21.4 3.2 %collective-permute-start.2 = (bf16[192,1024]{1,0:T(8,128)(2,1)S(1)}, bf16[192,1024]{1,0:T(8,128)(2,1)S(1)}, u32[]{:S(2)}, u32[]{:S(2)}) collective-permute-start(bf16[192,1024]{1,0:T(8,128)(2,1)S(1)} %constant_dynamic-update-slice_fusion.refs_0_), channel_id=1, source_target_pairs={{0,6},{2,0},{4,2},{6,4},{1,7},{3,1},{5,3},{7,5},{8,14},{10,8},{12,... | collective-permute-start | bytes 1179656 | tf_op jit(solution)/shard_map/ppermute | solution.py:208
  24.6 1.1 %collective-permute-start.10 = (bf16[64,1024]{1,0:T(8,128)(2,1)S(1)}, bf16[64,1024]{1,0:T(8,128)(2,1)S(1)}, u32[]{:S(2)}, u32[]{:S(2)}) collective-permute-start(bf16[64,1024]{1,0:T(8,128)(2,1)S(1)} %bitcast.9), channel_id=1, source_target_pairs={{0,8},{8,0},{1,9},{9,1},{2,10},{10,2},{3,11},{11,3},{4,12},{12,4},... | collective-permute-start | bytes 393224 | tf_op jit(solution)/shard_map/ppermute | solution.py:203
  25.7 7.0 %collective-permute-done.10.refs_2_.refs_6_ = bf16[64,1024]{1,0:T(8,128)(2,1)S(1)} collective-permute-done((bf16[64,1024]{1,0:T(8,128)(2,1)S(1)}, bf16[64,1024]{1,0:T(8,128)(2,1)S(1)}, u32[]{:S(2)}, u32[]{:S(2)}) %collective-permute-start.10) | collective-permute-done | bytes 131104 | tf_op jit(solution)/shard_map/ppermute | solution.py:203
  33.2 0.8 %collective-permute-done.12.refs_4_.refs_8_ = bf16[64,1024]{1,0:T(8,128)(2,1)S(1)} collective-permute-done((bf16[64,1024]{1,0:T(8,128)(2,1)S(1)}, bf16[64,1024]{1,0:T(8,128)(2,1)S(1)}, u32[]{:S(2)}, u32[]{:S(2)}) %collective-permute-start.12) | collective-permute-done | bytes 131104 | tf_op jit(solution)/shard_map/ppermute | solution.py:212
  34.6 0.6 collective-permute-start.16
  35.7 2.5 %evaluate.2 = (bf16[256,512]{1,0:T(8,128)(2,1)S(1)}, bf16[256,512]{1,0:T(8,128)(2,1)S(1)}) custom-call(bf16[256,4096]{1,0:T(8,128)(2,1)S(1)} %turn.1.turned_ref, s32[3,1,1024]{2,1,0:T(1,128)S(1)} %bitcast.14, f32[3,1,1024]{2,1,0:T(1,128)S(1)} %bitcast.17), custom_call_target="tpu_custom_call" | custom-call | flops 2147483648 | bytes 2097152 | tf_op jit(solution)/shard_map/evaluate/pallas_call | solution.py:235
  39.5 3.2 %collective-permute-done.16.refs_0_ = bf16[96,1024]{1,0:T(8,128)(2,1)S(1)} collective-permute-done((bf16[96,1024]{1,0:T(8,128)(2,1)S(1)}, bf16[96,1024]{1,0:T(8,128)(2,1)S(1)}, u32[]{:S(2)}, u32[]{:S(2)}) %collective-permute-start.16) | collective-permute-done | bytes 196640 | tf_op jit(solution)/shard_map/ppermute | solution.py:208
  42.7 1.4 %collective-permute-start.17 = (bf16[96,1024]{1,0:T(8,128)(2,1)S(1)}, bf16[96,1024]{1,0:T(8,128)(2,1)S(1)}, u32[]{:S(2)}, u32[]{:S(2)}) collective-permute-start(bf16[96,1024]{1,0:T(8,128)(2,1)S(1)} %slice.19), channel_id=1, source_target_pairs={{0,6},{2,0},{4,2},{6,4},{1,7},{3,1},{5,3},{7,5},{8,14},{10,8},{12,... | collective-permute-start | bytes 589832 | tf_op jit(solution)/shard_map/ppermute | solution.py:208
  44.2 2.5 %evaluate.3 = (bf16[256,512]{1,0:T(8,128)(2,1)S(1)}, bf16[256,512]{1,0:T(8,128)(2,1)S(1)}) custom-call(bf16[256,4096]{1,0:T(8,128)(2,1)S(1)} %turn.1.turned_ref, s32[3,1,1024]{2,1,0:T(1,128)S(1)} %bitcast.15, f32[3,1,1024]{2,1,0:T(1,128)S(1)} %bitcast.18), custom_call_target="tpu_custom_call" | custom-call | flops 2147483648 | bytes 2097152 | tf_op jit(solution)/shard_map/evaluate/pallas_call | solution.py:235
  46.7 2.1 %collective-permute-done.17.refs_1_ = bf16[96,1024]{1,0:T(8,128)(2,1)S(1)} collective-permute-done((bf16[96,1024]{1,0:T(8,128)(2,1)S(1)}, bf16[96,1024]{1,0:T(8,128)(2,1)S(1)}, u32[]{:S(2)}, u32[]{:S(2)}) %collective-permute-start.17) | collective-permute-done | bytes 196640 | tf_op jit(solution)/shard_map/ppermute | solution.py:208
  49.4 3.1 %ratio.1 = (bf16[1536,256]{1,0:T(8,128)(2,1)S(1)}, bf16[1024,256]{1,0:T(8,128)(2,1)}) custom-call(s32[1]{0:T(128)} %bitcast.me_ref, bf16[64,1024]{1,0:T(8,128)(2,1)S(1)} %bitcast.11, bf16[192,1024]{1,0:T(8,128)(2,1)S(1)} %constant_dynamic-update-slice_fusion.2.refs_1_.refs_5_, bf16[64,1024]{1,0:T(8,128)(2,1)S(1)} %collective-permute-done.10.refs_2_.refs_6_, ...), custom_call_target="tpu_custom_call" | custom-call | flops 1610612736 | bytes 2097152 | tf_op jit(solution)/shard_map/ratio/pallas_call | solution.py:300
  52.4 1.1 %couple.1.mixed_ref = f32[256,1024]{1,0:T(8,128)S(1)} custom-call(f32[1]{0:T(128)S(6)} %copy.12.energy_ref, f32[1]{0:T(128)S(6)} %copy.13.weight_ref, bf16[192,1024]{1,0:T(8,128)(2,1)S(1)} %constant_dynamic-update-slice_fusion.refs_0_, bf16[192,1024]{1,0:T(8,128)(2,1)S(1)} %collective-permute-done.1.refs_1_, ...), custom_call_target="tpu_custom_call" | custom-call | flops 536870912 | bytes 2097152 | tf_op jit(solution)/shard_map/couple/pallas_call | solution.py:310
  53.5 2.0 %finish.1 = bf16[1024,256]{1,0:T(8,128)(2,1)S(1)} custom-call(s32[1]{0:T(128)} %bitcast.me_ref, f32[1]{0:T(128)S(6)} %copy.13.weight_ref, f32[256,1024]{1,0:T(8,128)S(1)} %couple.1.mixed_ref, bf16[1536,256]{1,0:T(8,128)(2,1)S(1)} %get-tuple-element.16.refs_6_.rows_ref, bf16[96,1024]{1,0:T(8,128)(2,1)S(1)} %collective-permute-done.16.refs_0_, ...), custom_call_target="tpu_custom_call" | custom-call | flops 536870912 | bytes 2097152 | tf_op jit(solution)/shard_map/finish/pallas_call | solution.py:320
  55.6 15.1 %all_to_all.5 = bf16[8,128,256]{2,1,0:T(8,128)(2,1)S(1)} all-to-all(bf16[8,128,256]{2,1,0:T(8,128)(2,1)S(1)} %bitcast.6), channel_id=1, replica_groups=mesh['y'=4,'xl'=2,'xh'=2,'z'=4,'core'=2] {'y','xl'}, dimensions={0} | all-to-all | bytes 1048576 | tf_op jit(solution)/shard_map/all_to_all | solution.py:332
  70.7 0.7 %convert_reduce_fusion = f32[128,256]{1,0:T(8,128)} fusion(bf16[8,128,256]{2,1,0:T(8,128)(2,1)S(1)} %all_to_all.5), kind=kLoop, calls=%fused_computation | loop fusion | flops 491520 | bytes 655360 | tf_op jit(solution)/shard_map/reduce_sum | solution.py:333
  (43 shorter events, 2.3 us)
Async XLA Ops:
  0.0 13.3 %collective-permute-start.6 = (bf16[64,1024]{1,0:T(8,128)(2,1)}, bf16[64,1024]{1,0:T(8,128)(2,1)S(1)}, u32[]{:S(2)}, u32[]{:S(2)}) collective-permute-start(bf16[64,1024]{1,0:T(8,128)(2,1)} %bitcast.7), channel_id=1, source_target_pairs={{0,2},{2,4},{4,6},{6,0},{1,3},{3,5},{5,7},{7,1},{8,10},{10,12},{12... | collective-permute-start | bytes 393224 | tf_op jit(solution)/shard_map/ppermute | solution.py:208
  2.0 11.4 %collective-permute-start.7 = (bf16[64,1024]{1,0:T(8,128)(2,1)}, bf16[64,1024]{1,0:T(8,128)(2,1)S(1)}, u32[]{:S(2)}, u32[]{:S(2)}) collective-permute-start(bf16[64,1024]{1,0:T(8,128)(2,1)} %bitcast.8), channel_id=1, source_target_pairs={{0,6},{2,0},{4,2},{6,4},{1,7},{3,1},{5,3},{7,5},{8,14},{10,8},{12,... | collective-permute-start | bytes 393224 | tf_op jit(solution)/shard_map/ppermute | solution.py:208
  4.2 1.9 %copy-start.1 = (s32[1,3,1024]{2,0,1:T(1,128)S(1)}, s32[1,3,1024]{2,0,1:T(1,128)}, u32[]{:S(2)}) copy-start(s32[1,3,1024]{2,0,1:T(1,128)} %param.9) | copy-start | bytes 36868
  4.2 2.0 %copy-start.2 = (f32[1,3,1024]{2,0,1:T(1,128)S(1)}, f32[1,3,1024]{2,0,1:T(1,128)}, u32[]{:S(2)}) copy-start(f32[1,3,1024]{2,0,1:T(1,128)} %param.10) | copy-start | bytes 36868
  4.2 2.0 %copy-start.3 = (s32[1024]{0:T(1024)S(1)}, s32[1024]{0:T(1024)}, u32[]{:S(2)}) copy-start(s32[1024]{0:T(1024)} %param.13) | copy-start | bytes 12292
  6.1 18.5 %copy-start = (bf16[1,64,1024]{2,1,0:T(8,128)(2,1)S(1)}, bf16[1,64,1024]{2,1,0:T(8,128)(2,1)}, u32[]{:S(2)}) copy-start(bf16[1,64,1024]{2,1,0:T(8,128)(2,1)} %param.8) | copy-start | bytes 393220
  10.2 7.9 %collective-permute-start = (bf16[96,1024]{1,0:T(8,128)(2,1)S(1)}, bf16[96,1024]{1,0:T(8,128)(2,1)S(1)}, u32[]{:S(2)}, u32[]{:S(2)}) collective-permute-start(bf16[96,1024]{1,0:T(8,128)(2,1)S(1)} %get-tuple-element.12), channel_id=1, source_target_pairs={{0,8},{8,0},{1,9},{9,1},{2,10},{10,2},{3,11},{11,3},{4,12},{12,4},... | collective-permute-start | bytes 589832 | tf_op jit(solution)/shard_map/ppermute | solution.py:203
  13.3 5.5 %collective-permute-start.8 = (bf16[32,1024]{1,0:T(8,128)(2,1)S(1)}, bf16[32,1024]{1,0:T(8,128)(2,1)S(1)}, u32[]{:S(2)}, u32[]{:S(2)}) collective-permute-start(bf16[32,1024]{1,0:T(8,128)(2,1)S(1)} %slice.16), channel_id=1, source_target_pairs={{0,2},{2,4},{4,6},{6,0},{1,3},{3,5},{5,7},{7,1},{8,10},{10,12},{12... | collective-permute-start | bytes 196616 | tf_op jit(solution)/shard_map/ppermute | solution.py:208
  13.4 5.4 %collective-permute-start.9 = (bf16[32,1024]{1,0:T(8,128)(2,1)S(1)}, bf16[32,1024]{1,0:T(8,128)(2,1)S(1)}, u32[]{:S(2)}, u32[]{:S(2)}) collective-permute-start(bf16[32,1024]{1,0:T(8,128)(2,1)S(1)} %slice.17), channel_id=1, source_target_pairs={{0,6},{2,0},{4,2},{6,4},{1,7},{3,1},{5,3},{7,5},{8,14},{10,8},{12,... | collective-permute-start | bytes 196616 | tf_op jit(solution)/shard_map/ppermute | solution.py:208
  18.1 14.6 %collective-permute-start.1 = (bf16[192,1024]{1,0:T(8,128)(2,1)S(1)}, bf16[192,1024]{1,0:T(8,128)(2,1)S(1)}, u32[]{:S(2)}, u32[]{:S(2)}) collective-permute-start(bf16[192,1024]{1,0:T(8,128)(2,1)S(1)} %constant_dynamic-update-slice_fusion.refs_0_), channel_id=1, source_target_pairs={{0,2},{2,4},{4,6},{6,0},{1,3},{3,5},{5,7},{7,1},{8,10},{10,12},{12... | collective-permute-start | bytes 1179656 | tf_op jit(solution)/shard_map/ppermute | solution.py:208
  18.9 15.3 %collective-permute-start.11 = (bf16[192,1024]{1,0:T(8,128)(2,1)S(1)}, bf16[192,1024]{1,0:T(8,128)(2,1)S(1)}, u32[]{:S(2)}, u32[]{:S(2)}) collective-permute-start(bf16[192,1024]{1,0:T(8,128)(2,1)S(1)} %constant_dynamic-update-slice_fusion.2.refs_1_.refs_5_), channel_id=1, source_target_pairs={{0,8},{8,0},{1,9},{9,1},{2,10},{10,2},{3,11},{11,3},{4,12},{12,4},... | collective-permute-start | bytes 1179656 | tf_op jit(solution)/shard_map/ppermute | solution.py:203
  21.4 13.8 %collective-permute-start.13 = (bf16[192,1024]{1,0:T(8,128)(2,1)S(1)}, bf16[192,1024]{1,0:T(8,128)(2,1)S(1)}, u32[]{:S(2)}, u32[]{:S(2)}) collective-permute-start(bf16[192,1024]{1,0:T(8,128)(2,1)S(1)} %constant_dynamic-update-slice_fusion.2.refs_1_.refs_5_), channel_id=1, source_target_pairs={{0,1},{1,0},{2,3},{3,2},{4,5},{5,4},{6,7},{7,6},{8,9},{9,8},{10,11... | collective-permute-start | bytes 1179656 | tf_op jit(solution)/shard_map/ppermute | solution.py:212
  21.4 13.8 %collective-permute-start.2 = (bf16[192,1024]{1,0:T(8,128)(2,1)S(1)}, bf16[192,1024]{1,0:T(8,128)(2,1)S(1)}, u32[]{:S(2)}, u32[]{:S(2)}) collective-permute-start(bf16[192,1024]{1,0:T(8,128)(2,1)S(1)} %constant_dynamic-update-slice_fusion.refs_0_), channel_id=1, source_target_pairs={{0,6},{2,0},{4,2},{6,4},{1,7},{3,1},{5,3},{7,5},{8,14},{10,8},{12,... | collective-permute-start | bytes 1179656 | tf_op jit(solution)/shard_map/ppermute | solution.py:208
  24.6 8.1 %collective-permute-start.10 = (bf16[64,1024]{1,0:T(8,128)(2,1)S(1)}, bf16[64,1024]{1,0:T(8,128)(2,1)S(1)}, u32[]{:S(2)}, u32[]{:S(2)}) collective-permute-start(bf16[64,1024]{1,0:T(8,128)(2,1)S(1)} %bitcast.9), channel_id=1, source_target_pairs={{0,8},{8,0},{1,9},{9,1},{2,10},{10,2},{3,11},{11,3},{4,12},{12,4},... | collective-permute-start | bytes 393224 | tf_op jit(solution)/shard_map/ppermute | solution.py:203
  32.7 1.3 %collective-permute-start.12 = (bf16[64,1024]{1,0:T(8,128)(2,1)S(1)}, bf16[64,1024]{1,0:T(8,128)(2,1)S(1)}, u32[]{:S(2)}, u32[]{:S(2)}) collective-permute-start(bf16[64,1024]{1,0:T(8,128)(2,1)S(1)} %bitcast.10), channel_id=1, source_target_pairs={{0,1},{1,0},{2,3},{3,2},{4,5},{5,4},{6,7},{7,6},{8,9},{9,8},{10,11... | collective-permute-start | bytes 393224 | tf_op jit(solution)/shard_map/ppermute | solution.py:212
  32.7 1.9 %collective-permute-start.14 = (bf16[64,1024]{1,0:T(8,128)(2,1)S(1)}, bf16[64,1024]{1,0:T(8,128)(2,1)S(1)}, u32[]{:S(2)}, u32[]{:S(2)}) collective-permute-start(bf16[64,1024]{1,0:T(8,128)(2,1)S(1)} %collective-permute-done.10.refs_2_.refs_6_), channel_id=1, source_target_pairs={{0,1},{1,0},{2,3},{3,2},{4,5},{5,4},{6,7},{7,6},{8,9},{9,8},{10,11... | collective-permute-start | bytes 393224 | tf_op jit(solution)/shard_map/ppermute | solution.py:212
  34.1 18.4 %collective-permute-start.3 = (bf16[192,1024]{1,0:T(8,128)(2,1)S(1)}, bf16[192,1024]{1,0:T(8,128)(2,1)S(1)}, u32[]{:S(2)}, u32[]{:S(2)}) collective-permute-start(bf16[192,1024]{1,0:T(8,128)(2,1)S(1)} %constant_dynamic-update-slice_fusion.refs_0_), channel_id=1, source_target_pairs={{0,1},{1,0},{2,3},{3,2},{4,5},{5,4},{6,7},{7,6},{8,9},{9,8},{10,11... | collective-permute-start | bytes 1179656 | tf_op jit(solution)/shard_map/ppermute | solution.py:212
  34.2 14.6 %collective-permute-start.15 = (bf16[192,1024]{1,0:T(8,128)(2,1)S(1)}, bf16[192,1024]{1,0:T(8,128)(2,1)S(1)}, u32[]{:S(2)}, u32[]{:S(2)}) collective-permute-start(bf16[192,1024]{1,0:T(8,128)(2,1)S(1)} %collective-permute-done.11.refs_3_.refs_7_), channel_id=1, source_target_pairs={{0,1},{1,0},{2,3},{3,2},{4,5},{5,4},{6,7},{7,6},{8,9},{9,8},{10,11... | collective-permute-start | bytes 1179656 | tf_op jit(solution)/shard_map/ppermute | solution.py:212
  34.6 8.2 %collective-permute-start.16 = (bf16[96,1024]{1,0:T(8,128)(2,1)S(1)}, bf16[96,1024]{1,0:T(8,128)(2,1)S(1)}, u32[]{:S(2)}, u32[]{:S(2)}) collective-permute-start(bf16[96,1024]{1,0:T(8,128)(2,1)S(1)} %slice.18), channel_id=1, source_target_pairs={{0,2},{2,4},{4,6},{6,0},{1,3},{3,5},{5,7},{7,1},{8,10},{10,12},{12... | collective-permute-start | bytes 589832 | tf_op jit(solution)/shard_map/ppermute | solution.py:208
  35.2 17.2 %collective-permute-start.4 = (bf16[192,1024]{1,0:T(8,128)(2,1)S(1)}, bf16[192,1024]{1,0:T(8,128)(2,1)S(1)}, u32[]{:S(2)}, u32[]{:S(2)}) collective-permute-start(bf16[192,1024]{1,0:T(8,128)(2,1)S(1)} %collective-permute-done.1.refs_1_), channel_id=1, source_target_pairs={{0,1},{1,0},{2,3},{3,2},{4,5},{5,4},{6,7},{7,6},{8,9},{9,8},{10,11... | collective-permute-start | bytes 1179656 | tf_op jit(solution)/shard_map/ppermute | solution.py:212
  35.2 17.2 %collective-permute-start.5 = (bf16[192,1024]{1,0:T(8,128)(2,1)S(1)}, bf16[192,1024]{1,0:T(8,128)(2,1)S(1)}, u32[]{:S(2)}, u32[]{:S(2)}) collective-permute-start(bf16[192,1024]{1,0:T(8,128)(2,1)S(1)} %collective-permute-done.2.refs_2_), channel_id=1, source_target_pairs={{0,1},{1,0},{2,3},{3,2},{4,5},{5,4},{6,7},{7,6},{8,9},{9,8},{10,11... | collective-permute-start | bytes 1179656 | tf_op jit(solution)/shard_map/ppermute | solution.py:212
  42.7 6.1 %collective-permute-start.17 = (bf16[96,1024]{1,0:T(8,128)(2,1)S(1)}, bf16[96,1024]{1,0:T(8,128)(2,1)S(1)}, u32[]{:S(2)}, u32[]{:S(2)}) collective-permute-start(bf16[96,1024]{1,0:T(8,128)(2,1)S(1)} %slice.19), channel_id=1, source_target_pairs={{0,6},{2,0},{4,2},{6,4},{1,7},{3,1},{5,3},{7,5},{8,14},{10,8},{12,... | collective-permute-start | bytes 589832 | tf_op jit(solution)/shard_map/ppermute | solution.py:208
  48.8 4.7 %collective-permute-start.18 = (bf16[96,1024]{1,0:T(8,128)(2,1)S(1)}, bf16[96,1024]{1,0:T(8,128)(2,1)S(1)}, u32[]{:S(2)}, u32[]{:S(2)}) collective-permute-start(bf16[96,1024]{1,0:T(8,128)(2,1)S(1)} %collective-permute-done.16.refs_0_), channel_id=1, source_target_pairs={{0,1},{1,0},{2,3},{3,2},{4,5},{5,4},{6,7},{7,6},{8,9},{9,8},{10,11... | collective-permute-start | bytes 589832 | tf_op jit(solution)/shard_map/ppermute | solution.py:212
  48.9 4.7 %collective-permute-start.19 = (bf16[96,1024]{1,0:T(8,128)(2,1)S(1)}, bf16[96,1024]{1,0:T(8,128)(2,1)S(1)}, u32[]{:S(2)}, u32[]{:S(2)}) collective-permute-start(bf16[96,1024]{1,0:T(8,128)(2,1)S(1)} %collective-permute-done.17.refs_1_), channel_id=1, source_target_pairs={{0,1},{1,0},{2,3},{3,2},{4,5},{5,4},{6,7},{7,6},{8,9},{9,8},{10,11... | collective-permute-start | bytes 589832 | tf_op jit(solution)/shard_map/ppermute | solution.py:212

commit v3 on v2

--- a/solution.py
+++ b/solution.py
@@ -103,9 +103,11 @@
         w_ref[g * PLANE:(g + 1) * PLANE, :] = (vx[g:g + 1, :] * value).astype(BF16)
 
 
-def early_kernel(me_ref, turned_ref, cell_ref, frac_ref, occ_ref, lapt_ref, slot_ref, *w_refs, shards):
+def early_kernel(turned_ref, cell_ref, frac_ref, occ_ref, lapt_ref, slot_ref, *w_refs, shards):
     slots, electrons = lapt_ref.shape
-    slot, picker = slot_tables(me_ref[0], occ_ref[...], shards, turned_ref.shape[0], slots)
+    plane, along, core = place(shards // 4)
+    me = (plane * (shards // 4) + along[0]) * 2 + core
+    slot, picker = slot_tables(me, occ_ref[...], shards, turned_ref.shape[0], slots)
     slot_ref[...] = slot
     chosen = mm(picker, turned_ref[...]).astype(BF16)
     tiles = [slice(first, first + TILE) for first in range(0, electrons, TILE)]
@@ -133,18 +135,18 @@
         lap_ref[:, here] = mm(turned_ref[...], w_refs[2 * (t % 2) + 1][...]).astype(BF16)
 
 
-def place(me_ref, z_count):
-    me = me_ref[0]
-    core = lax.rem(me, 2)
-    z = lax.rem(lax.div(me, 2), z_count)
-    plane = lax.div(me, 2 * z_count)
-    along = [lax.rem(z + dz, z_count) for dz in (0, z_count - 1, 1, 2)]
-    return plane, along, core
-
-
-def inverse_times(me_ref, z_count, inv_refs, right, out_ref, size):
-    plane, along, core = place(me_ref, z_count)
-    blocks = [(p * z_count + z) * 2 + c for c in (core, 1 - core) for p in (plane, 1 - plane) for z in along]
+def place(z_count):
+    core, z, plane = lax.axis_index("core"), lax.axis_index("z"), lax.axis_index("xh")
+    return plane, [lax.rem(z + dz, z_count) for dz in (0, z_count - 1, 1, 2)], core
+
+
+def owners(z_count):
+    plane, along, core = place(z_count)
+    return [(p * z_count + z) * 2 + c for c in (core, 1 - core) for p in (plane, 1 - plane) for z in along]
+
+
+def inverse_times(z_count, inv_refs, right, out_ref, size):
+    blocks = owners(z_count)
     first = 0
     for ref in inv_refs:
         value = mm_nt(ref[...], right).astype(out_ref.dtype)
@@ -155,15 +157,14 @@
         first += count
 
 
-def ratio_kernel(me_ref, *refs, parts, z_count, slots, size):
+def ratio_kernel(*refs, parts, z_count, slots, size):
     inv_refs, val_refs = refs[:parts], refs[parts:-3]
     slot_ref, rows_ref, ratio_ref = refs[-3:]
     val = jnp.concatenate([ref[...] for ref in val_refs], axis=1)
-    inverse_times(me_ref, z_count, inv_refs, val, ratio_ref, size)
+    inverse_times(z_count, inv_refs, val, ratio_ref, size)
     ratio = ratio_ref[...]
     slot = slot_ref[...]
-    plane, along, core = place(me_ref, z_count)
-    blocks = [(p * z_count + z) * 2 + c for c in (core, 1 - core) for z in along for p in (plane, 1 - plane)]
+    blocks = owners(z_count)
     for j in range(0, len(blocks), 2):
         ids = lax.broadcasted_iota(jnp.int32, (slots, slot.shape[1]), 0)
         pick = jnp.concatenate([(ids + block * slots == slot).astype(F32) for block in blocks[j:j + 2]], axis=0)
@@ -178,24 +179,24 @@
     return total
 
 
-def couple_kernel(energy_ref, weight_ref, *refs, firsts):
-    near_refs = refs[:len(firsts)]
-    rows_ref, val_a, val_b, lap_a, lap_b, mixed_ref = refs[len(firsts):]
-    total = coupled(rows_ref, list(zip(firsts, near_refs)))
+def couple_kernel(energy_ref, weight_ref, near_own_ref, near_other_ref, rows_ref, val_a, val_b, lap_a, lap_b, mixed_ref):
+    half = rows_ref.shape[0] // 2
+    total = coupled(rows_ref, [(0, near_own_ref), (half, near_other_ref)])
     val = jnp.concatenate([val_a[...], val_b[...]], axis=1).astype(F32)
     lap = jnp.concatenate([lap_a[...], lap_b[...]], axis=1).astype(F32)
-    mixed_ref[...] = weight_ref[0] * (energy_ref[0] * val - 0.5 * (lap - total))
-
-
-def finish_kernel(me_ref, weight_ref, mixed_ref, rows_ref, *refs, firsts, z_count, size):
-    far_refs, inv_refs, out_ref = refs[:len(firsts)], refs[len(firsts):-1], refs[-1]
-    total = coupled(rows_ref, list(zip(firsts, far_refs)))
-    mixed = (mixed_ref[...] + (0.5 * weight_ref[0]) * total).astype(BF16)
-    inverse_times(me_ref, z_count, inv_refs, mixed, out_ref, size)
+    mixed_ref[...] = energy_ref[...] * val - 0.5 * (lap - total)
+
+
+def finish_kernel(weight_ref, mixed_ref, rows_ref, far_own_ref, far_other_ref, *refs, z_count, size):
+    inv_refs, out_ref = refs[:-1], refs[-1]
+    half = rows_ref.shape[0] // 2
+    near = half - far_own_ref.shape[0]
+    total = coupled(rows_ref, [(near, far_own_ref), (half + near, far_other_ref)])
+    mixed = (weight_ref[...] * (mixed_ref[...] + 0.5 * total)).astype(BF16)
+    inverse_times(z_count, inv_refs, mixed, out_ref, size)
 
 
 VMEM = pl.BlockSpec(memory_space=pltpu.VMEM)
-SMEM = pl.BlockSpec(memory_space=pltpu.SMEM)
 HBM = pl.BlockSpec(memory_space=pltpu.HBM)
 
 
@@ -218,9 +219,8 @@
     z_count = lax.axis_size("z")
     shards = 2 * z_count * 2
     slots = 3 * electrons // (2 * shards)
-    xh, z, core = lax.axis_index("xh"), lax.axis_index("z"), lax.axis_index("core")
-    me = ((xh * z_count + z) * 2 + core).astype(jnp.int32).reshape(1)
-
+
+    along_z = (1, -1, 2)
     out = lambda *shape_dtype: jax.ShapeDtypeStruct(*shape_dtype)
     halves = 2
     part = electrons // halves
@@ -245,25 +245,22 @@
 
     cell_index, fraction = jnp.transpose(cell_index, (1, 0, 2)), jnp.transpose(fraction, (1, 0, 2))
     mine = inverse.reshape(rows, electrons)
-    half = rows // 2
-
-    inv_below = ring_pass(mine, 1)
-    inv_above = ring_pass(mine, -1)
-    inv_far_mine = ring_swap(mine)
-    inv_first = ring_pass(inv_below[:half], 1)
-    inv_second = ring_pass(inv_above[half:], -1)
-    inv_rest = jnp.concatenate([inv_below, inv_above, inv_first, inv_second], axis=0)
-    inv_far_rest = ring_swap(inv_rest)
-    inv_others = [core_swap(mine), core_swap(inv_rest), core_swap(inv_far_mine)]
-    inv_others.append(core_swap(inv_far_rest))
-    inv_all = [mine, inv_rest, inv_far_mine, inv_far_rest] + inv_others
+
+    inv_pieces = [mine]
+    for shift in along_z:
+        inv_pieces.append(ring_pass(mine, shift))
+    inv_plane = jnp.concatenate(inv_pieces, axis=0)
+    inv_far = ring_swap(inv_plane)
+    inv_plane_other = core_swap(inv_plane)
+    inv_far_other = core_swap(inv_far)
+    inv_all = [inv_plane, inv_far, inv_plane_other, inv_far_other]
 
     turned = pl.pallas_call(
         turn_kernel,
         out_shape=out((width, cells), BF16),
         in_specs=[HBM],
         out_specs=VMEM,
-        scratch_shapes=[pltpu.VMEM((cells, width), BF16), pltpu.SemaphoreType.DMA((4,))],
+        scratch_shapes=[pltpu.VMEM((cells, width), BF16), pltpu.SemaphoreType.DMA((8,))],
         compiler_params=params(50),
         cost_estimate=cost(cells * width * 64),
         name="turn",
@@ -271,61 +268,60 @@
     lapt_mine, slot = pl.pallas_call(
         functools.partial(early_kernel, shards=shards),
         out_shape=[out((slots, electrons), BF16), out((1, electrons), jnp.int32)],
-        in_specs=[SMEM] + [VMEM] * 4,
+        in_specs=[VMEM] * 4,
         out_specs=[VMEM] * 2,
         scratch_shapes=[pltpu.VMEM((cells, TILE), BF16)] * 2,
         compiler_params=params(32),
         cost_estimate=cost(slots * cells * electrons),
         name="early",
-    )(me, turned, cell_index, fraction, occupied.reshape(1, electrons))
+    )(turned, cell_index, fraction, occupied.reshape(1, electrons))
     val_a, lap_a = evaluate(0)
     val_b, lap_b = evaluate(1)
 
     lapt_far = ring_swap(lapt_mine)
-    lap_pair = jnp.concatenate([lapt_mine, lapt_far], axis=0)
-    lap_below = ring_pass(lap_pair, 1)
-    lap_above = ring_pass(lap_pair, -1)
-    lap_first = ring_pass(lap_below[:slots], 1)
-    lap_second = ring_pass(lap_above[slots:], -1)
-    near = [lap_pair, lap_below, lap_above]
-    far = [lap_first, lap_second]
-    near += [core_swap(piece) for piece in near]
-    far += [core_swap(piece) for piece in far]
+    near, far = [lapt_mine], []
+    for shift in along_z:
+        near.append(ring_pass(lapt_mine, shift))
+    near.append(lapt_far)
+    for shift in along_z:
+        far.append(ring_pass(lapt_far, shift))
+    near = jnp.concatenate(near, axis=0)
+    far = jnp.concatenate(far, axis=0)
+    near_other = core_swap(near)
+    far_other = core_swap(far)
     total = shards * slots
-    near_firsts = [0, 2 * slots, 4 * slots]
-    near_firsts += [first + total // 2 for first in near_firsts]
-    far_firsts = [6 * slots, 7 * slots]
-    far_firsts += [first + total // 2 for first in far_firsts]
-
-    ratio_rows, _ = pl.pallas_call(
+
+    ratio_rows = pl.pallas_call(
         functools.partial(ratio_kernel, parts=len(inv_all), z_count=z_count, slots=slots, size=rows),
-        out_shape=[out((total, width), BF16), out((electrons, width), BF16)],
-        in_specs=[SMEM] + [VMEM] * (len(inv_all) + 3),
-        out_specs=[VMEM] * 2,
+        out_shape=out((total, width), BF16),
+        in_specs=[VMEM] * (len(inv_all) + 3),
+        out_specs=VMEM,
+        scratch_shapes=[pltpu.VMEM((electrons, width), BF16)],
         compiler_params=params(24),
         cost_estimate=cost(3 * electrons * electrons * width),
         name="ratio",
-    )(me, *inv_all, val_a, val_b, slot)
-
+    )(*inv_all, val_a, val_b, slot)
+
+    energy, weight = energies.reshape(1, 1), weights.reshape(1, 1)
     mixed = pl.pallas_call(
-        functools.partial(couple_kernel, firsts=near_firsts),
+        couple_kernel,
         out_shape=out((width, electrons), F32),
-        in_specs=[SMEM] * 2 + [VMEM] * (len(near) + 5),
+        in_specs=[VMEM] * 9,
         out_specs=VMEM,
         compiler_params=params(24),
         cost_estimate=cost(electrons * electrons * width),
         name="couple",
-    )(energies, weights, *near, ratio_rows, val_a, val_b, lap_a, lap_b)
+    )(energy, weight, near, near_other, ratio_rows, val_a, val_b, lap_a, lap_b)
 
     partial = pl.pallas_call(
-        functools.partial(finish_kernel, firsts=far_firsts, z_count=z_count, size=rows),
+        functools.partial(finish_kernel, z_count=z_count, size=rows),
         out_shape=out((electrons, width), BF16),
-        in_specs=[SMEM] * 2 + [VMEM] * (2 + len(far) + len(inv_all)),
+        in_specs=[VMEM] * (5 + len(inv_all)),
         out_specs=VMEM,
         compiler_params=params(24),
         cost_estimate=cost(electrons * electrons * width),
         name="finish",
-    )(me, weights, mixed, ratio_rows, *far, *inv_all)
+    )(weight, mixed, ratio_rows, far, far_other, *inv_all)
 
     walkers = ("y", "xl")
     count = lax.axis_size(walkers)

time: 71.6 us -> 63.3 us (0.88)
  waiting for transfers between devices: 15.2 us -> 11.7 us
  starting transfers between devices: 21.6 us -> 18.6 us
  Pallas kernels: 17.1 us -> 14.9 us
    ppermute x3 -> x2, waiting for transfers between devices: 8.38 us -> 3.76 us  [ring_swap(): return lax.ppermute(piece, 'xh', [(0, 1), (1, 0)])]
    ppermute x3 -> x2, starting transfers between devices: 6.72 us -> 3.6 us  [ring_swap(): return lax.ppermute(piece, 'xh', [(0, 1), (1, 0)])]
    ppermute x8 -> x9, waiting for transfers between devices: 6.01 us -> 7.95 us  [ring_pass(): lax.ppermute(piece, 'z', [(i, (i + shift) % count) for i in range(count)])]
    pallas_call x1, Pallas kernels: 3.07 us -> 1.74 us  [gradient(): pl.pallas_call(functools.partial(ratio_kernel, parts=len(inv_all), z_coun...]
    ppermute x8 -> x9, starting transfers between devices: 12.8 us -> 14.1 us  [ring_pass(): lax.ppermute(piece, 'z', [(i, (i + shift) % count) for i in range(count)])]
    ppermute x9 -> x4, starting transfers between devices: 2.04 us -> 0.93 us  [core_swap(): return lax.ppermute(piece, 'core', [(0, 1), (1, 0)])]
    pallas_call x2, Pallas kernels: 3.09 us -> 2.08 us  [the longest x1 1.32 us: gradient(): pl.pallas_call(functools.partial(finish_kernel, z_count=z_count, size=row...]
    ppermute x9 -> x4, waiting for transfers between devices: 0.84 us -> 0.01 us  [core_swap(): return lax.ppermute(piece, 'core', [(0, 1), (1, 0)])]
  transfers between devices with their start and end apart: 20 -> 15, of which waited for: 6 -> 5; matrix products, arithmetic and copies ran while one was open for 0% -> 0% of each run, Pallas kernels for 21% -> 22%
where the time goes in v3:
time: 63.3 us; the launch traced here: 62.9 us
  starting transfers between devices  18.6 us (29%)
  blocking collectives  15.3 us (24%)
  Pallas kernels  14.9 us (24%)
  waiting for transfers between devices  11.7 us (18%)
  between operations  1.5 us (2%)
  other arithmetic  0.76 us (1%)
    all_to_all x1, blocking collectives, gradient(): lax.all_to_all(partial.reshape(count, electrons // count, width), walkers...  15.3 us
    ppermute x9, starting transfers between devices, ring_pass(): lax.ppermute(piece, 'z', [(i, (i + shift) % count) for i in range(count)])  14.1 us
    ppermute x9, waiting for transfers between devices, ring_pass(): lax.ppermute(piece, 'z', [(i, (i + shift) % count) for i in range(count)])  7.95 us
    pallas_call x2, Pallas kernels, evaluate(): pl.pallas_call(functools.partial(eval_kernel, first=h * part), out_shape=...  5.03 us
    pallas_call x1, Pallas kernels, gradient(): pl.pallas_call(functools.partial(early_kernel, shards=shards), out_shape=...  4.01 us
    ppermute x2, waiting for transfers between devices, ring_swap(): return lax.ppermute(piece, 'xh', [(0, 1), (1, 0)])  3.76 us
    ppermute x2, starting transfers between devices, ring_swap(): return lax.ppermute(piece, 'xh', [(0, 1), (1, 0)])  3.6 us
    pallas_call x1, Pallas kernels, gradient(): pl.pallas_call(turn_kernel, out_shape=out((width, cells), BF16), in_specs...  2.03 us
  transfers between devices with their start and end apart: 15, of which 5 were waited for; matrix products, arithmetic and copies ran while one was open for 0% of the time, Pallas kernels for 22%

profile of v3, /device:TPU:0, one launch (start us, length us, event | category | flops | bytes accessed | tf_op | source)
XLA Modules:
  0.0 62.9 jit_solution(15365383334932549011)
XLA Ops:
  0.0 2.1 %collective-permute-start.5 = (bf16[64,1024]{1,0:T(8,128)(2,1)}, bf16[64,1024]{1,0:T(8,128)(2,1)S(1)}, u32[]{:S(2)}, u32[]{:S(2)}) collective-permute-start(bf16[64,1024]{1,0:T(8,128)(2,1)} %bitcast.18), channel_id=1, source_target_pairs={{0,2},{2,4},{4,6},{6,0},{1,3},{3,5},{5,7},{7,1},{8,10},{10,12},{12... | collective-permute-start | bytes 393224 | tf_op jit(solution)/shard_map/ppermute | solution.py:209
  2.1 2.2 %collective-permute-start.6 = (bf16[64,1024]{1,0:T(8,128)(2,1)}, bf16[64,1024]{1,0:T(8,128)(2,1)S(1)}, u32[]{:S(2)}, u32[]{:S(2)}) collective-permute-start(bf16[64,1024]{1,0:T(8,128)(2,1)} %bitcast.19), channel_id=1, source_target_pairs={{0,6},{2,0},{4,2},{6,4},{1,7},{3,1},{5,3},{7,5},{8,14},{10,8},{12,... | collective-permute-start | bytes 393224 | tf_op jit(solution)/shard_map/ppermute | solution.py:209
  4.3 1.8 %collective-permute-start.7 = (bf16[64,1024]{1,0:T(8,128)(2,1)}, bf16[64,1024]{1,0:T(8,128)(2,1)S(1)}, u32[]{:S(2)}, u32[]{:S(2)}) collective-permute-start(bf16[64,1024]{1,0:T(8,128)(2,1)} %bitcast.20), channel_id=1, source_target_pairs={{0,4},{2,6},{4,0},{6,2},{1,5},{3,7},{5,1},{7,3},{8,12},{10,14},{12... | collective-permute-start | bytes 393224 | tf_op jit(solution)/shard_map/ppermute | solution.py:209
  6.1 2.0 %turn.1.turned_ref = bf16[256,4096]{1,0:T(8,128)(2,1)S(1)} custom-call(bf16[4096,256]{1,0:T(8,128)(2,1)} %coef_hbm.1), custom_call_target="tpu_custom_call" | custom-call | flops 134217728 | bytes 2097152 | tf_op jit(solution)/shard_map/turn/pallas_call | solution.py:258
  8.2 4.0 %early.1 = (bf16[96,1024]{1,0:T(8,128)(2,1)S(1)}, s32[1,1024]{1,0:T(1,128)S(1)}) custom-call(bf16[256,4096]{1,0:T(8,128)(2,1)S(1)} %turn.1.turned_ref, s32[3,1,1024]{2,1,0:T(1,128)S(1)} %bitcast.11, f32[3,1,1024]{2,1,0:T(1,128)S(1)} %bitcast.14, s32[1,1024]{1,0:T(1,128)S(1)} %bitcast.17), custom_call_target="tpu_custom_call" | custom-call | flops 805306368 | bytes 2097152 | tf_op jit(solution)/shard_map/early/pallas_call | solution.py:268
  12.2 1.1 %collective-permute-start = (bf16[96,1024]{1,0:T(8,128)(2,1)S(1)}, bf16[96,1024]{1,0:T(8,128)(2,1)S(1)}, u32[]{:S(2)}, u32[]{:S(2)}) collective-permute-start(bf16[96,1024]{1,0:T(8,128)(2,1)S(1)} %get-tuple-element.11), channel_id=1, source_target_pairs={{0,2},{2,4},{4,6},{6,0},{1,3},{3,5},{5,7},{7,1},{8,10},{10,12},{12... | collective-permute-start | bytes 589832 | tf_op jit(solution)/shard_map/ppermute | solution.py:209
  13.3 3.0 %collective-permute-start.3 = (bf16[96,1024]{1,0:T(8,128)(2,1)S(1)}, bf16[96,1024]{1,0:T(8,128)(2,1)S(1)}, u32[]{:S(2)}, u32[]{:S(2)}) collective-permute-start(bf16[96,1024]{1,0:T(8,128)(2,1)S(1)} %get-tuple-element.11), channel_id=1, source_target_pairs={{0,8},{8,0},{1,9},{9,1},{2,10},{10,2},{3,11},{11,3},{4,12},{12,4},... | collective-permute-start | bytes 589832 | tf_op jit(solution)/shard_map/ppermute | solution.py:204
  16.3 2.3 %collective-permute-start.1 = (bf16[96,1024]{1,0:T(8,128)(2,1)S(1)}, bf16[96,1024]{1,0:T(8,128)(2,1)S(1)}, u32[]{:S(2)}, u32[]{:S(2)}) collective-permute-start(bf16[96,1024]{1,0:T(8,128)(2,1)S(1)} %get-tuple-element.11), channel_id=1, source_target_pairs={{0,6},{2,0},{4,2},{6,4},{1,7},{3,1},{5,3},{7,5},{8,14},{10,8},{12,... | collective-permute-start | bytes 589832 | tf_op jit(solution)/shard_map/ppermute | solution.py:209
  19.2 0.6 collective-permute-start.8
  19.8 1.1 %collective-permute-done.3 = bf16[96,1024]{1,0:T(8,128)(2,1)S(1)} collective-permute-done((bf16[96,1024]{1,0:T(8,128)(2,1)S(1)}, bf16[96,1024]{1,0:T(8,128)(2,1)S(1)}, u32[]{:S(2)}, u32[]{:S(2)}) %collective-permute-start.3) | collective-permute-done | bytes 196640 | tf_op jit(solution)/shard_map/ppermute | solution.py:204
  20.9 1.2 %collective-permute-start.11 = (bf16[96,1024]{1,0:T(8,128)(2,1)S(1)}, bf16[96,1024]{1,0:T(8,128)(2,1)S(1)}, u32[]{:S(2)}, u32[]{:S(2)}) collective-permute-start(bf16[96,1024]{1,0:T(8,128)(2,1)S(1)} %collective-permute-done.3), channel_id=1, source_target_pairs={{0,2},{2,4},{4,6},{6,0},{1,3},{3,5},{5,7},{7,1},{8,10},{10,12},{12... | collective-permute-start | bytes 589832 | tf_op jit(solution)/shard_map/ppermute | solution.py:209
  22.2 2.0 %collective-permute-start.12 = (bf16[96,1024]{1,0:T(8,128)(2,1)S(1)}, bf16[96,1024]{1,0:T(8,128)(2,1)S(1)}, u32[]{:S(2)}, u32[]{:S(2)}) collective-permute-start(bf16[96,1024]{1,0:T(8,128)(2,1)S(1)} %collective-permute-done.3), channel_id=1, source_target_pairs={{0,6},{2,0},{4,2},{6,4},{1,7},{3,1},{5,3},{7,5},{8,14},{10,8},{12,... | collective-permute-start | bytes 589832 | tf_op jit(solution)/shard_map/ppermute | solution.py:209
  24.2 3.0 %collective-permute-done.1 = bf16[96,1024]{1,0:T(8,128)(2,1)S(1)} collective-permute-done((bf16[96,1024]{1,0:T(8,128)(2,1)S(1)}, bf16[96,1024]{1,0:T(8,128)(2,1)S(1)}, u32[]{:S(2)}, u32[]{:S(2)}) %collective-permute-start.1) | collective-permute-done | bytes 196640 | tf_op jit(solution)/shard_map/ppermute | solution.py:209
  28.7 0.6 collective-permute-start.9
  29.3 0.8 %collective-permute-start.13 = (bf16[96,1024]{1,0:T(8,128)(2,1)S(1)}, bf16[96,1024]{1,0:T(8,128)(2,1)S(1)}, u32[]{:S(2)}, u32[]{:S(2)}) collective-permute-start(bf16[96,1024]{1,0:T(8,128)(2,1)S(1)} %collective-permute-done.3), channel_id=1, source_target_pairs={{0,4},{2,6},{4,0},{6,2},{1,5},{3,7},{5,1},{7,3},{8,12},{10,14},{12... | collective-permute-start | bytes 589832 | tf_op jit(solution)/shard_map/ppermute | solution.py:209
  30.1 2.6 %collective-permute-done.8.refs_1_ = bf16[256,1024]{1,0:T(8,128)(2,1)S(1)} collective-permute-done((bf16[256,1024]{1,0:T(8,128)(2,1)S(1)}, bf16[256,1024]{1,0:T(8,128)(2,1)S(1)}, u32[]{:S(2)}, u32[]{:S(2)}) %collective-permute-start.8) | collective-permute-done | bytes 524320 | tf_op jit(solution)/shard_map/ppermute | solution.py:204
  32.8 4.8 %collective-permute-done.13 = bf16[96,1024]{1,0:T(8,128)(2,1)S(1)} collective-permute-done((bf16[96,1024]{1,0:T(8,128)(2,1)S(1)}, bf16[96,1024]{1,0:T(8,128)(2,1)S(1)}, u32[]{:S(2)}, u32[]{:S(2)}) %collective-permute-start.13) | collective-permute-done | bytes 196640 | tf_op jit(solution)/shard_map/ppermute | solution.py:209
  37.9 2.5 %evaluate.2 = (bf16[256,512]{1,0:T(8,128)(2,1)S(1)}, bf16[256,512]{1,0:T(8,128)(2,1)S(1)}) custom-call(bf16[256,4096]{1,0:T(8,128)(2,1)S(1)} %turn.1.turned_ref, s32[3,1,1024]{2,1,0:T(1,128)S(1)} %bitcast.12, f32[3,1,1024]{2,1,0:T(1,128)S(1)} %bitcast.15), custom_call_target="tpu_custom_call" | custom-call | flops 2147483648 | bytes 2097152 | tf_op jit(solution)/shard_map/evaluate/pallas_call | solution.py:235
  40.5 2.5 %evaluate.3 = (bf16[256,512]{1,0:T(8,128)(2,1)S(1)}, bf16[256,512]{1,0:T(8,128)(2,1)S(1)}) custom-call(bf16[256,4096]{1,0:T(8,128)(2,1)S(1)} %turn.1.turned_ref, s32[3,1,1024]{2,1,0:T(1,128)S(1)} %bitcast.13, f32[3,1,1024]{2,1,0:T(1,128)S(1)} %bitcast.16), custom_call_target="tpu_custom_call" | custom-call | flops 2147483648 | bytes 2097152 | tf_op jit(solution)/shard_map/evaluate/pallas_call | solution.py:235
  43.0 1.7 %ratio.1.rows_ref = bf16[1536,256]{1,0:T(8,128)(2,1)S(1)} custom-call(bf16[256,1024]{1,0:T(8,128)(2,1)S(1)} %pad_maximum_fusion.refs_0_, bf16[256,1024]{1,0:T(8,128)(2,1)S(1)} %collective-permute-done.8.refs_1_, bf16[256,1024]{1,0:T(8,128)(2,1)S(1)} %collective-permute-done.9.refs_2_, bf16[256,1024]{1,0:T(8,128)(2,1)S(1)} %collective-permute-done.10.refs_3_, ...), custom_call_target="tpu_custom_call" | custom-call | flops 1610612736 | bytes 2097152 | tf_op jit(solution)/shard_map/ratio/pallas_call | solution.py:294
  44.8 0.8 %couple.1.mixed_ref = f32[256,1024]{1,0:T(8,128)S(1)} custom-call(f32[1,1]{1,0:T(1,128)} %bitcast.7.energy_ref, f32[1,1]{1,0:T(1,128)} %bitcast.8.weight_ref, bf16[480,1024]{1,0:T(8,128)(2,1)S(1)} %constant_dynamic-update-slice_fusion.near_own_ref, bf16[480,1024]{1,0:T(8,128)(2,1)S(1)} %collective-permute-done.4.near_other_ref, ...), custom_call_target="tpu_custom_call" | custom-call | flops 536870912 | bytes 2097152 | tf_op jit(solution)/shard_map/couple/pallas_call | solution.py:306
  45.6 1.3 %finish.1 = bf16[1024,256]{1,0:T(8,128)(2,1)S(1)} custom-call(f32[1,1]{1,0:T(1,128)} %bitcast.9.weight_ref, f32[256,1024]{1,0:T(8,128)S(1)} %couple.1.mixed_ref, bf16[1536,256]{1,0:T(8,128)(2,1)S(1)} %ratio.1.rows_ref, bf16[288,1024]{1,0:T(8,128)(2,1)S(1)} %constant_dynamic-update-slice_fusion.5.far_own_ref, ...), custom_call_target="tpu_custom_call" | custom-call | flops 536870912 | bytes 2097152 | tf_op jit(solution)/shard_map/finish/pallas_call | solution.py:316
  46.9 15.3 %all_to_all.5 = bf16[8,128,256]{2,1,0:T(8,128)(2,1)S(1)} all-to-all(bf16[8,128,256]{2,1,0:T(8,128)(2,1)S(1)} %bitcast.10), channel_id=1, replica_groups=mesh['y'=4,'xl'=2,'xh'=2,'z'=4,'core'=2] {'y','xl'}, dimensions={0} | all-to-all | bytes 1048576 | tf_op jit(solution)/shard_map/all_to_all | solution.py:328
  62.2 0.7 %convert_reduce_fusion = f32[128,256]{1,0:T(8,128)} fusion(bf16[8,128,256]{2,1,0:T(8,128)(2,1)S(1)} %all_to_all.5), kind=kLoop, calls=%fused_computation | loop fusion | flops 491520 | bytes 655360 | tf_op jit(solution)/shard_map/reduce_sum | solution.py:329
  (32 shorter events, 1.2 us)
Async XLA Ops:
  0.0 8.1 %copy-start = (s32[1,3,1024]{2,0,1:T(1,128)S(1)}, s32[1,3,1024]{2,0,1:T(1,128)}, u32[]{:S(2)}) copy-start(s32[1,3,1024]{2,0,1:T(1,128)} %param.9) | copy-start | bytes 36868
  0.0 8.2 %copy-start.1 = (f32[1,3,1024]{2,0,1:T(1,128)S(1)}, f32[1,3,1024]{2,0,1:T(1,128)}, u32[]{:S(2)}) copy-start(f32[1,3,1024]{2,0,1:T(1,128)} %param.10) | copy-start | bytes 36868
  0.0 8.2 %copy-start.2 = (s32[1024]{0:T(1024)S(1)}, s32[1024]{0:T(1024)}, u32[]{:S(2)}) copy-start(s32[1024]{0:T(1024)} %param.13) | copy-start | bytes 12292
  0.0 16.3 %collective-permute-start.5 = (bf16[64,1024]{1,0:T(8,128)(2,1)}, bf16[64,1024]{1,0:T(8,128)(2,1)S(1)}, u32[]{:S(2)}, u32[]{:S(2)}) collective-permute-start(bf16[64,1024]{1,0:T(8,128)(2,1)} %bitcast.18), channel_id=1, source_target_pairs={{0,2},{2,4},{4,6},{6,0},{1,3},{3,5},{5,7},{7,1},{8,10},{10,12},{12... | collective-permute-start | bytes 393224 | tf_op jit(solution)/shard_map/ppermute | solution.py:209
  2.1 16.5 %collective-permute-start.6 = (bf16[64,1024]{1,0:T(8,128)(2,1)}, bf16[64,1024]{1,0:T(8,128)(2,1)S(1)}, u32[]{:S(2)}, u32[]{:S(2)}) collective-permute-start(bf16[64,1024]{1,0:T(8,128)(2,1)} %bitcast.19), channel_id=1, source_target_pairs={{0,6},{2,0},{4,2},{6,4},{1,7},{3,1},{5,3},{7,5},{8,14},{10,8},{12,... | collective-permute-start | bytes 393224 | tf_op jit(solution)/shard_map/ppermute | solution.py:209
  4.3 14.9 %collective-permute-start.7 = (bf16[64,1024]{1,0:T(8,128)(2,1)}, bf16[64,1024]{1,0:T(8,128)(2,1)S(1)}, u32[]{:S(2)}, u32[]{:S(2)}) collective-permute-start(bf16[64,1024]{1,0:T(8,128)(2,1)} %bitcast.20), channel_id=1, source_target_pairs={{0,4},{2,6},{4,0},{6,2},{1,5},{3,7},{5,1},{7,3},{8,12},{10,14},{12... | collective-permute-start | bytes 393224 | tf_op jit(solution)/shard_map/ppermute | solution.py:209
  8.1 11.0 %copy-start.3 = (bf16[1,64,1024]{2,1,0:T(8,128)(2,1)S(1)}, bf16[1,64,1024]{2,1,0:T(8,128)(2,1)}, u32[]{:S(2)}) copy-start(bf16[1,64,1024]{2,1,0:T(8,128)(2,1)} %param.8) | copy-start | bytes 393220
  12.2 10.0 %collective-permute-start = (bf16[96,1024]{1,0:T(8,128)(2,1)S(1)}, bf16[96,1024]{1,0:T(8,128)(2,1)S(1)}, u32[]{:S(2)}, u32[]{:S(2)}) collective-permute-start(bf16[96,1024]{1,0:T(8,128)(2,1)S(1)} %get-tuple-element.11), channel_id=1, source_target_pairs={{0,2},{2,4},{4,6},{6,0},{1,3},{3,5},{5,7},{7,1},{8,10},{10,12},{12... | collective-permute-start | bytes 589832 | tf_op jit(solution)/shard_map/ppermute | solution.py:209
  13.3 7.6 %collective-permute-start.3 = (bf16[96,1024]{1,0:T(8,128)(2,1)S(1)}, bf16[96,1024]{1,0:T(8,128)(2,1)S(1)}, u32[]{:S(2)}, u32[]{:S(2)}) collective-permute-start(bf16[96,1024]{1,0:T(8,128)(2,1)S(1)} %get-tuple-element.11), channel_id=1, source_target_pairs={{0,8},{8,0},{1,9},{9,1},{2,10},{10,2},{3,11},{11,3},{4,12},{12,4},... | collective-permute-start | bytes 589832 | tf_op jit(solution)/shard_map/ppermute | solution.py:204
  16.3 10.9 %collective-permute-start.1 = (bf16[96,1024]{1,0:T(8,128)(2,1)S(1)}, bf16[96,1024]{1,0:T(8,128)(2,1)S(1)}, u32[]{:S(2)}, u32[]{:S(2)}) collective-permute-start(bf16[96,1024]{1,0:T(8,128)(2,1)S(1)} %get-tuple-element.11), channel_id=1, source_target_pairs={{0,6},{2,0},{4,2},{6,4},{1,7},{3,1},{5,3},{7,5},{8,14},{10,8},{12,... | collective-permute-start | bytes 589832 | tf_op jit(solution)/shard_map/ppermute | solution.py:209
  18.6 8.6 %collective-permute-start.2 = (bf16[96,1024]{1,0:T(8,128)(2,1)S(1)}, bf16[96,1024]{1,0:T(8,128)(2,1)S(1)}, u32[]{:S(2)}, u32[]{:S(2)}) collective-permute-start(bf16[96,1024]{1,0:T(8,128)(2,1)S(1)} %get-tuple-element.11), channel_id=1, source_target_pairs={{0,4},{2,6},{4,0},{6,2},{1,5},{3,7},{5,1},{7,3},{8,12},{10,14},{12... | collective-permute-start | bytes 589832 | tf_op jit(solution)/shard_map/ppermute | solution.py:209
  19.2 13.6 %collective-permute-start.8 = (bf16[256,1024]{1,0:T(8,128)(2,1)S(1)}, bf16[256,1024]{1,0:T(8,128)(2,1)S(1)}, u32[]{:S(2)}, u32[]{:S(2)}) collective-permute-start(bf16[256,1024]{1,0:T(8,128)(2,1)S(1)} %pad_maximum_fusion.refs_0_), channel_id=1, source_target_pairs={{0,8},{8,0},{1,9},{9,1},{2,10},{10,2},{3,11},{11,3},{4,12},{12,4},... | collective-permute-start | bytes 1572872 | tf_op jit(solution)/shard_map/ppermute | solution.py:204
  20.9 8.4 %collective-permute-start.11 = (bf16[96,1024]{1,0:T(8,128)(2,1)S(1)}, bf16[96,1024]{1,0:T(8,128)(2,1)S(1)}, u32[]{:S(2)}, u32[]{:S(2)}) collective-permute-start(bf16[96,1024]{1,0:T(8,128)(2,1)S(1)} %collective-permute-done.3), channel_id=1, source_target_pairs={{0,2},{2,4},{4,6},{6,0},{1,3},{3,5},{5,7},{7,1},{8,10},{10,12},{12... | collective-permute-start | bytes 589832 | tf_op jit(solution)/shard_map/ppermute | solution.py:209
  22.2 10.6 %collective-permute-start.12 = (bf16[96,1024]{1,0:T(8,128)(2,1)S(1)}, bf16[96,1024]{1,0:T(8,128)(2,1)S(1)}, u32[]{:S(2)}, u32[]{:S(2)}) collective-permute-start(bf16[96,1024]{1,0:T(8,128)(2,1)S(1)} %collective-permute-done.3), channel_id=1, source_target_pairs={{0,6},{2,0},{4,2},{6,4},{1,7},{3,1},{5,3},{7,5},{8,14},{10,8},{12,... | collective-permute-start | bytes 589832 | tf_op jit(solution)/shard_map/ppermute | solution.py:209
  27.3 17.5 %collective-permute-start.4 = (bf16[480,1024]{1,0:T(8,128)(2,1)S(1)}, bf16[480,1024]{1,0:T(8,128)(2,1)S(1)}, u32[]{:S(2)}, u32[]{:S(2)}) collective-permute-start(bf16[480,1024]{1,0:T(8,128)(2,1)S(1)} %constant_dynamic-update-slice_fusion.near_own_ref), channel_id=1, source_target_pairs={{0,1},{1,0},{2,3},{3,2},{4,5},{5,4},{6,7},{7,6},{8,9},{9,8},{10,11... | collective-permute-start | bytes 2949128 | tf_op jit(solution)/shard_map/ppermute | solution.py:213
  28.7 14.3 %collective-permute-start.9 = (bf16[256,1024]{1,0:T(8,128)(2,1)S(1)}, bf16[256,1024]{1,0:T(8,128)(2,1)S(1)}, u32[]{:S(2)}, u32[]{:S(2)}) collective-permute-start(bf16[256,1024]{1,0:T(8,128)(2,1)S(1)} %pad_maximum_fusion.refs_0_), channel_id=1, source_target_pairs={{0,1},{1,0},{2,3},{3,2},{4,5},{5,4},{6,7},{7,6},{8,9},{9,8},{10,11... | collective-permute-start | bytes 1572872 | tf_op jit(solution)/shard_map/ppermute | solution.py:213
  29.3 8.3 %collective-permute-start.13 = (bf16[96,1024]{1,0:T(8,128)(2,1)S(1)}, bf16[96,1024]{1,0:T(8,128)(2,1)S(1)}, u32[]{:S(2)}, u32[]{:S(2)}) collective-permute-start(bf16[96,1024]{1,0:T(8,128)(2,1)S(1)} %collective-permute-done.3), channel_id=1, source_target_pairs={{0,4},{2,6},{4,0},{6,2},{1,5},{3,7},{5,1},{7,3},{8,12},{10,14},{12... | collective-permute-start | bytes 589832 | tf_op jit(solution)/shard_map/ppermute | solution.py:209
  32.8 10.2 %collective-permute-start.10 = (bf16[256,1024]{1,0:T(8,128)(2,1)S(1)}, bf16[256,1024]{1,0:T(8,128)(2,1)S(1)}, u32[]{:S(2)}, u32[]{:S(2)}) collective-permute-start(bf16[256,1024]{1,0:T(8,128)(2,1)S(1)} %collective-permute-done.8.refs_1_), channel_id=1, source_target_pairs={{0,1},{1,0},{2,3},{3,2},{4,5},{5,4},{6,7},{7,6},{8,9},{9,8},{10,11... | collective-permute-start | bytes 1572872 | tf_op jit(solution)/shard_map/ppermute | solution.py:213
  37.7 7.9 %collective-permute-start.14 = (bf16[288,1024]{1,0:T(8,128)(2,1)S(1)}, bf16[288,1024]{1,0:T(8,128)(2,1)S(1)}, u32[]{:S(2)}, u32[]{:S(2)}) collective-permute-start(bf16[288,1024]{1,0:T(8,128)(2,1)S(1)} %constant_dynamic-update-slice_fusion.5.far_own_ref), channel_id=1, source_target_pairs={{0,1},{1,0},{2,3},{3,2},{4,5},{5,4},{6,7},{7,6},{8,9},{9,8},{10,11... | collective-permute-start | bytes 1769480 | tf_op jit(solution)/shard_map/ppermute | solution.py:213

commit v4 on v3

--- a/solution.py
+++ b/solution.py
@@ -110,12 +110,21 @@
     slot, picker = slot_tables(me, occ_ref[...], shards, turned_ref.shape[0], slots)
     slot_ref[...] = slot
     chosen = mm(picker, turned_ref[...]).astype(BF16)
-    tiles = [slice(first, first + TILE) for first in range(0, electrons, TILE)]
-    build_laplacian(weight_tables(cell_ref, frac_ref, tiles[0]), w_refs[0])
-    for t, here in enumerate(tiles):
-        if t + 1 < len(tiles):
-            build_laplacian(weight_tables(cell_ref, frac_ref, tiles[t + 1]), w_refs[(t + 1) % 2])
-        lapt_ref[:, here] = mm(chosen, w_refs[t % 2][...]).astype(BF16)
+
+    def build(t):
+        vx, cx, value, curve = weight_tables(cell_ref, frac_ref, slice(t * TILE, (t + 1) * TILE))
+        value = value.astype(BF16).reshape(GRID, GRID, TILE)
+        curve = curve.astype(BF16).reshape(GRID, GRID, TILE)
+        for g in range(GRID):
+            x_value = jnp.broadcast_to(vx[g:g + 1, :], (GRID, TILE)).astype(BF16)[None]
+            x_curve = jnp.broadcast_to(cx[g:g + 1, :], (GRID, TILE)).astype(BF16)[None]
+            w_refs[t % 2][g * PLANE:(g + 1) * PLANE, :] = (x_curve * value + x_value * curve).reshape(PLANE, TILE)
+
+    build(0)
+    for t in range(electrons // TILE):
+        if (t + 1) * TILE < electrons:
+            build(t + 1)
+        lapt_ref[:, t * TILE:(t + 1) * TILE] = mm(chosen, w_refs[t % 2][...]).astype(BF16)
 
 
 def eval_kernel(turned_ref, cell_ref, frac_ref, val_ref, lap_ref, *w_refs, first):
@@ -179,20 +188,17 @@
     return total
 
 
-def couple_kernel(energy_ref, weight_ref, near_own_ref, near_other_ref, rows_ref, val_a, val_b, lap_a, lap_b, mixed_ref):
+def finish_kernel(energy_ref, weight_ref, near_own_ref, far_own_ref, near_other_ref, far_other_ref, rows_ref,
+                  val_a, val_b, lap_a, lap_b, *refs, z_count, size):
+    inv_refs, out_ref = refs[:-1], refs[-1]
     half = rows_ref.shape[0] // 2
-    total = coupled(rows_ref, [(0, near_own_ref), (half, near_other_ref)])
+    near = near_own_ref.shape[0]
+    total = coupled(rows_ref, [
+        (0, near_own_ref), (near, far_own_ref), (half, near_other_ref), (half + near, far_other_ref)
+    ])
     val = jnp.concatenate([val_a[...], val_b[...]], axis=1).astype(F32)
     lap = jnp.concatenate([lap_a[...], lap_b[...]], axis=1).astype(F32)
-    mixed_ref[...] = energy_ref[...] * val - 0.5 * (lap - total)
-
-
-def finish_kernel(weight_ref, mixed_ref, rows_ref, far_own_ref, far_other_ref, *refs, z_count, size):
-    inv_refs, out_ref = refs[:-1], refs[-1]
-    half = rows_ref.shape[0] // 2
-    near = half - far_own_ref.shape[0]
-    total = coupled(rows_ref, [(near, far_own_ref), (half + near, far_other_ref)])
-    mixed = (weight_ref[...] * (mixed_ref[...] + 0.5 * total)).astype(BF16)
+    mixed = (weight_ref[...] * (energy_ref[...] * val - 0.5 * (lap - total))).astype(BF16)
     inverse_times(z_count, inv_refs, mixed, out_ref, size)
 
 
@@ -246,11 +252,14 @@
     cell_index, fraction = jnp.transpose(cell_index, (1, 0, 2)), jnp.transpose(fraction, (1, 0, 2))
     mine = inverse.reshape(rows, electrons)
 
-    inv_pieces = [mine]
+    inv_pieces = []
     for shift in along_z:
         inv_pieces.append(ring_pass(mine, shift))
-    inv_plane = jnp.concatenate(inv_pieces, axis=0)
-    inv_far = ring_swap(inv_plane)
+    inv_far_mine = ring_swap(mine)
+    inv_rest = jnp.concatenate(inv_pieces, axis=0)
+    inv_far_rest = ring_swap(inv_rest)
+    inv_plane = jnp.concatenate([mine, inv_rest], axis=0)
+    inv_far = jnp.concatenate([inv_far_mine, inv_far_rest], axis=0)
     inv_plane_other = core_swap(inv_plane)
     inv_far_other = core_swap(inv_far)
     inv_all = [inv_plane, inv_far, inv_plane_other, inv_far_other]
@@ -303,25 +312,15 @@
     )(*inv_all, val_a, val_b, slot)
 
     energy, weight = energies.reshape(1, 1), weights.reshape(1, 1)
-    mixed = pl.pallas_call(
-        couple_kernel,
-        out_shape=out((width, electrons), F32),
-        in_specs=[VMEM] * 9,
-        out_specs=VMEM,
-        compiler_params=params(24),
-        cost_estimate=cost(electrons * electrons * width),
-        name="couple",
-    )(energy, weight, near, near_other, ratio_rows, val_a, val_b, lap_a, lap_b)
-
     partial = pl.pallas_call(
         functools.partial(finish_kernel, z_count=z_count, size=rows),
         out_shape=out((electrons, width), BF16),
-        in_specs=[VMEM] * (5 + len(inv_all)),
+        in_specs=[VMEM] * (11 + len(inv_all)),
         out_specs=VMEM,
         compiler_params=params(24),
-        cost_estimate=cost(electrons * electrons * width),
+        cost_estimate=cost(3 * electrons * electrons * width),
         name="finish",
-    )(weight, mixed, ratio_rows, far, far_other, *inv_all)
+    )(energy, weight, near, far, near_other, far_other, ratio_rows, val_a, val_b, lap_a, lap_b, *inv_all)
 
     walkers = ("y", "xl")
     count = lax.axis_size(walkers)

time: 63.3 us -> 68 us (1.074)
  starting transfers between devices: 18.6 us -> 21.6 us
  waiting for transfers between devices: 11.7 us -> 14.7 us
  Pallas kernels: 14.9 us -> 13.8 us
    ppermute x2 -> x3, starting transfers between devices: 3.6 us -> 6.63 us  [ring_swap(): return lax.ppermute(piece, 'xh', [(0, 1), (1, 0)])]
    ppermute x2 -> x3, waiting for transfers between devices: 3.76 us -> 5.47 us  [ring_swap(): return lax.ppermute(piece, 'xh', [(0, 1), (1, 0)])]
    ppermute x9, waiting for transfers between devices: 7.95 us -> 9.19 us  [ring_pass(): lax.ppermute(piece, 'z', [(i, (i + shift) % count) for i in range(count)])]
    pallas_call x1, Pallas kernels: 4.01 us -> 3.06 us  [gradient(): pl.pallas_call(functools.partial(early_kernel, shards=shards), out_shape=...]
    pallas_call x1 -> x0, Pallas kernels: 0.76 us -> none  [gradient(): pl.pallas_call(couple_kernel, out_shape=out((width, electrons), F32), in_...]
  transfers between devices with their start and end apart: 15 -> 16, of which waited for: 5 -> 4; matrix products, arithmetic and copies ran while one was open for 0% -> 0% of each run, Pallas kernels for 22% -> 18%
where the time goes in v4:
time: 68 us; the launch traced here: 67.6 us
  starting transfers between devices  21.6 us (32%)
  blocking collectives  15 us (22%)
  waiting for transfers between devices  14.7 us (22%)
  Pallas kernels  13.8 us (20%)
  between operations  1.55 us (2%)
  other arithmetic  0.79 us (1%)
    all_to_all x1, blocking collectives, gradient(): lax.all_to_all(partial.reshape(count, electrons // count, width), walkers...  15 us
    ppermute x9, starting transfers between devices, ring_pass(): lax.ppermute(piece, 'z', [(i, (i + shift) % count) for i in range(count)])  14.5 us
    ppermute x9, waiting for transfers between devices, ring_pass(): lax.ppermute(piece, 'z', [(i, (i + shift) % count) for i in range(count)])  9.19 us
    ppermute x3, starting transfers between devices, ring_swap(): return lax.ppermute(piece, 'xh', [(0, 1), (1, 0)])  6.63 us
    ppermute x3, waiting for transfers between devices, ring_swap(): return lax.ppermute(piece, 'xh', [(0, 1), (1, 0)])  5.47 us
    pallas_call x2, Pallas kernels, evaluate(): pl.pallas_call(functools.partial(eval_kernel, first=h * part), out_shape=...  5.03 us
    pallas_call x1, Pallas kernels, gradient(): pl.pallas_call(functools.partial(early_kernel, shards=shards), out_shape=...  3.06 us
    pallas_call x1, Pallas kernels, gradient(): pl.pallas_call(turn_kernel, out_shape=out((width, cells), BF16), in_specs...  2.03 us
  transfers between devices with their start and end apart: 16, of which 4 were waited for; matrix products, arithmetic and copies ran while one was open for 0% of the time, Pallas kernels for 18%

profile of v4, /device:TPU:0, one launch (start us, length us, event | category | flops | bytes accessed | tf_op | source)
XLA Modules:
  0.0 67.6 jit_solution(7883283749698003662)
XLA Ops:
  0.0 4.2 %collective-permute-start.10 = (bf16[64,1024]{1,0:T(8,128)(2,1)}, bf16[64,1024]{1,0:T(8,128)(2,1)S(1)}, u32[]{:S(2)}, u32[]{:S(2)}) collective-permute-start(bf16[64,1024]{1,0:T(8,128)(2,1)} %bitcast.17), channel_id=1, source_target_pairs={{0,6},{2,0},{4,2},{6,4},{1,7},{3,1},{5,3},{7,5},{8,14},{10,8},{12,... | collective-permute-start | bytes 393224 | tf_op jit(solution)/shard_map/ppermute | solution.py:215
  4.2 1.3 %collective-permute-start.9 = (bf16[64,1024]{1,0:T(8,128)(2,1)}, bf16[64,1024]{1,0:T(8,128)(2,1)S(1)}, u32[]{:S(2)}, u32[]{:S(2)}) collective-permute-start(bf16[64,1024]{1,0:T(8,128)(2,1)} %bitcast.19), channel_id=1, source_target_pairs={{0,2},{2,4},{4,6},{6,0},{1,3},{3,5},{5,7},{7,1},{8,10},{10,12},{12... | collective-permute-start | bytes 393224 | tf_op jit(solution)/shard_map/ppermute | solution.py:215
  5.5 3.0 %collective-permute-start.12 = (bf16[64,1024]{1,0:T(8,128)(2,1)}, bf16[64,1024]{1,0:T(8,128)(2,1)S(1)}, u32[]{:S(2)}, u32[]{:S(2)}) collective-permute-start(bf16[64,1024]{1,0:T(8,128)(2,1)} %bitcast.20), channel_id=1, source_target_pairs={{0,8},{8,0},{1,9},{9,1},{2,10},{10,2},{3,11},{11,3},{4,12},{12,4},... | collective-permute-start | bytes 393224 | tf_op jit(solution)/shard_map/ppermute | solution.py:210
  8.5 2.0 %turn.1.turned_ref = bf16[256,4096]{1,0:T(8,128)(2,1)S(1)} custom-call(bf16[4096,256]{1,0:T(8,128)(2,1)} %coef_hbm.1), custom_call_target="tpu_custom_call" | custom-call | flops 134217728 | bytes 2097152 | tf_op jit(solution)/shard_map/turn/pallas_call | solution.py:267
  10.6 3.1 %early.1 = (bf16[96,1024]{1,0:T(8,128)(2,1)S(1)}, s32[1,1024]{1,0:T(1,128)S(1)}) custom-call(bf16[256,4096]{1,0:T(8,128)(2,1)S(1)} %turn.1.turned_ref, s32[3,1,1024]{2,1,0:T(1,128)S(1)} %bitcast.10, f32[3,1,1024]{2,1,0:T(1,128)S(1)} %bitcast.13, s32[1,1024]{1,0:T(1,128)S(1)} %bitcast.16), custom_call_target="tpu_custom_call" | custom-call | flops 805306368 | bytes 2097152 | tf_op jit(solution)/shard_map/early/pallas_call | solution.py:277
  13.7 2.3 %collective-permute-start = (bf16[96,1024]{1,0:T(8,128)(2,1)S(1)}, bf16[96,1024]{1,0:T(8,128)(2,1)S(1)}, u32[]{:S(2)}, u32[]{:S(2)}) collective-permute-start(bf16[96,1024]{1,0:T(8,128)(2,1)S(1)} %get-tuple-element.11), channel_id=1, source_target_pairs={{0,2},{2,4},{4,6},{6,0},{1,3},{3,5},{5,7},{7,1},{8,10},{10,12},{12... | collective-permute-start | bytes 589832 | tf_op jit(solution)/shard_map/ppermute | solution.py:215
  16.0 1.1 %collective-permute-start.1 = (bf16[96,1024]{1,0:T(8,128)(2,1)S(1)}, bf16[96,1024]{1,0:T(8,128)(2,1)S(1)}, u32[]{:S(2)}, u32[]{:S(2)}) collective-permute-start(bf16[96,1024]{1,0:T(8,128)(2,1)S(1)} %get-tuple-element.11), channel_id=1, source_target_pairs={{0,6},{2,0},{4,2},{6,4},{1,7},{3,1},{5,3},{7,5},{8,14},{10,8},{12,... | collective-permute-start | bytes 589832 | tf_op jit(solution)/shard_map/ppermute | solution.py:215
  17.1 1.1 %collective-permute-start.2 = (bf16[96,1024]{1,0:T(8,128)(2,1)S(1)}, bf16[96,1024]{1,0:T(8,128)(2,1)S(1)}, u32[]{:S(2)}, u32[]{:S(2)}) collective-permute-start(bf16[96,1024]{1,0:T(8,128)(2,1)S(1)} %get-tuple-element.11), channel_id=1, source_target_pairs={{0,4},{2,6},{4,0},{6,2},{1,5},{3,7},{5,1},{7,3},{8,12},{10,14},{12... | collective-permute-start | bytes 589832 | tf_op jit(solution)/shard_map/ppermute | solution.py:215
  18.1 0.5 collective-permute-start.3
  18.7 3.1 %collective-permute-start.13 = (bf16[192,1024]{1,0:T(8,128)(2,1)S(1)}, bf16[192,1024]{1,0:T(8,128)(2,1)S(1)}, u32[]{:S(2)}, u32[]{:S(2)}) collective-permute-start(bf16[192,1024]{1,0:T(8,128)(2,1)S(1)} %pad_maximum_fusion.1), channel_id=1, source_target_pairs={{0,8},{8,0},{1,9},{9,1},{2,10},{10,2},{3,11},{11,3},{4,12},{12,4},... | collective-permute-start | bytes 1179656 | tf_op jit(solution)/shard_map/ppermute | solution.py:210
  22.0 5.5 %collective-permute-done.3 = bf16[96,1024]{1,0:T(8,128)(2,1)S(1)} collective-permute-done((bf16[96,1024]{1,0:T(8,128)(2,1)S(1)}, bf16[96,1024]{1,0:T(8,128)(2,1)S(1)}, u32[]{:S(2)}, u32[]{:S(2)}) %collective-permute-start.3) | collective-permute-done | bytes 196640 | tf_op jit(solution)/shard_map/ppermute | solution.py:210
  27.4 0.5 collective-permute-start.4
  28.0 2.8 %collective-permute-start.5 = (bf16[96,1024]{1,0:T(8,128)(2,1)S(1)}, bf16[96,1024]{1,0:T(8,128)(2,1)S(1)}, u32[]{:S(2)}, u32[]{:S(2)}) collective-permute-start(bf16[96,1024]{1,0:T(8,128)(2,1)S(1)} %collective-permute-done.3), channel_id=1, source_target_pairs={{0,6},{2,0},{4,2},{6,4},{1,7},{3,1},{5,3},{7,5},{8,14},{10,8},{12,... | collective-permute-start | bytes 589832 | tf_op jit(solution)/shard_map/ppermute | solution.py:215
  30.9 3.4 %collective-permute-done.4 = bf16[96,1024]{1,0:T(8,128)(2,1)S(1)} collective-permute-done((bf16[96,1024]{1,0:T(8,128)(2,1)S(1)}, bf16[96,1024]{1,0:T(8,128)(2,1)S(1)}, u32[]{:S(2)}, u32[]{:S(2)}) %collective-permute-start.4) | collective-permute-done | bytes 196640 | tf_op jit(solution)/shard_map/ppermute | solution.py:215
  34.3 1.2 %collective-permute-start.6 = (bf16[96,1024]{1,0:T(8,128)(2,1)S(1)}, bf16[96,1024]{1,0:T(8,128)(2,1)S(1)}, u32[]{:S(2)}, u32[]{:S(2)}) collective-permute-start(bf16[96,1024]{1,0:T(8,128)(2,1)S(1)} %collective-permute-done.3), channel_id=1, source_target_pairs={{0,4},{2,6},{4,0},{6,2},{1,5},{3,7},{5,1},{7,3},{8,12},{10,14},{12... | collective-permute-start | bytes 589832 | tf_op jit(solution)/shard_map/ppermute | solution.py:215
  35.6 0.5 collective-permute-done.5
  36.2 5.2 %collective-permute-done.6 = bf16[96,1024]{1,0:T(8,128)(2,1)S(1)} collective-permute-done((bf16[96,1024]{1,0:T(8,128)(2,1)S(1)}, bf16[96,1024]{1,0:T(8,128)(2,1)S(1)}, u32[]{:S(2)}, u32[]{:S(2)}) %collective-permute-start.6) | collective-permute-done | bytes 196640 | tf_op jit(solution)/shard_map/ppermute | solution.py:215
  41.5 0.3 collective-permute-start.8
  43.1 2.5 %evaluate.2 = (bf16[256,512]{1,0:T(8,128)(2,1)S(1)}, bf16[256,512]{1,0:T(8,128)(2,1)S(1)}) custom-call(bf16[256,4096]{1,0:T(8,128)(2,1)S(1)} %turn.1.turned_ref, s32[3,1,1024]{2,1,0:T(1,128)S(1)} %bitcast.11, f32[3,1,1024]{2,1,0:T(1,128)S(1)} %bitcast.14), custom_call_target="tpu_custom_call" | custom-call | flops 2147483648 | bytes 2097152 | tf_op jit(solution)/shard_map/evaluate/pallas_call | solution.py:241
  45.6 2.5 %evaluate.3 = (bf16[256,512]{1,0:T(8,128)(2,1)S(1)}, bf16[256,512]{1,0:T(8,128)(2,1)S(1)}) custom-call(bf16[256,4096]{1,0:T(8,128)(2,1)S(1)} %turn.1.turned_ref, s32[3,1,1024]{2,1,0:T(1,128)S(1)} %bitcast.12, f32[3,1,1024]{2,1,0:T(1,128)S(1)} %bitcast.15), custom_call_target="tpu_custom_call" | custom-call | flops 2147483648 | bytes 2097152 | tf_op jit(solution)/shard_map/evaluate/pallas_call | solution.py:241
  48.1 1.7 %ratio.1.rows_ref = bf16[1536,256]{1,0:T(8,128)(2,1)S(1)} custom-call(bf16[256,1024]{1,0:T(8,128)(2,1)S(1)} %pad_maximum_fusion.refs_0_, bf16[256,1024]{1,0:T(8,128)(2,1)S(1)} %constant_dynamic-update-slice_fusion.8.refs_1_, bf16[256,1024]{1,0:T(8,128)(2,1)S(1)} %collective-permute-done.14.refs_2_, bf16[256,1024]{1,0:T(8,128)(2,1)S(1)} %collective-permute-done.15.refs_3_, ...), custom_call_target="tpu_custom_call" | custom-call | flops 1610612736 | bytes 2097152 | tf_op jit(solution)/shard_map/ratio/pallas_call | solution.py:303
  49.9 1.9 %finish.1 = bf16[1024,256]{1,0:T(8,128)(2,1)S(1)} custom-call(f32[1,1]{1,0:T(1,128)} %bitcast.7.energy_ref, f32[1,1]{1,0:T(1,128)} %bitcast.8.weight_ref, bf16[480,1024]{1,0:T(8,128)(2,1)S(1)} %constant_dynamic-update-slice_fusion.near_own_ref, bf16[288,1024]{1,0:T(8,128)(2,1)S(1)} %constant_dynamic-update-slice_fusion.5.far_own_ref, ...), custom_call_target="tpu_custom_call" | custom-call | flops 1610612736 | bytes 2097152 | tf_op jit(solution)/shard_map/finish/pallas_call | solution.py:315
  51.9 15.0 %all_to_all.5 = bf16[8,128,256]{2,1,0:T(8,128)(2,1)S(1)} all-to-all(bf16[8,128,256]{2,1,0:T(8,128)(2,1)S(1)} %bitcast.9), channel_id=1, replica_groups=mesh['y'=4,'xl'=2,'xh'=2,'z'=4,'core'=2] {'y','xl'}, dimensions={0} | all-to-all | bytes 1048576 | tf_op jit(solution)/shard_map/all_to_all | solution.py:327
  66.9 0.7 %convert_reduce_fusion = f32[128,256]{1,0:T(8,128)} fusion(bf16[8,128,256]{2,1,0:T(8,128)(2,1)S(1)} %all_to_all.5), kind=kLoop, calls=%fused_computation | loop fusion | flops 491520 | bytes 655360 | tf_op jit(solution)/shard_map/reduce_sum | solution.py:328
  (36 shorter events, 0.5 us)
Async XLA Ops:
  0.0 10.6 %copy-start = (s32[1,3,1024]{2,0,1:T(1,128)S(1)}, s32[1,3,1024]{2,0,1:T(1,128)}, u32[]{:S(2)}) copy-start(s32[1,3,1024]{2,0,1:T(1,128)} %param.9) | copy-start | bytes 36868
  0.0 10.6 %copy-start.1 = (f32[1,3,1024]{2,0,1:T(1,128)S(1)}, f32[1,3,1024]{2,0,1:T(1,128)}, u32[]{:S(2)}) copy-start(f32[1,3,1024]{2,0,1:T(1,128)} %param.10) | copy-start | bytes 36868
  0.0 10.6 %copy-start.2 = (s32[1024]{0:T(1024)S(1)}, s32[1024]{0:T(1024)}, u32[]{:S(2)}) copy-start(s32[1024]{0:T(1024)} %param.13) | copy-start | bytes 12292
  0.0 16.0 %collective-permute-start.10 = (bf16[64,1024]{1,0:T(8,128)(2,1)}, bf16[64,1024]{1,0:T(8,128)(2,1)S(1)}, u32[]{:S(2)}, u32[]{:S(2)}) collective-permute-start(bf16[64,1024]{1,0:T(8,128)(2,1)} %bitcast.17), channel_id=1, source_target_pairs={{0,6},{2,0},{4,2},{6,4},{1,7},{3,1},{5,3},{7,5},{8,14},{10,8},{12,... | collective-permute-start | bytes 393224 | tf_op jit(solution)/shard_map/ppermute | solution.py:215
  4.2 12.8 %collective-permute-start.11 = (bf16[64,1024]{1,0:T(8,128)(2,1)}, bf16[64,1024]{1,0:T(8,128)(2,1)S(1)}, u32[]{:S(2)}, u32[]{:S(2)}) collective-permute-start(bf16[64,1024]{1,0:T(8,128)(2,1)} %bitcast.18), channel_id=1, source_target_pairs={{0,4},{2,6},{4,0},{6,2},{1,5},{3,7},{5,1},{7,3},{8,12},{10,14},{12... | collective-permute-start | bytes 393224 | tf_op jit(solution)/shard_map/ppermute | solution.py:215
  4.2 13.9 %collective-permute-start.9 = (bf16[64,1024]{1,0:T(8,128)(2,1)}, bf16[64,1024]{1,0:T(8,128)(2,1)S(1)}, u32[]{:S(2)}, u32[]{:S(2)}) collective-permute-start(bf16[64,1024]{1,0:T(8,128)(2,1)} %bitcast.19), channel_id=1, source_target_pairs={{0,2},{2,4},{4,6},{6,0},{1,3},{3,5},{5,7},{7,1},{8,10},{10,12},{12... | collective-permute-start | bytes 393224 | tf_op jit(solution)/shard_map/ppermute | solution.py:215
  5.5 13.2 %collective-permute-start.12 = (bf16[64,1024]{1,0:T(8,128)(2,1)}, bf16[64,1024]{1,0:T(8,128)(2,1)S(1)}, u32[]{:S(2)}, u32[]{:S(2)}) collective-permute-start(bf16[64,1024]{1,0:T(8,128)(2,1)} %bitcast.20), channel_id=1, source_target_pairs={{0,8},{8,0},{1,9},{9,1},{2,10},{10,2},{3,11},{11,3},{4,12},{12,4},... | collective-permute-start | bytes 393224 | tf_op jit(solution)/shard_map/ppermute | solution.py:210
  10.6 8.1 %copy-start.3 = (bf16[1,64,1024]{2,1,0:T(8,128)(2,1)S(1)}, bf16[1,64,1024]{2,1,0:T(8,128)(2,1)}, u32[]{:S(2)}) copy-start(bf16[1,64,1024]{2,1,0:T(8,128)(2,1)} %param.8) | copy-start | bytes 393220
  13.7 8.2 %collective-permute-start = (bf16[96,1024]{1,0:T(8,128)(2,1)S(1)}, bf16[96,1024]{1,0:T(8,128)(2,1)S(1)}, u32[]{:S(2)}, u32[]{:S(2)}) collective-permute-start(bf16[96,1024]{1,0:T(8,128)(2,1)S(1)} %get-tuple-element.11), channel_id=1, source_target_pairs={{0,2},{2,4},{4,6},{6,0},{1,3},{3,5},{5,7},{7,1},{8,10},{10,12},{12... | collective-permute-start | bytes 589832 | tf_op jit(solution)/shard_map/ppermute | solution.py:215
  16.0 12.0 %collective-permute-start.1 = (bf16[96,1024]{1,0:T(8,128)(2,1)S(1)}, bf16[96,1024]{1,0:T(8,128)(2,1)S(1)}, u32[]{:S(2)}, u32[]{:S(2)}) collective-permute-start(bf16[96,1024]{1,0:T(8,128)(2,1)S(1)} %get-tuple-element.11), channel_id=1, source_target_pairs={{0,6},{2,0},{4,2},{6,4},{1,7},{3,1},{5,3},{7,5},{8,14},{10,8},{12,... | collective-permute-start | bytes 589832 | tf_op jit(solution)/shard_map/ppermute | solution.py:215
  17.1 13.7 %collective-permute-start.2 = (bf16[96,1024]{1,0:T(8,128)(2,1)S(1)}, bf16[96,1024]{1,0:T(8,128)(2,1)S(1)}, u32[]{:S(2)}, u32[]{:S(2)}) collective-permute-start(bf16[96,1024]{1,0:T(8,128)(2,1)S(1)} %get-tuple-element.11), channel_id=1, source_target_pairs={{0,4},{2,6},{4,0},{6,2},{1,5},{3,7},{5,1},{7,3},{8,12},{10,14},{12... | collective-permute-start | bytes 589832 | tf_op jit(solution)/shard_map/ppermute | solution.py:215
  18.1 9.3 %collective-permute-start.3 = (bf16[96,1024]{1,0:T(8,128)(2,1)S(1)}, bf16[96,1024]{1,0:T(8,128)(2,1)S(1)}, u32[]{:S(2)}, u32[]{:S(2)}) collective-permute-start(bf16[96,1024]{1,0:T(8,128)(2,1)S(1)} %get-tuple-element.11), channel_id=1, source_target_pairs={{0,8},{8,0},{1,9},{9,1},{2,10},{10,2},{3,11},{11,3},{4,12},{12,4},... | collective-permute-start | bytes 589832 | tf_op jit(solution)/shard_map/ppermute | solution.py:210
  18.7 17.4 %collective-permute-start.13 = (bf16[192,1024]{1,0:T(8,128)(2,1)S(1)}, bf16[192,1024]{1,0:T(8,128)(2,1)S(1)}, u32[]{:S(2)}, u32[]{:S(2)}) collective-permute-start(bf16[192,1024]{1,0:T(8,128)(2,1)S(1)} %pad_maximum_fusion.1), channel_id=1, source_target_pairs={{0,8},{8,0},{1,9},{9,1},{2,10},{10,2},{3,11},{11,3},{4,12},{12,4},... | collective-permute-start | bytes 1179656 | tf_op jit(solution)/shard_map/ppermute | solution.py:210
  21.9 26.2 %collective-permute-start.14 = (bf16[256,1024]{1,0:T(8,128)(2,1)S(1)}, bf16[256,1024]{1,0:T(8,128)(2,1)S(1)}, u32[]{:S(2)}, u32[]{:S(2)}) collective-permute-start(bf16[256,1024]{1,0:T(8,128)(2,1)S(1)} %pad_maximum_fusion.refs_0_), channel_id=1, source_target_pairs={{0,1},{1,0},{2,3},{3,2},{4,5},{5,4},{6,7},{7,6},{8,9},{9,8},{10,11... | collective-permute-start | bytes 1572872 | tf_op jit(solution)/shard_map/ppermute | solution.py:219
  27.4 6.9 %collective-permute-start.4 = (bf16[96,1024]{1,0:T(8,128)(2,1)S(1)}, bf16[96,1024]{1,0:T(8,128)(2,1)S(1)}, u32[]{:S(2)}, u32[]{:S(2)}) collective-permute-start(bf16[96,1024]{1,0:T(8,128)(2,1)S(1)} %collective-permute-done.3), channel_id=1, source_target_pairs={{0,2},{2,4},{4,6},{6,0},{1,3},{3,5},{5,7},{7,1},{8,10},{10,12},{12... | collective-permute-start | bytes 589832 | tf_op jit(solution)/shard_map/ppermute | solution.py:215
  28.0 8.1 %collective-permute-start.5 = (bf16[96,1024]{1,0:T(8,128)(2,1)S(1)}, bf16[96,1024]{1,0:T(8,128)(2,1)S(1)}, u32[]{:S(2)}, u32[]{:S(2)}) collective-permute-start(bf16[96,1024]{1,0:T(8,128)(2,1)S(1)} %collective-permute-done.3), channel_id=1, source_target_pairs={{0,6},{2,0},{4,2},{6,4},{1,7},{3,1},{5,3},{7,5},{8,14},{10,8},{12,... | collective-permute-start | bytes 589832 | tf_op jit(solution)/shard_map/ppermute | solution.py:215
  30.8 19.1 %collective-permute-start.7 = (bf16[480,1024]{1,0:T(8,128)(2,1)S(1)}, bf16[480,1024]{1,0:T(8,128)(2,1)S(1)}, u32[]{:S(2)}, u32[]{:S(2)}) collective-permute-start(bf16[480,1024]{1,0:T(8,128)(2,1)S(1)} %constant_dynamic-update-slice_fusion.near_own_ref), channel_id=1, source_target_pairs={{0,1},{1,0},{2,3},{3,2},{4,5},{5,4},{6,7},{7,6},{8,9},{9,8},{10,11... | collective-permute-start | bytes 2949128 | tf_op jit(solution)/shard_map/ppermute | solution.py:219
  34.3 7.2 %collective-permute-start.6 = (bf16[96,1024]{1,0:T(8,128)(2,1)S(1)}, bf16[96,1024]{1,0:T(8,128)(2,1)S(1)}, u32[]{:S(2)}, u32[]{:S(2)}) collective-permute-start(bf16[96,1024]{1,0:T(8,128)(2,1)S(1)} %collective-permute-done.3), channel_id=1, source_target_pairs={{0,4},{2,6},{4,0},{6,2},{1,5},{3,7},{5,1},{7,3},{8,12},{10,14},{12... | collective-permute-start | bytes 589832 | tf_op jit(solution)/shard_map/ppermute | solution.py:215
  36.2 12.0 %collective-permute-start.15 = (bf16[256,1024]{1,0:T(8,128)(2,1)S(1)}, bf16[256,1024]{1,0:T(8,128)(2,1)S(1)}, u32[]{:S(2)}, u32[]{:S(2)}) collective-permute-start(bf16[256,1024]{1,0:T(8,128)(2,1)S(1)} %constant_dynamic-update-slice_fusion.8.refs_1_), channel_id=1, source_target_pairs={{0,1},{1,0},{2,3},{3,2},{4,5},{5,4},{6,7},{7,6},{8,9},{9,8},{10,11... | collective-permute-start | bytes 1572872 | tf_op jit(solution)/shard_map/ppermute | solution.py:219
  41.5 8.4 %collective-permute-start.8 = (bf16[288,1024]{1,0:T(8,128)(2,1)S(1)}, bf16[288,1024]{1,0:T(8,128)(2,1)S(1)}, u32[]{:S(2)}, u32[]{:S(2)}) collective-permute-start(bf16[288,1024]{1,0:T(8,128)(2,1)S(1)} %constant_dynamic-update-slice_fusion.5.far_own_ref), channel_id=1, source_target_pairs={{0,1},{1,0},{2,3},{3,2},{4,5},{5,4},{6,7},{7,6},{8,9},{9,8},{10,11... | collective-permute-start | bytes 1769480 | tf_op jit(solution)/shard_map/ppermute | solution.py:219

commit v5 on v4

--- a/solution.py
+++ b/solution.py
@@ -105,8 +105,8 @@
 
 def early_kernel(turned_ref, cell_ref, frac_ref, occ_ref, lapt_ref, slot_ref, *w_refs, shards):
     slots, electrons = lapt_ref.shape
-    plane, along, core = place(shards // 4)
-    me = (plane * (shards // 4) + along[0]) * 2 + core
+    plane, z, core = place()
+    me = (plane * (shards // 4) + z) * 2 + core
     slot, picker = slot_tables(me, occ_ref[...], shards, turned_ref.shape[0], slots)
     slot_ref[...] = slot
     chosen = mm(picker, turned_ref[...]).astype(BF16)
@@ -144,18 +144,27 @@
         lap_ref[:, here] = mm(turned_ref[...], w_refs[2 * (t % 2) + 1][...]).astype(BF16)
 
 
-def place(z_count):
-    core, z, plane = lax.axis_index("core"), lax.axis_index("z"), lax.axis_index("xh")
-    return plane, [lax.rem(z + dz, z_count) for dz in (0, z_count - 1, 1, 2)], core
-
-
-def owners(z_count):
-    plane, along, core = place(z_count)
+def place():
+    return lax.axis_index("xh"), lax.axis_index("z"), lax.axis_index("core")
+
+
+def owners(z_count, along):
+    plane, _, core = place()
     return [(p * z_count + z) * 2 + c for c in (core, 1 - core) for p in (plane, 1 - plane) for z in along]
 
 
+def inverse_owners(z_count):
+    z = place()[1]
+    return owners(z_count, [z ^ k for k in (0, 1, 3, 2)])
+
+
+def slot_owners(z_count):
+    z = place()[1]
+    return owners(z_count, [lax.rem(z + k, z_count) for k in (0, z_count - 1, 1, 2)])
+
+
 def inverse_times(z_count, inv_refs, right, out_ref, size):
-    blocks = owners(z_count)
+    blocks = inverse_owners(z_count)
     first = 0
     for ref in inv_refs:
         value = mm_nt(ref[...], right).astype(out_ref.dtype)
@@ -173,7 +182,7 @@
     inverse_times(z_count, inv_refs, val, ratio_ref, size)
     ratio = ratio_ref[...]
     slot = slot_ref[...]
-    blocks = owners(z_count)
+    blocks = slot_owners(z_count)
     for j in range(0, len(blocks), 2):
         ids = lax.broadcasted_iota(jnp.int32, (slots, slot.shape[1]), 0)
         pick = jnp.concatenate([(ids + block * slots == slot).astype(F32) for block in blocks[j:j + 2]], axis=0)
@@ -215,6 +224,10 @@
     return lax.ppermute(piece, "z", [(i, (i + shift) % count) for i in range(count)])
 
 
+def ring_trade(piece, bits):
+    return lax.ppermute(piece, "z", [(i, i ^ bits) for i in range(lax.axis_size("z"))])
+
+
 def core_swap(piece):
     return lax.ppermute(piece, "core", [(0, 1), (1, 0)])
 
@@ -252,14 +265,9 @@
     cell_index, fraction = jnp.transpose(cell_index, (1, 0, 2)), jnp.transpose(fraction, (1, 0, 2))
     mine = inverse.reshape(rows, electrons)
 
-    inv_pieces = []
-    for shift in along_z:
-        inv_pieces.append(ring_pass(mine, shift))
-    inv_far_mine = ring_swap(mine)
-    inv_rest = jnp.concatenate(inv_pieces, axis=0)
-    inv_far_rest = ring_swap(inv_rest)
-    inv_plane = jnp.concatenate([mine, inv_rest], axis=0)
-    inv_far = jnp.concatenate([inv_far_mine, inv_far_rest], axis=0)
+    inv_pair = jnp.concatenate([mine, ring_trade(mine, 1)], axis=0)
+    inv_plane = jnp.concatenate([inv_pair, ring_trade(inv_pair, 3)], axis=0)
+    inv_far = ring_swap(inv_plane)
     inv_plane_other = core_swap(inv_plane)
     inv_far_other = core_swap(inv_far)
     inv_all = [inv_plane, inv_far, inv_plane_other, inv_far_other]

time: 68 us -> 66.2 us (0.974)
  waiting for transfers between devices: 14.7 us -> 13.1 us
    ppermute x9 -> x6, waiting for transfers between devices: 9.19 us -> 0.02 us  [ring_pass(): lax.ppermute(piece, 'z', [(i, (i + shift) % count) for i in range(count)])]
    ppermute x0 -> x2, waiting for transfers between devices: none -> 6.17 us  [ring_trade(): lax.ppermute(piece, 'z', [(i, i ^ bits) for i in range(lax.axis_size('z'))])]
    ppermute x9 -> x6, starting transfers between devices: 14.5 us -> 8.62 us  [ring_pass(): lax.ppermute(piece, 'z', [(i, (i + shift) % count) for i in range(count)])]
    ppermute x0 -> x2, starting transfers between devices: none -> 5.32 us  [ring_trade(): lax.ppermute(piece, 'z', [(i, i ^ bits) for i in range(lax.axis_size('z'))])]
    ppermute x3 -> x2, waiting for transfers between devices: 5.47 us -> 6.93 us  [ring_swap(): return lax.ppermute(piece, 'xh', [(0, 1), (1, 0)])]
    ppermute x3 -> x2, starting transfers between devices: 6.63 us -> 6.37 us  [ring_swap(): return lax.ppermute(piece, 'xh', [(0, 1), (1, 0)])]
  transfers between devices with their start and end apart: 16 -> 14, of which waited for: 4 -> 2; matrix products, arithmetic and copies ran while one was open for 0% -> 0% of each run, Pallas kernels for 18% -> 18%
where the time goes in v5:
time: 66.2 us; the launch traced here: 66 us
  starting transfers between devices  21.3 us (32%)
  blocking collectives  15.4 us (23%)
  Pallas kernels  13.8 us (21%)
  waiting for transfers between devices  13.1 us (20%)
  between operations  1.5 us (2%)
  other arithmetic  0.78 us (1%)
    all_to_all x1, blocking collectives, gradient(): lax.all_to_all(partial.reshape(count, electrons // count, width), walkers...  15.4 us
    ppermute x6, starting transfers between devices, ring_pass(): lax.ppermute(piece, 'z', [(i, (i + shift) % count) for i in range(count)])  8.62 us
    ppermute x2, waiting for transfers between devices, ring_swap(): return lax.ppermute(piece, 'xh', [(0, 1), (1, 0)])  6.93 us
    ppermute x2, starting transfers between devices, ring_swap(): return lax.ppermute(piece, 'xh', [(0, 1), (1, 0)])  6.37 us
    ppermute x2, waiting for transfers between devices, ring_trade(): lax.ppermute(piece, 'z', [(i, i ^ bits) for i in range(lax.axis_size('z'))])  6.17 us
    ppermute x2, starting transfers between devices, ring_trade(): lax.ppermute(piece, 'z', [(i, i ^ bits) for i in range(lax.axis_size('z'))])  5.32 us
    pallas_call x2, Pallas kernels, evaluate(): pl.pallas_call(functools.partial(eval_kernel, first=h * part), out_shape=...  5.03 us
    pallas_call x1, Pallas kernels, gradient(): pl.pallas_call(functools.partial(early_kernel, shards=shards), out_shape=...  3.06 us
  transfers between devices with their start and end apart: 14, of which 2 were waited for; matrix products, arithmetic and copies ran while one was open for 0% of the time, Pallas kernels for 18%

profile of v5, /device:TPU:0, one launch (start us, length us, event | category | flops | bytes accessed | tf_op | source)
XLA Modules:
  0.0 66.0 jit_solution(2567665428217938199)
XLA Ops:
  0.0 2.1 %collective-permute-start.9 = (bf16[64,1024]{1,0:T(8,128)(2,1)}, bf16[64,1024]{1,0:T(8,128)(2,1)S(1)}, u32[]{:S(2)}, u32[]{:S(2)}) collective-permute-start(bf16[64,1024]{1,0:T(8,128)(2,1)} %bitcast.17), channel_id=1, source_target_pairs={{0,2},{2,0},{4,6},{6,4},{1,3},{3,1},{5,7},{7,5},{8,10},{10,8},{12,... | collective-permute-start | bytes 393224 | tf_op jit(solution)/shard_map/ppermute | solution.py:228
  2.1 2.0 %turn.1.turned_ref = bf16[256,4096]{1,0:T(8,128)(2,1)S(1)} custom-call(bf16[4096,256]{1,0:T(8,128)(2,1)} %coef_hbm.1), custom_call_target="tpu_custom_call" | custom-call | flops 134217728 | bytes 2097152 | tf_op jit(solution)/shard_map/turn/pallas_call | solution.py:275
  4.2 0.0 copy-start.3
  4.2 3.1 %early.1 = (bf16[96,1024]{1,0:T(8,128)(2,1)S(1)}, s32[1,1024]{1,0:T(1,128)S(1)}) custom-call(bf16[256,4096]{1,0:T(8,128)(2,1)S(1)} %turn.1.turned_ref, s32[3,1,1024]{2,1,0:T(1,128)S(1)} %bitcast.10, f32[3,1,1024]{2,1,0:T(1,128)S(1)} %bitcast.13, s32[1,1024]{1,0:T(1,128)S(1)} %bitcast.16), custom_call_target="tpu_custom_call" | custom-call | flops 805306368 | bytes 2097152 | tf_op jit(solution)/shard_map/early/pallas_call | solution.py:285
  7.3 0.1 collective-permute-start
  7.4 3.1 %collective-permute-start.3 = (bf16[96,1024]{1,0:T(8,128)(2,1)S(1)}, bf16[96,1024]{1,0:T(8,128)(2,1)S(1)}, u32[]{:S(2)}, u32[]{:S(2)}) collective-permute-start(bf16[96,1024]{1,0:T(8,128)(2,1)S(1)} %get-tuple-element.11), channel_id=1, source_target_pairs={{0,8},{8,0},{1,9},{9,1},{2,10},{10,2},{3,11},{11,3},{4,12},{12,4},... | collective-permute-start | bytes 589832 | tf_op jit(solution)/shard_map/ppermute | solution.py:219
  10.5 3.2 %collective-permute-start.10 = (bf16[128,1024]{1,0:T(8,128)(2,1)S(1)}, bf16[128,1024]{1,0:T(8,128)(2,1)S(1)}, u32[]{:S(2)}, u32[]{:S(2)}) collective-permute-start(bf16[128,1024]{1,0:T(8,128)(2,1)S(1)} %pad_maximum_fusion.1), channel_id=1, source_target_pairs={{0,6},{2,4},{4,2},{6,0},{1,7},{3,5},{5,3},{7,1},{8,14},{10,12},{12... | collective-permute-start | bytes 786440 | tf_op jit(solution)/shard_map/ppermute | solution.py:228
  13.7 0.1 collective-permute-start.1
  13.8 2.7 %collective-permute-start.2 = (bf16[96,1024]{1,0:T(8,128)(2,1)S(1)}, bf16[96,1024]{1,0:T(8,128)(2,1)S(1)}, u32[]{:S(2)}, u32[]{:S(2)}) collective-permute-start(bf16[96,1024]{1,0:T(8,128)(2,1)S(1)} %get-tuple-element.11), channel_id=1, source_target_pairs={{0,4},{2,6},{4,0},{6,2},{1,5},{3,7},{5,1},{7,3},{8,12},{10,14},{12... | collective-permute-start | bytes 589832 | tf_op jit(solution)/shard_map/ppermute | solution.py:224
  16.5 2.0 %collective-permute-start.4 = (bf16[96,1024]{1,0:T(8,128)(2,1)S(1)}, bf16[96,1024]{1,0:T(8,128)(2,1)S(1)}, u32[]{:S(2)}, u32[]{:S(2)}) collective-permute-start(bf16[96,1024]{1,0:T(8,128)(2,1)S(1)} %collective-permute-done.3), channel_id=1, source_target_pairs={{0,2},{2,4},{4,6},{6,0},{1,3},{3,5},{5,7},{7,1},{8,10},{10,12},{12... | collective-permute-start | bytes 589832 | tf_op jit(solution)/shard_map/ppermute | solution.py:224
  18.5 1.4 %collective-permute-start.5 = (bf16[96,1024]{1,0:T(8,128)(2,1)S(1)}, bf16[96,1024]{1,0:T(8,128)(2,1)S(1)}, u32[]{:S(2)}, u32[]{:S(2)}) collective-permute-start(bf16[96,1024]{1,0:T(8,128)(2,1)S(1)} %collective-permute-done.3), channel_id=1, source_target_pairs={{0,6},{2,0},{4,2},{6,4},{1,7},{3,1},{5,3},{7,5},{8,14},{10,8},{12,... | collective-permute-start | bytes 589832 | tf_op jit(solution)/shard_map/ppermute | solution.py:224
  19.8 6.2 %collective-permute-done.10 = bf16[128,1024]{1,0:T(8,128)(2,1)S(1)} collective-permute-done((bf16[128,1024]{1,0:T(8,128)(2,1)S(1)}, bf16[128,1024]{1,0:T(8,128)(2,1)S(1)}, u32[]{:S(2)}, u32[]{:S(2)}) %collective-permute-start.10) | collective-permute-done | bytes 262176 | tf_op jit(solution)/shard_map/ppermute | solution.py:228
  26.0 3.3 %collective-permute-start.11 = (bf16[256,1024]{1,0:T(8,128)(2,1)S(1)}, bf16[256,1024]{1,0:T(8,128)(2,1)S(1)}, u32[]{:S(2)}, u32[]{:S(2)}) collective-permute-start(bf16[256,1024]{1,0:T(8,128)(2,1)S(1)} %pad_maximum_fusion.refs_0_), channel_id=1, source_target_pairs={{0,8},{8,0},{1,9},{9,1},{2,10},{10,2},{3,11},{11,3},{4,12},{12,4},... | collective-permute-start | bytes 1572872 | tf_op jit(solution)/shard_map/ppermute | solution.py:219
  29.4 0.1 collective-permute-start.7
  29.5 2.5 %collective-permute-start.6 = (bf16[96,1024]{1,0:T(8,128)(2,1)S(1)}, bf16[96,1024]{1,0:T(8,128)(2,1)S(1)}, u32[]{:S(2)}, u32[]{:S(2)}) collective-permute-start(bf16[96,1024]{1,0:T(8,128)(2,1)S(1)} %collective-permute-done.3), channel_id=1, source_target_pairs={{0,4},{2,6},{4,0},{6,2},{1,5},{3,7},{5,1},{7,3},{8,12},{10,14},{12... | collective-permute-start | bytes 589832 | tf_op jit(solution)/shard_map/ppermute | solution.py:224
  31.9 0.1 collective-permute-start.12
  32.1 6.9 %collective-permute-done.11.refs_1_ = bf16[256,1024]{1,0:T(8,128)(2,1)S(1)} collective-permute-done((bf16[256,1024]{1,0:T(8,128)(2,1)S(1)}, bf16[256,1024]{1,0:T(8,128)(2,1)S(1)}, u32[]{:S(2)}, u32[]{:S(2)}) %collective-permute-start.11) | collective-permute-done | bytes 524320 | tf_op jit(solution)/shard_map/ppermute | solution.py:219
  39.1 0.8 %collective-permute-start.8 = (bf16[288,1024]{1,0:T(8,128)(2,1)S(1)}, bf16[288,1024]{1,0:T(8,128)(2,1)S(1)}, u32[]{:S(2)}, u32[]{:S(2)}) collective-permute-start(bf16[288,1024]{1,0:T(8,128)(2,1)S(1)} %constant_dynamic-update-slice_fusion.5.far_own_ref), channel_id=1, source_target_pairs={{0,1},{1,0},{2,3},{3,2},{4,5},{5,4},{6,7},{7,6},{8,9},{9,8},{10,11... | collective-permute-start | bytes 1769480 | tf_op jit(solution)/shard_map/ppermute | solution.py:232
  41.1 2.5 %evaluate.2 = (bf16[256,512]{1,0:T(8,128)(2,1)S(1)}, bf16[256,512]{1,0:T(8,128)(2,1)S(1)}) custom-call(bf16[256,4096]{1,0:T(8,128)(2,1)S(1)} %turn.1.turned_ref, s32[3,1,1024]{2,1,0:T(1,128)S(1)} %bitcast.11, f32[3,1,1024]{2,1,0:T(1,128)S(1)} %bitcast.14), custom_call_target="tpu_custom_call" | custom-call | flops 2147483648 | bytes 2097152 | tf_op jit(solution)/shard_map/evaluate/pallas_call | solution.py:254
  43.7 2.5 %evaluate.3 = (bf16[256,512]{1,0:T(8,128)(2,1)S(1)}, bf16[256,512]{1,0:T(8,128)(2,1)S(1)}) custom-call(bf16[256,4096]{1,0:T(8,128)(2,1)S(1)} %turn.1.turned_ref, s32[3,1,1024]{2,1,0:T(1,128)S(1)} %bitcast.12, f32[3,1,1024]{2,1,0:T(1,128)S(1)} %bitcast.15), custom_call_target="tpu_custom_call" | custom-call | flops 2147483648 | bytes 2097152 | tf_op jit(solution)/shard_map/evaluate/pallas_call | solution.py:254
  46.2 1.7 %ratio.1.rows_ref = bf16[1536,256]{1,0:T(8,128)(2,1)S(1)} custom-call(bf16[256,1024]{1,0:T(8,128)(2,1)S(1)} %pad_maximum_fusion.refs_0_, bf16[256,1024]{1,0:T(8,128)(2,1)S(1)} %collective-permute-done.11.refs_1_, bf16[256,1024]{1,0:T(8,128)(2,1)S(1)} %collective-permute-done.12.refs_2_, bf16[256,1024]{1,0:T(8,128)(2,1)S(1)} %collective-permute-done.13.refs_3_, ...), custom_call_target="tpu_custom_call" | custom-call | flops 1610612736 | bytes 2097152 | tf_op jit(solution)/shard_map/ratio/pallas_call | solution.py:311
  48.0 1.9 %finish.1 = bf16[1024,256]{1,0:T(8,128)(2,1)S(1)} custom-call(f32[1,1]{1,0:T(1,128)} %bitcast.7.energy_ref, f32[1,1]{1,0:T(1,128)} %bitcast.8.weight_ref, bf16[480,1024]{1,0:T(8,128)(2,1)S(1)} %constant_dynamic-update-slice_fusion.near_own_ref, bf16[288,1024]{1,0:T(8,128)(2,1)S(1)} %constant_dynamic-update-slice_fusion.5.far_own_ref, ...), custom_call_target="tpu_custom_call" | custom-call | flops 1610612736 | bytes 2097152 | tf_op jit(solution)/shard_map/finish/pallas_call | solution.py:323
  49.9 15.4 %all_to_all.5 = bf16[8,128,256]{2,1,0:T(8,128)(2,1)S(1)} all-to-all(bf16[8,128,256]{2,1,0:T(8,128)(2,1)S(1)} %bitcast.9), channel_id=1, replica_groups=mesh['y'=4,'xl'=2,'xh'=2,'z'=4,'core'=2] {'y','xl'}, dimensions={0} | all-to-all | bytes 1048576 | tf_op jit(solution)/shard_map/all_to_all | solution.py:335
  65.3 0.7 %convert_reduce_fusion = f32[128,256]{1,0:T(8,128)} fusion(bf16[8,128,256]{2,1,0:T(8,128)(2,1)S(1)} %all_to_all.5), kind=kLoop, calls=%fused_computation | loop fusion | flops 491520 | bytes 655360 | tf_op jit(solution)/shard_map/reduce_sum | solution.py:336
  (30 shorter events, 0.2 us)
Async XLA Ops:
  0.0 4.2 %copy-start = (s32[1,3,1024]{2,0,1:T(1,128)S(1)}, s32[1,3,1024]{2,0,1:T(1,128)}, u32[]{:S(2)}) copy-start(s32[1,3,1024]{2,0,1:T(1,128)} %param.9) | copy-start | bytes 36868
  0.0 4.2 %copy-start.1 = (f32[1,3,1024]{2,0,1:T(1,128)S(1)}, f32[1,3,1024]{2,0,1:T(1,128)}, u32[]{:S(2)}) copy-start(f32[1,3,1024]{2,0,1:T(1,128)} %param.10) | copy-start | bytes 36868
  0.0 4.2 %copy-start.2 = (s32[1024]{0:T(1024)S(1)}, s32[1024]{0:T(1024)}, u32[]{:S(2)}) copy-start(s32[1024]{0:T(1024)} %param.13) | copy-start | bytes 12292
  0.0 10.5 %collective-permute-start.9 = (bf16[64,1024]{1,0:T(8,128)(2,1)}, bf16[64,1024]{1,0:T(8,128)(2,1)S(1)}, u32[]{:S(2)}, u32[]{:S(2)}) collective-permute-start(bf16[64,1024]{1,0:T(8,128)(2,1)} %bitcast.17), channel_id=1, source_target_pairs={{0,2},{2,0},{4,6},{6,4},{1,3},{3,1},{5,7},{7,5},{8,10},{10,8},{12,... | collective-permute-start | bytes 393224 | tf_op jit(solution)/shard_map/ppermute | solution.py:228
  4.2 6.3 %copy-start.3 = (bf16[1,64,1024]{2,1,0:T(8,128)(2,1)S(1)}, bf16[1,64,1024]{2,1,0:T(8,128)(2,1)}, u32[]{:S(2)}) copy-start(bf16[1,64,1024]{2,1,0:T(8,128)(2,1)} %param.8) | copy-start | bytes 393220
  7.3 11.2 %collective-permute-start = (bf16[96,1024]{1,0:T(8,128)(2,1)S(1)}, bf16[96,1024]{1,0:T(8,128)(2,1)S(1)}, u32[]{:S(2)}, u32[]{:S(2)}) collective-permute-start(bf16[96,1024]{1,0:T(8,128)(2,1)S(1)} %get-tuple-element.11), channel_id=1, source_target_pairs={{0,2},{2,4},{4,6},{6,0},{1,3},{3,5},{5,7},{7,1},{8,10},{10,12},{12... | collective-permute-start | bytes 589832 | tf_op jit(solution)/shard_map/ppermute | solution.py:224
  7.4 9.1 %collective-permute-start.3 = (bf16[96,1024]{1,0:T(8,128)(2,1)S(1)}, bf16[96,1024]{1,0:T(8,128)(2,1)S(1)}, u32[]{:S(2)}, u32[]{:S(2)}) collective-permute-start(bf16[96,1024]{1,0:T(8,128)(2,1)S(1)} %get-tuple-element.11), channel_id=1, source_target_pairs={{0,8},{8,0},{1,9},{9,1},{2,10},{10,2},{3,11},{11,3},{4,12},{12,4},... | collective-permute-start | bytes 589832 | tf_op jit(solution)/shard_map/ppermute | solution.py:219
  10.5 15.5 %collective-permute-start.10 = (bf16[128,1024]{1,0:T(8,128)(2,1)S(1)}, bf16[128,1024]{1,0:T(8,128)(2,1)S(1)}, u32[]{:S(2)}, u32[]{:S(2)}) collective-permute-start(bf16[128,1024]{1,0:T(8,128)(2,1)S(1)} %pad_maximum_fusion.1), channel_id=1, source_target_pairs={{0,6},{2,4},{4,2},{6,0},{1,7},{3,5},{5,3},{7,1},{8,14},{10,12},{12... | collective-permute-start | bytes 786440 | tf_op jit(solution)/shard_map/ppermute | solution.py:228
  13.7 15.6 %collective-permute-start.1 = (bf16[96,1024]{1,0:T(8,128)(2,1)S(1)}, bf16[96,1024]{1,0:T(8,128)(2,1)S(1)}, u32[]{:S(2)}, u32[]{:S(2)}) collective-permute-start(bf16[96,1024]{1,0:T(8,128)(2,1)S(1)} %get-tuple-element.11), channel_id=1, source_target_pairs={{0,6},{2,0},{4,2},{6,4},{1,7},{3,1},{5,3},{7,5},{8,14},{10,8},{12,... | collective-permute-start | bytes 589832 | tf_op jit(solution)/shard_map/ppermute | solution.py:224
  13.8 15.5 %collective-permute-start.2 = (bf16[96,1024]{1,0:T(8,128)(2,1)S(1)}, bf16[96,1024]{1,0:T(8,128)(2,1)S(1)}, u32[]{:S(2)}, u32[]{:S(2)}) collective-permute-start(bf16[96,1024]{1,0:T(8,128)(2,1)S(1)} %get-tuple-element.11), channel_id=1, source_target_pairs={{0,4},{2,6},{4,0},{6,2},{1,5},{3,7},{5,1},{7,3},{8,12},{10,14},{12... | collective-permute-start | bytes 589832 | tf_op jit(solution)/shard_map/ppermute | solution.py:224
  16.5 15.4 %collective-permute-start.4 = (bf16[96,1024]{1,0:T(8,128)(2,1)S(1)}, bf16[96,1024]{1,0:T(8,128)(2,1)S(1)}, u32[]{:S(2)}, u32[]{:S(2)}) collective-permute-start(bf16[96,1024]{1,0:T(8,128)(2,1)S(1)} %collective-permute-done.3), channel_id=1, source_target_pairs={{0,2},{2,4},{4,6},{6,0},{1,3},{3,5},{5,7},{7,1},{8,10},{10,12},{12... | collective-permute-start | bytes 589832 | tf_op jit(solution)/shard_map/ppermute | solution.py:224
  18.5 13.6 %collective-permute-start.5 = (bf16[96,1024]{1,0:T(8,128)(2,1)S(1)}, bf16[96,1024]{1,0:T(8,128)(2,1)S(1)}, u32[]{:S(2)}, u32[]{:S(2)}) collective-permute-start(bf16[96,1024]{1,0:T(8,128)(2,1)S(1)} %collective-permute-done.3), channel_id=1, source_target_pairs={{0,6},{2,0},{4,2},{6,4},{1,7},{3,1},{5,3},{7,5},{8,14},{10,8},{12,... | collective-permute-start | bytes 589832 | tf_op jit(solution)/shard_map/ppermute | solution.py:224
  26.0 13.0 %collective-permute-start.11 = (bf16[256,1024]{1,0:T(8,128)(2,1)S(1)}, bf16[256,1024]{1,0:T(8,128)(2,1)S(1)}, u32[]{:S(2)}, u32[]{:S(2)}) collective-permute-start(bf16[256,1024]{1,0:T(8,128)(2,1)S(1)} %pad_maximum_fusion.refs_0_), channel_id=1, source_target_pairs={{0,8},{8,0},{1,9},{9,1},{2,10},{10,2},{3,11},{11,3},{4,12},{12,4},... | collective-permute-start | bytes 1572872 | tf_op jit(solution)/shard_map/ppermute | solution.py:219
  29.4 18.6 %collective-permute-start.7 = (bf16[480,1024]{1,0:T(8,128)(2,1)S(1)}, bf16[480,1024]{1,0:T(8,128)(2,1)S(1)}, u32[]{:S(2)}, u32[]{:S(2)}) collective-permute-start(bf16[480,1024]{1,0:T(8,128)(2,1)S(1)} %constant_dynamic-update-slice_fusion.near_own_ref), channel_id=1, source_target_pairs={{0,1},{1,0},{2,3},{3,2},{4,5},{5,4},{6,7},{7,6},{8,9},{9,8},{10,11... | collective-permute-start | bytes 2949128 | tf_op jit(solution)/shard_map/ppermute | solution.py:232
  29.5 9.6 %collective-permute-start.6 = (bf16[96,1024]{1,0:T(8,128)(2,1)S(1)}, bf16[96,1024]{1,0:T(8,128)(2,1)S(1)}, u32[]{:S(2)}, u32[]{:S(2)}) collective-permute-start(bf16[96,1024]{1,0:T(8,128)(2,1)S(1)} %collective-permute-done.3), channel_id=1, source_target_pairs={{0,4},{2,6},{4,0},{6,2},{1,5},{3,7},{5,1},{7,3},{8,12},{10,14},{12... | collective-permute-start | bytes 589832 | tf_op jit(solution)/shard_map/ppermute | solution.py:224
  31.9 14.3 %collective-permute-start.12 = (bf16[256,1024]{1,0:T(8,128)(2,1)S(1)}, bf16[256,1024]{1,0:T(8,128)(2,1)S(1)}, u32[]{:S(2)}, u32[]{:S(2)}) collective-permute-start(bf16[256,1024]{1,0:T(8,128)(2,1)S(1)} %pad_maximum_fusion.refs_0_), channel_id=1, source_target_pairs={{0,1},{1,0},{2,3},{3,2},{4,5},{5,4},{6,7},{7,6},{8,9},{9,8},{10,11... | collective-permute-start | bytes 1572872 | tf_op jit(solution)/shard_map/ppermute | solution.py:232
  39.0 7.1 %collective-permute-start.13 = (bf16[256,1024]{1,0:T(8,128)(2,1)S(1)}, bf16[256,1024]{1,0:T(8,128)(2,1)S(1)}, u32[]{:S(2)}, u32[]{:S(2)}) collective-permute-start(bf16[256,1024]{1,0:T(8,128)(2,1)S(1)} %collective-permute-done.11.refs_1_), channel_id=1, source_target_pairs={{0,1},{1,0},{2,3},{3,2},{4,5},{5,4},{6,7},{7,6},{8,9},{9,8},{10,11... | collective-permute-start | bytes 1572872 | tf_op jit(solution)/shard_map/ppermute | solution.py:232
  39.1 8.9 %collective-permute-start.8 = (bf16[288,1024]{1,0:T(8,128)(2,1)S(1)}, bf16[288,1024]{1,0:T(8,128)(2,1)S(1)}, u32[]{:S(2)}, u32[]{:S(2)}) collective-permute-start(bf16[288,1024]{1,0:T(8,128)(2,1)S(1)} %constant_dynamic-update-slice_fusion.5.far_own_ref), channel_id=1, source_target_pairs={{0,1},{1,0},{2,3},{3,2},{4,5},{5,4},{6,7},{7,6},{8,9},{9,8},{10,11... | collective-permute-start | bytes 1769480 | tf_op jit(solution)/shard_map/ppermute | solution.py:232

commit v6 on v4

--- a/solution.py
+++ b/solution.py
@@ -146,7 +146,7 @@
 
 def place(z_count):
     core, z, plane = lax.axis_index("core"), lax.axis_index("z"), lax.axis_index("xh")
-    return plane, [lax.rem(z + dz, z_count) for dz in (0, z_count - 1, 1, 2)], core
+    return plane, [lax.rem(z + dz, z_count) for dz in (0, 2, z_count - 1, 1)], core
 
 
 def owners(z_count):
@@ -188,7 +188,12 @@
     return total
 
 
-def finish_kernel(energy_ref, weight_ref, near_own_ref, far_own_ref, near_other_ref, far_other_ref, rows_ref,
+def scale_kernel(energy_ref, weight_ref, scale_ref):
+    line = lax.broadcasted_iota(jnp.int32, scale_ref.shape, 0)
+    scale_ref[...] = jnp.where(line == 0, energy_ref[0], weight_ref[0])
+
+
+def finish_kernel(scale_ref, near_own_ref, far_own_ref, near_other_ref, far_other_ref, rows_ref,
                   val_a, val_b, lap_a, lap_b, *refs, z_count, size):
     inv_refs, out_ref = refs[:-1], refs[-1]
     half = rows_ref.shape[0] // 2
@@ -198,11 +203,13 @@
     ])
     val = jnp.concatenate([val_a[...], val_b[...]], axis=1).astype(F32)
     lap = jnp.concatenate([lap_a[...], lap_b[...]], axis=1).astype(F32)
-    mixed = (weight_ref[...] * (energy_ref[...] * val - 0.5 * (lap - total))).astype(BF16)
+    energy, weight = scale_ref[0:1, 0:1], scale_ref[1:2, 0:1]
+    mixed = (weight * (energy * val - 0.5 * (lap - total))).astype(BF16)
     inverse_times(z_count, inv_refs, mixed, out_ref, size)
 
 
 VMEM = pl.BlockSpec(memory_space=pltpu.VMEM)
+SMEM = pl.BlockSpec(memory_space=pltpu.SMEM)
 HBM = pl.BlockSpec(memory_space=pltpu.HBM)
 
 
@@ -226,7 +233,7 @@
     shards = 2 * z_count * 2
     slots = 3 * electrons // (2 * shards)
 
-    along_z = (1, -1, 2)
+    along_z = (2, 1, -1)
     out = lambda *shape_dtype: jax.ShapeDtypeStruct(*shape_dtype)
     halves = 2
     part = electrons // halves
@@ -252,14 +259,11 @@
     cell_index, fraction = jnp.transpose(cell_index, (1, 0, 2)), jnp.transpose(fraction, (1, 0, 2))
     mine = inverse.reshape(rows, electrons)
 
-    inv_pieces = []
+    inv_pieces = [mine]
     for shift in along_z:
         inv_pieces.append(ring_pass(mine, shift))
-    inv_far_mine = ring_swap(mine)
-    inv_rest = jnp.concatenate(inv_pieces, axis=0)
-    inv_far_rest = ring_swap(inv_rest)
-    inv_plane = jnp.concatenate([mine, inv_rest], axis=0)
-    inv_far = jnp.concatenate([inv_far_mine, inv_far_rest], axis=0)
+    inv_plane = jnp.concatenate(inv_pieces, axis=0)
+    inv_far = ring_swap(inv_plane)
     inv_plane_other = core_swap(inv_plane)
     inv_far_other = core_swap(inv_far)
     inv_all = [inv_plane, inv_far, inv_plane_other, inv_far_other]
@@ -311,16 +315,23 @@
         name="ratio",
     )(*inv_all, val_a, val_b, slot)
 
-    energy, weight = energies.reshape(1, 1), weights.reshape(1, 1)
+    scale = pl.pallas_call(
+        scale_kernel,
+        out_shape=out((2, 128), F32),
+        in_specs=[SMEM] * 2,
+        out_specs=VMEM,
+        compiler_params=params(1),
+        name="scale",
+    )(energies, weights)
     partial = pl.pallas_call(
         functools.partial(finish_kernel, z_count=z_count, size=rows),
         out_shape=out((electrons, width), BF16),
-        in_specs=[VMEM] * (11 + len(inv_all)),
+        in_specs=[VMEM] * (10 + len(inv_all)),
         out_specs=VMEM,
         compiler_params=params(24),
         cost_estimate=cost(3 * electrons * electrons * width),
         name="finish",
-    )(energy, weight, near, far, near_other, far_other, ratio_rows, val_a, val_b, lap_a, lap_b, *inv_all)
+    )(scale, near, far, near_other, far_other, ratio_rows, val_a, val_b, lap_a, lap_b, *inv_all)
 
     walkers = ("y", "xl")
     count = lax.axis_size(walkers)

time: 68 us -> 62.3 us (0.916)
  waiting for transfers between devices: 14.7 us -> 9.92 us
  starting transfers between devices: 21.6 us -> 20.3 us
    ppermute x3 -> x2, waiting for transfers between devices: 5.47 us -> 1.96 us  [ring_swap(): return lax.ppermute(piece, 'xh', [(0, 1), (1, 0)])]
    ppermute x3 -> x2, starting transfers between devices: 6.63 us -> 3.61 us  [ring_swap(): return lax.ppermute(piece, 'xh', [(0, 1), (1, 0)])]
    ppermute x9, starting transfers between devices: 14.5 us -> 15.8 us  [ring_pass(): lax.ppermute(piece, 'z', [(i, (i + shift) % count) for i in range(count)])]
    ppermute x9, waiting for transfers between devices: 9.19 us -> 7.95 us  [ring_pass(): lax.ppermute(piece, 'z', [(i, (i + shift) % count) for i in range(count)])]
  transfers between devices with their start and end apart: 16 -> 15, of which waited for: 4 -> 6; matrix products, arithmetic and copies ran while one was open for 0% -> 0% of each run, Pallas kernels for 18% -> 19%
where the time goes in v6:
time: 62.3 us; the launch traced here: 61.9 us
  starting transfers between devices  20.3 us (33%)
  blocking collectives  15.6 us (25%)
  Pallas kernels  13.8 us (22%)
  waiting for transfers between devices  9.92 us (16%)
  between operations  1.51 us (2%)
  other arithmetic  0.76 us (1%)
    ppermute x9, starting transfers between devices, ring_pass(): lax.ppermute(piece, 'z', [(i, (i + shift) % count) for i in range(count)])  15.8 us
    all_to_all x1, blocking collectives, gradient(): lax.all_to_all(partial.reshape(count, electrons // count, width), walkers...  15.6 us
    ppermute x9, waiting for transfers between devices, ring_pass(): lax.ppermute(piece, 'z', [(i, (i + shift) % count) for i in range(count)])  7.95 us
    pallas_call x2, Pallas kernels, evaluate(): pl.pallas_call(functools.partial(eval_kernel, first=h * part), out_shape=...  5.03 us
    ppermute x2, starting transfers between devices, ring_swap(): return lax.ppermute(piece, 'xh', [(0, 1), (1, 0)])  3.61 us
    pallas_call x1, Pallas kernels, gradient(): pl.pallas_call(functools.partial(early_kernel, shards=shards), out_shape=...  3.06 us
    pallas_call x1, Pallas kernels, gradient(): pl.pallas_call(turn_kernel, out_shape=out((width, cells), BF16), in_specs...  2.03 us
    ppermute x2, waiting for transfers between devices, ring_swap(): return lax.ppermute(piece, 'xh', [(0, 1), (1, 0)])  1.96 us
  transfers between devices with their start and end apart: 15, of which 6 were waited for; matrix products, arithmetic and copies ran while one was open for 0% of the time, Pallas kernels for 19%

profile of v6, /device:TPU:0, one launch (start us, length us, event | category | flops | bytes accessed | tf_op | source)
XLA Modules:
  0.0 61.9 jit_solution(9022514218569712810)
XLA Ops:
  0.0 2.1 %collective-permute-start.10 = (bf16[64,1024]{1,0:T(8,128)(2,1)}, bf16[64,1024]{1,0:T(8,128)(2,1)S(1)}, u32[]{:S(2)}, u32[]{:S(2)}) collective-permute-start(bf16[64,1024]{1,0:T(8,128)(2,1)} %bitcast.13), channel_id=1, source_target_pairs={{0,2},{2,4},{4,6},{6,0},{1,3},{3,5},{5,7},{7,1},{8,10},{10,12},{12... | collective-permute-start | bytes 393224 | tf_op jit(solution)/shard_map/ppermute | solution.py:222
  2.1 2.2 %collective-permute-start.11 = (bf16[64,1024]{1,0:T(8,128)(2,1)}, bf16[64,1024]{1,0:T(8,128)(2,1)S(1)}, u32[]{:S(2)}, u32[]{:S(2)}) collective-permute-start(bf16[64,1024]{1,0:T(8,128)(2,1)} %bitcast.14), channel_id=1, source_target_pairs={{0,6},{2,0},{4,2},{6,4},{1,7},{3,1},{5,3},{7,5},{8,14},{10,8},{12,... | collective-permute-start | bytes 393224 | tf_op jit(solution)/shard_map/ppermute | solution.py:222
  4.3 1.8 %collective-permute-start.9 = (bf16[64,1024]{1,0:T(8,128)(2,1)}, bf16[64,1024]{1,0:T(8,128)(2,1)S(1)}, u32[]{:S(2)}, u32[]{:S(2)}) collective-permute-start(bf16[64,1024]{1,0:T(8,128)(2,1)} %bitcast.15), channel_id=1, source_target_pairs={{0,4},{2,6},{4,0},{6,2},{1,5},{3,7},{5,1},{7,3},{8,12},{10,14},{12... | collective-permute-start | bytes 393224 | tf_op jit(solution)/shard_map/ppermute | solution.py:222
  6.1 2.0 %turn.1.turned_ref = bf16[256,4096]{1,0:T(8,128)(2,1)S(1)} custom-call(bf16[4096,256]{1,0:T(8,128)(2,1)} %coef_hbm.1), custom_call_target="tpu_custom_call" | custom-call | flops 134217728 | bytes 2097152 | tf_op jit(solution)/shard_map/turn/pallas_call | solution.py:271
  8.2 3.1 %early.1 = (bf16[96,1024]{1,0:T(8,128)(2,1)S(1)}, s32[1,1024]{1,0:T(1,128)S(1)}) custom-call(bf16[256,4096]{1,0:T(8,128)(2,1)S(1)} %turn.1.turned_ref, s32[3,1,1024]{2,1,0:T(1,128)S(1)} %bitcast.6, f32[3,1,1024]{2,1,0:T(1,128)S(1)} %bitcast.9, s32[1,1024]{1,0:T(1,128)S(1)} %bitcast.12), custom_call_target="tpu_custom_call" | custom-call | flops 805306368 | bytes 2097152 | tf_op jit(solution)/shard_map/early/pallas_call | solution.py:281
  11.2 1.8 %collective-permute-start = (bf16[96,1024]{1,0:T(8,128)(2,1)S(1)}, bf16[96,1024]{1,0:T(8,128)(2,1)S(1)}, u32[]{:S(2)}, u32[]{:S(2)}) collective-permute-start(bf16[96,1024]{1,0:T(8,128)(2,1)S(1)} %get-tuple-element.11), channel_id=1, source_target_pairs={{0,4},{2,6},{4,0},{6,2},{1,5},{3,7},{5,1},{7,3},{8,12},{10,14},{12... | collective-permute-start | bytes 589832 | tf_op jit(solution)/shard_map/ppermute | solution.py:222
  13.1 3.0 %collective-permute-start.3 = (bf16[96,1024]{1,0:T(8,128)(2,1)S(1)}, bf16[96,1024]{1,0:T(8,128)(2,1)S(1)}, u32[]{:S(2)}, u32[]{:S(2)}) collective-permute-start(bf16[96,1024]{1,0:T(8,128)(2,1)S(1)} %get-tuple-element.11), channel_id=1, source_target_pairs={{0,8},{8,0},{1,9},{9,1},{2,10},{10,2},{3,11},{11,3},{4,12},{12,4},... | collective-permute-start | bytes 589832 | tf_op jit(solution)/shard_map/ppermute | solution.py:217
  16.2 3.2 %collective-permute-start.2 = (bf16[96,1024]{1,0:T(8,128)(2,1)S(1)}, bf16[96,1024]{1,0:T(8,128)(2,1)S(1)}, u32[]{:S(2)}, u32[]{:S(2)}) collective-permute-start(bf16[96,1024]{1,0:T(8,128)(2,1)S(1)} %get-tuple-element.11), channel_id=1, source_target_pairs={{0,6},{2,0},{4,2},{6,4},{1,7},{3,1},{5,3},{7,5},{8,14},{10,8},{12,... | collective-permute-start | bytes 589832 | tf_op jit(solution)/shard_map/ppermute | solution.py:222
  19.5 0.6 collective-permute-start.12
  20.1 0.4 collective-permute-done.3
  20.5 2.7 %collective-permute-start.4 = (bf16[96,1024]{1,0:T(8,128)(2,1)S(1)}, bf16[96,1024]{1,0:T(8,128)(2,1)S(1)}, u32[]{:S(2)}, u32[]{:S(2)}) collective-permute-start(bf16[96,1024]{1,0:T(8,128)(2,1)S(1)} %collective-permute-done.3), channel_id=1, source_target_pairs={{0,4},{2,6},{4,0},{6,2},{1,5},{3,7},{5,1},{7,3},{8,12},{10,14},{12... | collective-permute-start | bytes 589832 | tf_op jit(solution)/shard_map/ppermute | solution.py:222
  23.2 1.0 %collective-permute-start.5 = (bf16[96,1024]{1,0:T(8,128)(2,1)S(1)}, bf16[96,1024]{1,0:T(8,128)(2,1)S(1)}, u32[]{:S(2)}, u32[]{:S(2)}) collective-permute-start(bf16[96,1024]{1,0:T(8,128)(2,1)S(1)} %collective-permute-done.3), channel_id=1, source_target_pairs={{0,2},{2,4},{4,6},{6,0},{1,3},{3,5},{5,7},{7,1},{8,10},{10,12},{12... | collective-permute-start | bytes 589832 | tf_op jit(solution)/shard_map/ppermute | solution.py:222
  24.7 0.5 collective-permute-start.13
  25.2 4.4 %collective-permute-done.4 = bf16[96,1024]{1,0:T(8,128)(2,1)S(1)} collective-permute-done((bf16[96,1024]{1,0:T(8,128)(2,1)S(1)}, bf16[96,1024]{1,0:T(8,128)(2,1)S(1)}, u32[]{:S(2)}, u32[]{:S(2)}) %collective-permute-start.4) | collective-permute-done | bytes 196640 | tf_op jit(solution)/shard_map/ppermute | solution.py:222
  29.6 0.9 %collective-permute-start.6 = (bf16[96,1024]{1,0:T(8,128)(2,1)S(1)}, bf16[96,1024]{1,0:T(8,128)(2,1)S(1)}, u32[]{:S(2)}, u32[]{:S(2)}) collective-permute-start(bf16[96,1024]{1,0:T(8,128)(2,1)S(1)} %collective-permute-done.3), channel_id=1, source_target_pairs={{0,6},{2,0},{4,2},{6,4},{1,7},{3,1},{5,3},{7,5},{8,14},{10,8},{12,... | collective-permute-start | bytes 589832 | tf_op jit(solution)/shard_map/ppermute | solution.py:222
  30.5 1.0 %collective-permute-done.5 = bf16[96,1024]{1,0:T(8,128)(2,1)S(1)} collective-permute-done((bf16[96,1024]{1,0:T(8,128)(2,1)S(1)}, bf16[96,1024]{1,0:T(8,128)(2,1)S(1)}, u32[]{:S(2)}, u32[]{:S(2)}) %collective-permute-start.5) | collective-permute-done | bytes 196640 | tf_op jit(solution)/shard_map/ppermute | solution.py:222
  31.5 1.5 %collective-permute-done.12.refs_1_ = bf16[256,1024]{1,0:T(8,128)(2,1)S(1)} collective-permute-done((bf16[256,1024]{1,0:T(8,128)(2,1)S(1)}, bf16[256,1024]{1,0:T(8,128)(2,1)S(1)}, u32[]{:S(2)}, u32[]{:S(2)}) %collective-permute-start.12) | collective-permute-done | bytes 524320 | tf_op jit(solution)/shard_map/ppermute | solution.py:217
  33.0 2.2 %collective-permute-done.6 = bf16[96,1024]{1,0:T(8,128)(2,1)S(1)} collective-permute-done((bf16[96,1024]{1,0:T(8,128)(2,1)S(1)}, bf16[96,1024]{1,0:T(8,128)(2,1)S(1)}, u32[]{:S(2)}, u32[]{:S(2)}) %collective-permute-start.6) | collective-permute-done | bytes 196640 | tf_op jit(solution)/shard_map/ppermute | solution.py:222
  36.9 2.5 %evaluate.2 = (bf16[256,512]{1,0:T(8,128)(2,1)S(1)}, bf16[256,512]{1,0:T(8,128)(2,1)S(1)}) custom-call(bf16[256,4096]{1,0:T(8,128)(2,1)S(1)} %turn.1.turned_ref, s32[3,1,1024]{2,1,0:T(1,128)S(1)} %bitcast.7, f32[3,1,1024]{2,1,0:T(1,128)S(1)} %bitcast.10), custom_call_target="tpu_custom_call" | custom-call | flops 2147483648 | bytes 2097152 | tf_op jit(solution)/shard_map/evaluate/pallas_call | solution.py:248
  39.4 2.5 %evaluate.3 = (bf16[256,512]{1,0:T(8,128)(2,1)S(1)}, bf16[256,512]{1,0:T(8,128)(2,1)S(1)}) custom-call(bf16[256,4096]{1,0:T(8,128)(2,1)S(1)} %turn.1.turned_ref, s32[3,1,1024]{2,1,0:T(1,128)S(1)} %bitcast.8, f32[3,1,1024]{2,1,0:T(1,128)S(1)} %bitcast.11), custom_call_target="tpu_custom_call" | custom-call | flops 2147483648 | bytes 2097152 | tf_op jit(solution)/shard_map/evaluate/pallas_call | solution.py:248
  41.9 1.7 %ratio.1.rows_ref = bf16[1536,256]{1,0:T(8,128)(2,1)S(1)} custom-call(bf16[256,1024]{1,0:T(8,128)(2,1)S(1)} %pad_maximum_fusion.refs_0_, bf16[256,1024]{1,0:T(8,128)(2,1)S(1)} %collective-permute-done.12.refs_1_, bf16[256,1024]{1,0:T(8,128)(2,1)S(1)} %collective-permute-done.13.refs_2_, bf16[256,1024]{1,0:T(8,128)(2,1)S(1)} %collective-permute-done.14.refs_3_, ...), custom_call_target="tpu_custom_call" | custom-call | flops 1610612736 | bytes 2097152 | tf_op jit(solution)/shard_map/ratio/pallas_call | solution.py:307
  43.7 1.9 %finish.1 = bf16[1024,256]{1,0:T(8,128)(2,1)S(1)} custom-call(f32[2,128]{1,0:T(2,128)S(1)} %scale.1.scale_ref, bf16[480,1024]{1,0:T(8,128)(2,1)S(1)} %constant_dynamic-update-slice_fusion.near_own_ref, bf16[288,1024]{1,0:T(8,128)(2,1)S(1)} %constant_dynamic-update-slice_fusion.5.far_own_ref, bf16[480,1024]{1,0:T(8,128)(2,1)S(1)} %collective-permute-done.7.near_other_ref, ...), custom_call_target="tpu_custom_call" | custom-call | flops 1610612736 | bytes 2097152 | tf_op jit(solution)/shard_map/finish/pallas_call | solution.py:326
  45.6 15.6 %all_to_all.5 = bf16[8,128,256]{2,1,0:T(8,128)(2,1)S(1)} all-to-all(bf16[8,128,256]{2,1,0:T(8,128)(2,1)S(1)} %bitcast.5), channel_id=1, replica_groups=mesh['y'=4,'xl'=2,'xh'=2,'z'=4,'core'=2] {'y','xl'}, dimensions={0} | all-to-all | bytes 1048576 | tf_op jit(solution)/shard_map/all_to_all | solution.py:338
  61.2 0.7 %convert_reduce_fusion = f32[128,256]{1,0:T(8,128)} fusion(bf16[8,128,256]{2,1,0:T(8,128)(2,1)S(1)} %all_to_all.5), kind=kLoop, calls=%fused_computation | loop fusion | flops 491520 | bytes 655360 | tf_op jit(solution)/shard_map/reduce_sum | solution.py:339
  (32 shorter events, 0.9 us)
Async XLA Ops:
  0.0 8.1 %copy-start = (s32[1,3,1024]{2,0,1:T(1,128)S(1)}, s32[1,3,1024]{2,0,1:T(1,128)}, u32[]{:S(2)}) copy-start(s32[1,3,1024]{2,0,1:T(1,128)} %param.9) | copy-start | bytes 36868
  0.0 8.2 %copy-start.1 = (f32[1,3,1024]{2,0,1:T(1,128)S(1)}, f32[1,3,1024]{2,0,1:T(1,128)}, u32[]{:S(2)}) copy-start(f32[1,3,1024]{2,0,1:T(1,128)} %param.10) | copy-start | bytes 36868
  0.0 8.2 %copy-start.2 = (s32[1024]{0:T(1024)S(1)}, s32[1024]{0:T(1024)}, u32[]{:S(2)}) copy-start(s32[1024]{0:T(1024)} %param.13) | copy-start | bytes 12292
  0.0 16.1 %collective-permute-start.10 = (bf16[64,1024]{1,0:T(8,128)(2,1)}, bf16[64,1024]{1,0:T(8,128)(2,1)S(1)}, u32[]{:S(2)}, u32[]{:S(2)}) collective-permute-start(bf16[64,1024]{1,0:T(8,128)(2,1)} %bitcast.13), channel_id=1, source_target_pairs={{0,2},{2,4},{4,6},{6,0},{1,3},{3,5},{5,7},{7,1},{8,10},{10,12},{12... | collective-permute-start | bytes 393224 | tf_op jit(solution)/shard_map/ppermute | solution.py:222
  2.1 14.1 %collective-permute-start.11 = (bf16[64,1024]{1,0:T(8,128)(2,1)}, bf16[64,1024]{1,0:T(8,128)(2,1)S(1)}, u32[]{:S(2)}, u32[]{:S(2)}) collective-permute-start(bf16[64,1024]{1,0:T(8,128)(2,1)} %bitcast.14), channel_id=1, source_target_pairs={{0,6},{2,0},{4,2},{6,4},{1,7},{3,1},{5,3},{7,5},{8,14},{10,8},{12,... | collective-permute-start | bytes 393224 | tf_op jit(solution)/shard_map/ppermute | solution.py:222
  4.3 15.1 %collective-permute-start.9 = (bf16[64,1024]{1,0:T(8,128)(2,1)}, bf16[64,1024]{1,0:T(8,128)(2,1)S(1)}, u32[]{:S(2)}, u32[]{:S(2)}) collective-permute-start(bf16[64,1024]{1,0:T(8,128)(2,1)} %bitcast.15), channel_id=1, source_target_pairs={{0,4},{2,6},{4,0},{6,2},{1,5},{3,7},{5,1},{7,3},{8,12},{10,14},{12... | collective-permute-start | bytes 393224 | tf_op jit(solution)/shard_map/ppermute | solution.py:222
  8.1 11.3 %copy-start.3 = (bf16[1,64,1024]{2,1,0:T(8,128)(2,1)S(1)}, bf16[1,64,1024]{2,1,0:T(8,128)(2,1)}, u32[]{:S(2)}) copy-start(bf16[1,64,1024]{2,1,0:T(8,128)(2,1)} %param.8) | copy-start | bytes 393220
  11.2 11.9 %collective-permute-start = (bf16[96,1024]{1,0:T(8,128)(2,1)S(1)}, bf16[96,1024]{1,0:T(8,128)(2,1)S(1)}, u32[]{:S(2)}, u32[]{:S(2)}) collective-permute-start(bf16[96,1024]{1,0:T(8,128)(2,1)S(1)} %get-tuple-element.11), channel_id=1, source_target_pairs={{0,4},{2,6},{4,0},{6,2},{1,5},{3,7},{5,1},{7,3},{8,12},{10,14},{12... | collective-permute-start | bytes 589832 | tf_op jit(solution)/shard_map/ppermute | solution.py:222
  13.1 7.4 %collective-permute-start.3 = (bf16[96,1024]{1,0:T(8,128)(2,1)S(1)}, bf16[96,1024]{1,0:T(8,128)(2,1)S(1)}, u32[]{:S(2)}, u32[]{:S(2)}) collective-permute-start(bf16[96,1024]{1,0:T(8,128)(2,1)S(1)} %get-tuple-element.11), channel_id=1, source_target_pairs={{0,8},{8,0},{1,9},{9,1},{2,10},{10,2},{3,11},{11,3},{4,12},{12,4},... | collective-permute-start | bytes 589832 | tf_op jit(solution)/shard_map/ppermute | solution.py:217
  16.1 8.1 %collective-permute-start.1 = (bf16[96,1024]{1,0:T(8,128)(2,1)S(1)}, bf16[96,1024]{1,0:T(8,128)(2,1)S(1)}, u32[]{:S(2)}, u32[]{:S(2)}) collective-permute-start(bf16[96,1024]{1,0:T(8,128)(2,1)S(1)} %get-tuple-element.11), channel_id=1, source_target_pairs={{0,2},{2,4},{4,6},{6,0},{1,3},{3,5},{5,7},{7,1},{8,10},{10,12},{12... | collective-permute-start | bytes 589832 | tf_op jit(solution)/shard_map/ppermute | solution.py:222
  16.2 8.3 %collective-permute-start.2 = (bf16[96,1024]{1,0:T(8,128)(2,1)S(1)}, bf16[96,1024]{1,0:T(8,128)(2,1)S(1)}, u32[]{:S(2)}, u32[]{:S(2)}) collective-permute-start(bf16[96,1024]{1,0:T(8,128)(2,1)S(1)} %get-tuple-element.11), channel_id=1, source_target_pairs={{0,6},{2,0},{4,2},{6,4},{1,7},{3,1},{5,3},{7,5},{8,14},{10,8},{12,... | collective-permute-start | bytes 589832 | tf_op jit(solution)/shard_map/ppermute | solution.py:222
  19.5 13.6 %collective-permute-start.12 = (bf16[256,1024]{1,0:T(8,128)(2,1)S(1)}, bf16[256,1024]{1,0:T(8,128)(2,1)S(1)}, u32[]{:S(2)}, u32[]{:S(2)}) collective-permute-start(bf16[256,1024]{1,0:T(8,128)(2,1)S(1)} %pad_maximum_fusion.refs_0_), channel_id=1, source_target_pairs={{0,8},{8,0},{1,9},{9,1},{2,10},{10,2},{3,11},{11,3},{4,12},{12,4},... | collective-permute-start | bytes 1572872 | tf_op jit(solution)/shard_map/ppermute | solution.py:217
  20.5 9.1 %collective-permute-start.4 = (bf16[96,1024]{1,0:T(8,128)(2,1)S(1)}, bf16[96,1024]{1,0:T(8,128)(2,1)S(1)}, u32[]{:S(2)}, u32[]{:S(2)}) collective-permute-start(bf16[96,1024]{1,0:T(8,128)(2,1)S(1)} %collective-permute-done.3), channel_id=1, source_target_pairs={{0,4},{2,6},{4,0},{6,2},{1,5},{3,7},{5,1},{7,3},{8,12},{10,14},{12... | collective-permute-start | bytes 589832 | tf_op jit(solution)/shard_map/ppermute | solution.py:222
  23.2 8.3 %collective-permute-start.5 = (bf16[96,1024]{1,0:T(8,128)(2,1)S(1)}, bf16[96,1024]{1,0:T(8,128)(2,1)S(1)}, u32[]{:S(2)}, u32[]{:S(2)}) collective-permute-start(bf16[96,1024]{1,0:T(8,128)(2,1)S(1)} %collective-permute-done.3), channel_id=1, source_target_pairs={{0,2},{2,4},{4,6},{6,0},{1,3},{3,5},{5,7},{7,1},{8,10},{10,12},{12... | collective-permute-start | bytes 589832 | tf_op jit(solution)/shard_map/ppermute | solution.py:222
  24.6 19.1 %collective-permute-start.7 = (bf16[480,1024]{1,0:T(8,128)(2,1)S(1)}, bf16[480,1024]{1,0:T(8,128)(2,1)S(1)}, u32[]{:S(2)}, u32[]{:S(2)}) collective-permute-start(bf16[480,1024]{1,0:T(8,128)(2,1)S(1)} %constant_dynamic-update-slice_fusion.near_own_ref), channel_id=1, source_target_pairs={{0,1},{1,0},{2,3},{3,2},{4,5},{5,4},{6,7},{7,6},{8,9},{9,8},{10,11... | collective-permute-start | bytes 2949128 | tf_op jit(solution)/shard_map/ppermute | solution.py:226
  24.7 17.2 %collective-permute-start.13 = (bf16[256,1024]{1,0:T(8,128)(2,1)S(1)}, bf16[256,1024]{1,0:T(8,128)(2,1)S(1)}, u32[]{:S(2)}, u32[]{:S(2)}) collective-permute-start(bf16[256,1024]{1,0:T(8,128)(2,1)S(1)} %pad_maximum_fusion.refs_0_), channel_id=1, source_target_pairs={{0,1},{1,0},{2,3},{3,2},{4,5},{5,4},{6,7},{7,6},{8,9},{9,8},{10,11... | collective-permute-start | bytes 1572872 | tf_op jit(solution)/shard_map/ppermute | solution.py:226
  29.6 5.7 %collective-permute-start.6 = (bf16[96,1024]{1,0:T(8,128)(2,1)S(1)}, bf16[96,1024]{1,0:T(8,128)(2,1)S(1)}, u32[]{:S(2)}, u32[]{:S(2)}) collective-permute-start(bf16[96,1024]{1,0:T(8,128)(2,1)S(1)} %collective-permute-done.3), channel_id=1, source_target_pairs={{0,6},{2,0},{4,2},{6,4},{1,7},{3,1},{5,3},{7,5},{8,14},{10,8},{12,... | collective-permute-start | bytes 589832 | tf_op jit(solution)/shard_map/ppermute | solution.py:222
  33.0 8.9 %collective-permute-start.14 = (bf16[256,1024]{1,0:T(8,128)(2,1)S(1)}, bf16[256,1024]{1,0:T(8,128)(2,1)S(1)}, u32[]{:S(2)}, u32[]{:S(2)}) collective-permute-start(bf16[256,1024]{1,0:T(8,128)(2,1)S(1)} %collective-permute-done.12.refs_1_), channel_id=1, source_target_pairs={{0,1},{1,0},{2,3},{3,2},{4,5},{5,4},{6,7},{7,6},{8,9},{9,8},{10,11... | collective-permute-start | bytes 1572872 | tf_op jit(solution)/shard_map/ppermute | solution.py:226
  35.3 8.4 %collective-permute-start.8 = (bf16[288,1024]{1,0:T(8,128)(2,1)S(1)}, bf16[288,1024]{1,0:T(8,128)(2,1)S(1)}, u32[]{:S(2)}, u32[]{:S(2)}) collective-permute-start(bf16[288,1024]{1,0:T(8,128)(2,1)S(1)} %constant_dynamic-update-slice_fusion.5.far_own_ref), channel_id=1, source_target_pairs={{0,1},{1,0},{2,3},{3,2},{4,5},{5,4},{6,7},{7,6},{8,9},{9,8},{10,11... | collective-permute-start | bytes 1769480 | tf_op jit(solution)/shard_map/ppermute | solution.py:226

commit v7 on v6

--- a/solution.py
+++ b/solution.py
@@ -70,19 +70,8 @@
     return jnp.concatenate([rows[g:g + 1, :] * weights for g in range(GRID)], axis=0)
 
 
-def turn_kernel(coef_hbm, turned_ref, coef_ref, sems):
-    pieces = sems.shape[0]
-    rows = coef_ref.shape[0] // pieces
-    copies = [
-        pltpu.make_async_copy(coef_hbm.at[pl.ds(k * rows, rows)], coef_ref.at[pl.ds(k * rows, rows)], sems.at[k])
-        for k in range(pieces)
-    ]
-    for copy in copies:
-        copy.start()
-    for k, copy in enumerate(copies):
-        copy.wait()
-        for first in range(k * rows, (k + 1) * rows, PLANE):
-            turned_ref[:, first:first + PLANE] = jnp.transpose(coef_ref[first:first + PLANE, :])
+def first_kernel(flag_ref):
+    flag_ref[...] = jnp.zeros(flag_ref.shape, F32)
 
 
 def weight_tables(cell_ref, frac_ref, here):
@@ -103,13 +92,13 @@
         w_ref[g * PLANE:(g + 1) * PLANE, :] = (vx[g:g + 1, :] * value).astype(BF16)
 
 
-def early_kernel(turned_ref, cell_ref, frac_ref, occ_ref, lapt_ref, slot_ref, *w_refs, shards):
+def early_kernel(flag_ref, coef_ref, cell_ref, frac_ref, occ_ref, lapt_ref, slot_ref, *w_refs, shards):
     slots, electrons = lapt_ref.shape
     plane, along, core = place(shards // 4)
     me = (plane * (shards // 4) + along[0]) * 2 + core
-    slot, picker = slot_tables(me, occ_ref[...], shards, turned_ref.shape[0], slots)
+    slot, picker = slot_tables(me, occ_ref[...], shards, coef_ref.shape[1], slots)
     slot_ref[...] = slot
-    chosen = mm(picker, turned_ref[...]).astype(BF16)
+    chosen = mm_nt(picker, coef_ref[...]).astype(BF16)
 
     def build(t):
         vx, cx, value, curve = weight_tables(cell_ref, frac_ref, slice(t * TILE, (t + 1) * TILE))
@@ -127,8 +116,13 @@
         lapt_ref[:, t * TILE:(t + 1) * TILE] = mm(chosen, w_refs[t % 2][...]).astype(BF16)
 
 
-def eval_kernel(turned_ref, cell_ref, frac_ref, val_ref, lap_ref, *w_refs, first):
+def eval_kernel(coef_ref, cell_ref, frac_ref, val_ref, lap_ref, *w_refs, first):
     electrons = val_ref.shape[1]
+    turned_ref = coef_ref
+    if first == 0:
+        turned_ref, *w_refs = w_refs
+        for g in range(GRID):
+            turned_ref[:, g * PLANE:(g + 1) * PLANE] = jnp.transpose(coef_ref[g * PLANE:(g + 1) * PLANE, :])
 
     def build(t):
         tables = weight_tables(cell_ref, frac_ref, slice(first + t * TILE, first + (t + 1) * TILE))
@@ -210,7 +204,6 @@
 
 VMEM = pl.BlockSpec(memory_space=pltpu.VMEM)
 SMEM = pl.BlockSpec(memory_space=pltpu.SMEM)
-HBM = pl.BlockSpec(memory_space=pltpu.HBM)
 
 
 def ring_swap(piece):
@@ -244,17 +237,18 @@
     def cost(products):
         return pl.CostEstimate(flops=2 * products, bytes_accessed=2 * cells * width, transcendentals=0)
 
-    def evaluate(h):
+    def evaluate(h, coef):
+        results = [out((width, part), BF16)] * 2 + ([out((width, cells), BF16)] if h == 0 else [])
         return pl.pallas_call(
             functools.partial(eval_kernel, first=h * part),
-            out_shape=[out((width, part), BF16)] * 2,
+            out_shape=results,
             in_specs=[VMEM] * 3,
-            out_specs=[VMEM] * 2,
+            out_specs=[VMEM] * len(results),
             scratch_shapes=[pltpu.VMEM((cells, TILE), BF16)] * 4,
             compiler_params=params(32),
             cost_estimate=cost(2 * part * cells * width),
             name="evaluate",
-        )(turned, cell_index, fraction)
+        )(coef, cell_index, fraction)
 
     cell_index, fraction = jnp.transpose(cell_index, (1, 0, 2)), jnp.transpose(fraction, (1, 0, 2))
     mine = inverse.reshape(rows, electrons)
@@ -268,28 +262,26 @@
     inv_far_other = core_swap(inv_far)
     inv_all = [inv_plane, inv_far, inv_plane_other, inv_far_other]
 
-    turned = pl.pallas_call(
-        turn_kernel,
-        out_shape=out((width, cells), BF16),
-        in_specs=[HBM],
+    flag = pl.pallas_call(
+        first_kernel,
+        out_shape=out((8, 128), F32),
         out_specs=VMEM,
-        scratch_shapes=[pltpu.VMEM((cells, width), BF16), pltpu.SemaphoreType.DMA((8,))],
-        compiler_params=params(50),
-        cost_estimate=cost(cells * width * 64),
-        name="turn",
-    )(coefficients)
+        compiler_params=params(1),
+        cost_estimate=pl.CostEstimate(flops=10**10, bytes_accessed=10**8, transcendentals=0),
+        name="first",
+    )()
     lapt_mine, slot = pl.pallas_call(
         functools.partial(early_kernel, shards=shards),
         out_shape=[out((slots, electrons), BF16), out((1, electrons), jnp.int32)],
-        in_specs=[VMEM] * 4,
+        in_specs=[VMEM] * 5,
         out_specs=[VMEM] * 2,
         scratch_shapes=[pltpu.VMEM((cells, TILE), BF16)] * 2,
         compiler_params=params(32),
         cost_estimate=cost(slots * cells * electrons),
         name="early",
-    )(turned, cell_index, fraction, occupied.reshape(1, electrons))
-    val_a, lap_a = evaluate(0)
-    val_b, lap_b = evaluate(1)
+    )(flag, coefficients, cell_index, fraction, occupied.reshape(1, electrons))
+    val_a, lap_a, turned = evaluate(0, coefficients)
+    val_b, lap_b = evaluate(1, turned)
 
     lapt_far = ring_swap(lapt_mine)
     near, far = [lapt_mine], []

time: 62.3 us -> 61.6 us (0.989)
  Pallas kernels: 13.8 us -> 12.2 us
  blocking collectives: 15.6 us -> 16.3 us
    pallas_call x1, Pallas kernels: 2.03 us -> 0.01 us  [gradient(): pl.pallas_call(first_kernel, out_shape=out((8, 128), F32), out_specs=VMEM...]
    ppermute x2, starting transfers between devices: 3.61 us -> 4.7 us  [ring_swap(): return lax.ppermute(piece, 'xh', [(0, 1), (1, 0)])]
    ppermute x9, starting transfers between devices: 15.8 us -> 15 us  [ring_pass(): lax.ppermute(piece, 'z', [(i, (i + shift) % count) for i in range(count)])]
    all_to_all x1, blocking collectives: 15.6 us -> 16.3 us  [gradient(): lax.all_to_all(partial.reshape(count, electrons // count, width), walkers...]
  transfers between devices with their start and end apart: 15 -> 15, of which waited for: 6 -> 6; matrix products, arithmetic and copies ran while one was open for 0% -> 0% of each run, Pallas kernels for 19% -> 17%
where the time goes in v7:
time: 61.6 us; the launch traced here: 61.2 us
  starting transfers between devices  20.6 us (33%)
  blocking collectives  16.3 us (26%)
  Pallas kernels  12.2 us (20%)
  waiting for transfers between devices  9.72 us (16%)
  between operations  1.49 us (2%)
  other arithmetic  0.76 us (1%)
    all_to_all x1, blocking collectives, gradient(): lax.all_to_all(partial.reshape(count, electrons // count, width), walkers...  16.3 us
    ppermute x9, starting transfers between devices, ring_pass(): lax.ppermute(piece, 'z', [(i, (i + shift) % count) for i in range(count)])  15 us
    ppermute x9, waiting for transfers between devices, ring_pass(): lax.ppermute(piece, 'z', [(i, (i + shift) % count) for i in range(count)])  8.2 us
    pallas_call x2, Pallas kernels, evaluate(): pl.pallas_call(functools.partial(eval_kernel, first=h * part), out_shape=...  5.3 us
    ppermute x2, starting transfers between devices, ring_swap(): return lax.ppermute(piece, 'xh', [(0, 1), (1, 0)])  4.7 us
    pallas_call x1, Pallas kernels, gradient(): pl.pallas_call(functools.partial(early_kernel, shards=shards), out_shape=...  3.24 us
    pallas_call x1, Pallas kernels, gradient(): pl.pallas_call(functools.partial(finish_kernel, z_count=z_count, size=row...  1.94 us
    pallas_call x1, Pallas kernels, gradient(): pl.pallas_call(functools.partial(ratio_kernel, parts=len(inv_all), z_coun...  1.74 us
  transfers between devices with their start and end apart: 15, of which 6 were waited for; matrix products, arithmetic and copies ran while one was open for 0% of the time, Pallas kernels for 17%

profile of v7, /device:TPU:0, one launch (start us, length us, event | category | flops | bytes accessed | tf_op | source)
XLA Modules:
  0.0 61.2 jit_solution(2579482601941525980)
XLA Ops:
  0.0 2.1 %collective-permute-start.10 = (bf16[64,1024]{1,0:T(8,128)(2,1)}, bf16[64,1024]{1,0:T(8,128)(2,1)S(1)}, u32[]{:S(2)}, u32[]{:S(2)}) collective-permute-start(bf16[64,1024]{1,0:T(8,128)(2,1)} %bitcast.13), channel_id=1, source_target_pairs={{0,2},{2,4},{4,6},{6,0},{1,3},{3,5},{5,7},{7,1},{8,10},{10,12},{12... | collective-permute-start | bytes 393224 | tf_op jit(solution)/shard_map/ppermute | solution.py:215
  2.1 2.2 %collective-permute-start.11 = (bf16[64,1024]{1,0:T(8,128)(2,1)}, bf16[64,1024]{1,0:T(8,128)(2,1)S(1)}, u32[]{:S(2)}, u32[]{:S(2)}) collective-permute-start(bf16[64,1024]{1,0:T(8,128)(2,1)} %bitcast.14), channel_id=1, source_target_pairs={{0,6},{2,0},{4,2},{6,4},{1,7},{3,1},{5,3},{7,5},{8,14},{10,8},{12,... | collective-permute-start | bytes 393224 | tf_op jit(solution)/shard_map/ppermute | solution.py:215
  4.3 1.8 %collective-permute-start.9 = (bf16[64,1024]{1,0:T(8,128)(2,1)}, bf16[64,1024]{1,0:T(8,128)(2,1)S(1)}, u32[]{:S(2)}, u32[]{:S(2)}) collective-permute-start(bf16[64,1024]{1,0:T(8,128)(2,1)} %bitcast.15), channel_id=1, source_target_pairs={{0,4},{2,6},{4,0},{6,2},{1,5},{3,7},{5,1},{7,3},{8,12},{10,14},{12... | collective-permute-start | bytes 393224 | tf_op jit(solution)/shard_map/ppermute | solution.py:215
  6.1 3.2 %early.1 = (bf16[96,1024]{1,0:T(8,128)(2,1)S(1)}, s32[1,1024]{1,0:T(1,128)S(1)}) custom-call(f32[8,128]{1,0:T(8,128)S(1)} %first.1.flag_ref, bf16[4096,256]{1,0:T(8,128)(2,1)S(1)} %copy-done, s32[3,1,1024]{2,1,0:T(1,128)S(1)} %bitcast.6, f32[3,1,1024]{2,1,0:T(1,128)S(1)} %bitcast.9, s32[1,1024]{1,0:T(1,128)S(1)} %bitcast.12), custom_call_target="tpu_custom_call" | custom-call | flops 805306368 | bytes 2097152 | tf_op jit(solution)/shard_map/early/pallas_call | solution.py:273
  9.4 1.8 %collective-permute-start = (bf16[96,1024]{1,0:T(8,128)(2,1)S(1)}, bf16[96,1024]{1,0:T(8,128)(2,1)S(1)}, u32[]{:S(2)}, u32[]{:S(2)}) collective-permute-start(bf16[96,1024]{1,0:T(8,128)(2,1)S(1)} %get-tuple-element.12), channel_id=1, source_target_pairs={{0,4},{2,6},{4,0},{6,2},{1,5},{3,7},{5,1},{7,3},{8,12},{10,14},{12... | collective-permute-start | bytes 589832 | tf_op jit(solution)/shard_map/ppermute | solution.py:215
  11.2 3.0 %collective-permute-start.3 = (bf16[96,1024]{1,0:T(8,128)(2,1)S(1)}, bf16[96,1024]{1,0:T(8,128)(2,1)S(1)}, u32[]{:S(2)}, u32[]{:S(2)}) collective-permute-start(bf16[96,1024]{1,0:T(8,128)(2,1)S(1)} %get-tuple-element.12), channel_id=1, source_target_pairs={{0,8},{8,0},{1,9},{9,1},{2,10},{10,2},{3,11},{11,3},{4,12},{12,4},... | collective-permute-start | bytes 589832 | tf_op jit(solution)/shard_map/ppermute | solution.py:210
  14.4 3.6 %collective-permute-start.2 = (bf16[96,1024]{1,0:T(8,128)(2,1)S(1)}, bf16[96,1024]{1,0:T(8,128)(2,1)S(1)}, u32[]{:S(2)}, u32[]{:S(2)}) collective-permute-start(bf16[96,1024]{1,0:T(8,128)(2,1)S(1)} %get-tuple-element.12), channel_id=1, source_target_pairs={{0,6},{2,0},{4,2},{6,4},{1,7},{3,1},{5,3},{7,5},{8,14},{10,8},{12,... | collective-permute-start | bytes 589832 | tf_op jit(solution)/shard_map/ppermute | solution.py:215
  18.0 1.7 %collective-permute-start.12 = (bf16[256,1024]{1,0:T(8,128)(2,1)S(1)}, bf16[256,1024]{1,0:T(8,128)(2,1)S(1)}, u32[]{:S(2)}, u32[]{:S(2)}) collective-permute-start(bf16[256,1024]{1,0:T(8,128)(2,1)S(1)} %pad_maximum_fusion.refs_0_), channel_id=1, source_target_pairs={{0,8},{8,0},{1,9},{9,1},{2,10},{10,2},{3,11},{11,3},{4,12},{12,4},... | collective-permute-start | bytes 1572872 | tf_op jit(solution)/shard_map/ppermute | solution.py:210
  19.7 1.6 %collective-permute-start.4 = (bf16[96,1024]{1,0:T(8,128)(2,1)S(1)}, bf16[96,1024]{1,0:T(8,128)(2,1)S(1)}, u32[]{:S(2)}, u32[]{:S(2)}) collective-permute-start(bf16[96,1024]{1,0:T(8,128)(2,1)S(1)} %collective-permute-done.3), channel_id=1, source_target_pairs={{0,4},{2,6},{4,0},{6,2},{1,5},{3,7},{5,1},{7,3},{8,12},{10,14},{12... | collective-permute-start | bytes 589832 | tf_op jit(solution)/shard_map/ppermute | solution.py:215
  21.3 1.0 %collective-permute-start.5 = (bf16[96,1024]{1,0:T(8,128)(2,1)S(1)}, bf16[96,1024]{1,0:T(8,128)(2,1)S(1)}, u32[]{:S(2)}, u32[]{:S(2)}) collective-permute-start(bf16[96,1024]{1,0:T(8,128)(2,1)S(1)} %collective-permute-done.3), channel_id=1, source_target_pairs={{0,2},{2,4},{4,6},{6,0},{1,3},{3,5},{5,7},{7,1},{8,10},{10,12},{12... | collective-permute-start | bytes 589832 | tf_op jit(solution)/shard_map/ppermute | solution.py:215
  22.4 0.5 collective-permute-done.2
  23.0 0.5 collective-permute-start.13
  23.5 4.3 %collective-permute-done.4 = bf16[96,1024]{1,0:T(8,128)(2,1)S(1)} collective-permute-done((bf16[96,1024]{1,0:T(8,128)(2,1)S(1)}, bf16[96,1024]{1,0:T(8,128)(2,1)S(1)}, u32[]{:S(2)}, u32[]{:S(2)}) %collective-permute-start.4) | collective-permute-done | bytes 196640 | tf_op jit(solution)/shard_map/ppermute | solution.py:215
  27.8 0.9 %collective-permute-start.6 = (bf16[96,1024]{1,0:T(8,128)(2,1)S(1)}, bf16[96,1024]{1,0:T(8,128)(2,1)S(1)}, u32[]{:S(2)}, u32[]{:S(2)}) collective-permute-start(bf16[96,1024]{1,0:T(8,128)(2,1)S(1)} %collective-permute-done.3), channel_id=1, source_target_pairs={{0,6},{2,0},{4,2},{6,4},{1,7},{3,1},{5,3},{7,5},{8,14},{10,8},{12,... | collective-permute-start | bytes 589832 | tf_op jit(solution)/shard_map/ppermute | solution.py:215
  28.7 0.9 %collective-permute-done.5 = bf16[96,1024]{1,0:T(8,128)(2,1)S(1)} collective-permute-done((bf16[96,1024]{1,0:T(8,128)(2,1)S(1)}, bf16[96,1024]{1,0:T(8,128)(2,1)S(1)}, u32[]{:S(2)}, u32[]{:S(2)}) %collective-permute-start.5) | collective-permute-done | bytes 196640 | tf_op jit(solution)/shard_map/ppermute | solution.py:215
  29.7 1.5 %collective-permute-done.12.refs_1_ = bf16[256,1024]{1,0:T(8,128)(2,1)S(1)} collective-permute-done((bf16[256,1024]{1,0:T(8,128)(2,1)S(1)}, bf16[256,1024]{1,0:T(8,128)(2,1)S(1)}, u32[]{:S(2)}, u32[]{:S(2)}) %collective-permute-start.12) | collective-permute-done | bytes 524320 | tf_op jit(solution)/shard_map/ppermute | solution.py:210
  31.2 2.3 %collective-permute-done.6 = bf16[96,1024]{1,0:T(8,128)(2,1)S(1)} collective-permute-done((bf16[96,1024]{1,0:T(8,128)(2,1)S(1)}, bf16[96,1024]{1,0:T(8,128)(2,1)S(1)}, u32[]{:S(2)}, u32[]{:S(2)}) %collective-permute-start.6) | collective-permute-done | bytes 196640 | tf_op jit(solution)/shard_map/ppermute | solution.py:215
  33.5 0.3 collective-permute-start.8
  35.1 2.7 %evaluate.2 = (bf16[256,512]{1,0:T(8,128)(2,1)S(1)}, bf16[256,512]{1,0:T(8,128)(2,1)S(1)}, bf16[256,4096]{1,0:T(8,128)(2,1)S(1)}) custom-call(bf16[4096,256]{1,0:T(8,128)(2,1)S(1)} %copy-done, s32[3,1,1024]{2,1,0:T(1,128)S(1)} %bitcast.7, f32[3,1,1024]{2,1,0:T(1,128)S(1)} %bitcast.10), custom_call_target="tpu_custom_call" | custom-call | flops 2147483648 | bytes 2097152 | tf_op jit(solution)/shard_map/evaluate/pallas_call | solution.py:242
  37.8 2.6 %evaluate.3 = (bf16[256,512]{1,0:T(8,128)(2,1)S(1)}, bf16[256,512]{1,0:T(8,128)(2,1)S(1)}) custom-call(bf16[256,4096]{1,0:T(8,128)(2,1)S(1)} %get-tuple-element.14.coef_ref, s32[3,1,1024]{2,1,0:T(1,128)S(1)} %bitcast.8, f32[3,1,1024]{2,1,0:T(1,128)S(1)} %bitcast.11), custom_call_target="tpu_custom_call" | custom-call | flops 2147483648 | bytes 2097152 | tf_op jit(solution)/shard_map/evaluate/pallas_call | solution.py:242
  40.5 1.7 %ratio.1.rows_ref = bf16[1536,256]{1,0:T(8,128)(2,1)S(1)} custom-call(bf16[256,1024]{1,0:T(8,128)(2,1)S(1)} %pad_maximum_fusion.refs_0_, bf16[256,1024]{1,0:T(8,128)(2,1)S(1)} %collective-permute-done.12.refs_1_, bf16[256,1024]{1,0:T(8,128)(2,1)S(1)} %collective-permute-done.13.refs_2_, bf16[256,1024]{1,0:T(8,128)(2,1)S(1)} %collective-permute-done.14.refs_3_, ...), custom_call_target="tpu_custom_call" | custom-call | flops 1610612736 | bytes 2097152 | tf_op jit(solution)/shard_map/ratio/pallas_call | solution.py:299
  42.2 1.9 %finish.1 = bf16[1024,256]{1,0:T(8,128)(2,1)S(1)} custom-call(f32[2,128]{1,0:T(2,128)S(1)} %scale.1.scale_ref, bf16[480,1024]{1,0:T(8,128)(2,1)S(1)} %constant_dynamic-update-slice_fusion.near_own_ref, bf16[288,1024]{1,0:T(8,128)(2,1)S(1)} %constant_dynamic-update-slice_fusion.5.far_own_ref, bf16[480,1024]{1,0:T(8,128)(2,1)S(1)} %collective-permute-done.7.near_other_ref, ...), custom_call_target="tpu_custom_call" | custom-call | flops 1610612736 | bytes 2097152 | tf_op jit(solution)/shard_map/finish/pallas_call | solution.py:318
  44.2 16.3 %all_to_all.5 = bf16[8,128,256]{2,1,0:T(8,128)(2,1)S(1)} all-to-all(bf16[8,128,256]{2,1,0:T(8,128)(2,1)S(1)} %bitcast.5), channel_id=1, replica_groups=mesh['y'=4,'xl'=2,'xh'=2,'z'=4,'core'=2] {'y','xl'}, dimensions={0} | all-to-all | bytes 1048576 | tf_op jit(solution)/shard_map/all_to_all | solution.py:330
  60.5 0.7 %convert_reduce_fusion = f32[128,256]{1,0:T(8,128)} fusion(bf16[8,128,256]{2,1,0:T(8,128)(2,1)S(1)} %all_to_all.5), kind=kLoop, calls=%fused_computation | loop fusion | flops 491520 | bytes 655360 | tf_op jit(solution)/shard_map/reduce_sum | solution.py:331
  (34 shorter events, 0.5 us)
Async XLA Ops:
  0.0 6.1 %copy-start = (bf16[4096,256]{1,0:T(8,128)(2,1)S(1)}, bf16[4096,256]{1,0:T(8,128)(2,1)}, u32[]{:S(2)}) copy-start(bf16[4096,256]{1,0:T(8,128)(2,1)} %coef_ref.3) | copy-start | bytes 6291460
  0.0 6.1 %copy-start.1 = (s32[1,3,1024]{2,0,1:T(1,128)S(1)}, s32[1,3,1024]{2,0,1:T(1,128)}, u32[]{:S(2)}) copy-start(s32[1,3,1024]{2,0,1:T(1,128)} %param.9) | copy-start | bytes 36868
  0.0 6.1 %copy-start.2 = (f32[1,3,1024]{2,0,1:T(1,128)S(1)}, f32[1,3,1024]{2,0,1:T(1,128)}, u32[]{:S(2)}) copy-start(f32[1,3,1024]{2,0,1:T(1,128)} %param.10) | copy-start | bytes 36868
  0.0 6.1 %copy-start.3 = (s32[1024]{0:T(1024)S(1)}, s32[1024]{0:T(1024)}, u32[]{:S(2)}) copy-start(s32[1024]{0:T(1024)} %param.13) | copy-start | bytes 12292
  0.0 14.2 %collective-permute-start.10 = (bf16[64,1024]{1,0:T(8,128)(2,1)}, bf16[64,1024]{1,0:T(8,128)(2,1)S(1)}, u32[]{:S(2)}, u32[]{:S(2)}) collective-permute-start(bf16[64,1024]{1,0:T(8,128)(2,1)} %bitcast.13), channel_id=1, source_target_pairs={{0,2},{2,4},{4,6},{6,0},{1,3},{3,5},{5,7},{7,1},{8,10},{10,12},{12... | collective-permute-start | bytes 393224 | tf_op jit(solution)/shard_map/ppermute | solution.py:215
  2.1 12.3 %collective-permute-start.11 = (bf16[64,1024]{1,0:T(8,128)(2,1)}, bf16[64,1024]{1,0:T(8,128)(2,1)S(1)}, u32[]{:S(2)}, u32[]{:S(2)}) collective-permute-start(bf16[64,1024]{1,0:T(8,128)(2,1)} %bitcast.14), channel_id=1, source_target_pairs={{0,6},{2,0},{4,2},{6,4},{1,7},{3,1},{5,3},{7,5},{8,14},{10,8},{12,... | collective-permute-start | bytes 393224 | tf_op jit(solution)/shard_map/ppermute | solution.py:215
  4.3 13.7 %collective-permute-start.9 = (bf16[64,1024]{1,0:T(8,128)(2,1)}, bf16[64,1024]{1,0:T(8,128)(2,1)S(1)}, u32[]{:S(2)}, u32[]{:S(2)}) collective-permute-start(bf16[64,1024]{1,0:T(8,128)(2,1)} %bitcast.15), channel_id=1, source_target_pairs={{0,4},{2,6},{4,0},{6,2},{1,5},{3,7},{5,1},{7,3},{8,12},{10,14},{12... | collective-permute-start | bytes 393224 | tf_op jit(solution)/shard_map/ppermute | solution.py:215
  6.1 11.9 %copy-start.4 = (bf16[1,64,1024]{2,1,0:T(8,128)(2,1)S(1)}, bf16[1,64,1024]{2,1,0:T(8,128)(2,1)}, u32[]{:S(2)}) copy-start(bf16[1,64,1024]{2,1,0:T(8,128)(2,1)} %param.8) | copy-start | bytes 393220
  9.4 11.9 %collective-permute-start = (bf16[96,1024]{1,0:T(8,128)(2,1)S(1)}, bf16[96,1024]{1,0:T(8,128)(2,1)S(1)}, u32[]{:S(2)}, u32[]{:S(2)}) collective-permute-start(bf16[96,1024]{1,0:T(8,128)(2,1)S(1)} %get-tuple-element.12), channel_id=1, source_target_pairs={{0,4},{2,6},{4,0},{6,2},{1,5},{3,7},{5,1},{7,3},{8,12},{10,14},{12... | collective-permute-start | bytes 589832 | tf_op jit(solution)/shard_map/ppermute | solution.py:215
  11.2 8.5 %collective-permute-start.3 = (bf16[96,1024]{1,0:T(8,128)(2,1)S(1)}, bf16[96,1024]{1,0:T(8,128)(2,1)S(1)}, u32[]{:S(2)}, u32[]{:S(2)}) collective-permute-start(bf16[96,1024]{1,0:T(8,128)(2,1)S(1)} %get-tuple-element.12), channel_id=1, source_target_pairs={{0,8},{8,0},{1,9},{9,1},{2,10},{10,2},{3,11},{11,3},{4,12},{12,4},... | collective-permute-start | bytes 589832 | tf_op jit(solution)/shard_map/ppermute | solution.py:210
  14.3 8.1 %collective-permute-start.1 = (bf16[96,1024]{1,0:T(8,128)(2,1)S(1)}, bf16[96,1024]{1,0:T(8,128)(2,1)S(1)}, u32[]{:S(2)}, u32[]{:S(2)}) collective-permute-start(bf16[96,1024]{1,0:T(8,128)(2,1)S(1)} %get-tuple-element.12), channel_id=1, source_target_pairs={{0,2},{2,4},{4,6},{6,0},{1,3},{3,5},{5,7},{7,1},{8,10},{10,12},{12... | collective-permute-start | bytes 589832 | tf_op jit(solution)/shard_map/ppermute | solution.py:215
  14.4 8.5 %collective-permute-start.2 = (bf16[96,1024]{1,0:T(8,128)(2,1)S(1)}, bf16[96,1024]{1,0:T(8,128)(2,1)S(1)}, u32[]{:S(2)}, u32[]{:S(2)}) collective-permute-start(bf16[96,1024]{1,0:T(8,128)(2,1)S(1)} %get-tuple-element.12), channel_id=1, source_target_pairs={{0,6},{2,0},{4,2},{6,4},{1,7},{3,1},{5,3},{7,5},{8,14},{10,8},{12,... | collective-permute-start | bytes 589832 | tf_op jit(solution)/shard_map/ppermute | solution.py:215
  18.0 13.1 %collective-permute-start.12 = (bf16[256,1024]{1,0:T(8,128)(2,1)S(1)}, bf16[256,1024]{1,0:T(8,128)(2,1)S(1)}, u32[]{:S(2)}, u32[]{:S(2)}) collective-permute-start(bf16[256,1024]{1,0:T(8,128)(2,1)S(1)} %pad_maximum_fusion.refs_0_), channel_id=1, source_target_pairs={{0,8},{8,0},{1,9},{9,1},{2,10},{10,2},{3,11},{11,3},{4,12},{12,4},... | collective-permute-start | bytes 1572872 | tf_op jit(solution)/shard_map/ppermute | solution.py:210
  19.7 8.1 %collective-permute-start.4 = (bf16[96,1024]{1,0:T(8,128)(2,1)S(1)}, bf16[96,1024]{1,0:T(8,128)(2,1)S(1)}, u32[]{:S(2)}, u32[]{:S(2)}) collective-permute-start(bf16[96,1024]{1,0:T(8,128)(2,1)S(1)} %collective-permute-done.3), channel_id=1, source_target_pairs={{0,4},{2,6},{4,0},{6,2},{1,5},{3,7},{5,1},{7,3},{8,12},{10,14},{12... | collective-permute-start | bytes 589832 | tf_op jit(solution)/shard_map/ppermute | solution.py:215
  21.3 8.3 %collective-permute-start.5 = (bf16[96,1024]{1,0:T(8,128)(2,1)S(1)}, bf16[96,1024]{1,0:T(8,128)(2,1)S(1)}, u32[]{:S(2)}, u32[]{:S(2)}) collective-permute-start(bf16[96,1024]{1,0:T(8,128)(2,1)S(1)} %collective-permute-done.3), channel_id=1, source_target_pairs={{0,2},{2,4},{4,6},{6,0},{1,3},{3,5},{5,7},{7,1},{8,10},{10,12},{12... | collective-permute-start | bytes 589832 | tf_op jit(solution)/shard_map/ppermute | solution.py:215
  22.9 19.3 %collective-permute-start.7 = (bf16[480,1024]{1,0:T(8,128)(2,1)S(1)}, bf16[480,1024]{1,0:T(8,128)(2,1)S(1)}, u32[]{:S(2)}, u32[]{:S(2)}) collective-permute-start(bf16[480,1024]{1,0:T(8,128)(2,1)S(1)} %constant_dynamic-update-slice_fusion.near_own_ref), channel_id=1, source_target_pairs={{0,1},{1,0},{2,3},{3,2},{4,5},{5,4},{6,7},{7,6},{8,9},{9,8},{10,11... | collective-permute-start | bytes 2949128 | tf_op jit(solution)/shard_map/ppermute | solution.py:219
  23.0 17.4 %collective-permute-start.13 = (bf16[256,1024]{1,0:T(8,128)(2,1)S(1)}, bf16[256,1024]{1,0:T(8,128)(2,1)S(1)}, u32[]{:S(2)}, u32[]{:S(2)}) collective-permute-start(bf16[256,1024]{1,0:T(8,128)(2,1)S(1)} %pad_maximum_fusion.refs_0_), channel_id=1, source_target_pairs={{0,1},{1,0},{2,3},{3,2},{4,5},{5,4},{6,7},{7,6},{8,9},{9,8},{10,11... | collective-permute-start | bytes 1572872 | tf_op jit(solution)/shard_map/ppermute | solution.py:219
  27.8 5.7 %collective-permute-start.6 = (bf16[96,1024]{1,0:T(8,128)(2,1)S(1)}, bf16[96,1024]{1,0:T(8,128)(2,1)S(1)}, u32[]{:S(2)}, u32[]{:S(2)}) collective-permute-start(bf16[96,1024]{1,0:T(8,128)(2,1)S(1)} %collective-permute-done.3), channel_id=1, source_target_pairs={{0,6},{2,0},{4,2},{6,4},{1,7},{3,1},{5,3},{7,5},{8,14},{10,8},{12,... | collective-permute-start | bytes 589832 | tf_op jit(solution)/shard_map/ppermute | solution.py:215
  31.2 9.3 %collective-permute-start.14 = (bf16[256,1024]{1,0:T(8,128)(2,1)S(1)}, bf16[256,1024]{1,0:T(8,128)(2,1)S(1)}, u32[]{:S(2)}, u32[]{:S(2)}) collective-permute-start(bf16[256,1024]{1,0:T(8,128)(2,1)S(1)} %collective-permute-done.12.refs_1_), channel_id=1, source_target_pairs={{0,1},{1,0},{2,3},{3,2},{4,5},{5,4},{6,7},{7,6},{8,9},{9,8},{10,11... | collective-permute-start | bytes 1572872 | tf_op jit(solution)/shard_map/ppermute | solution.py:219
  33.5 8.7 %collective-permute-start.8 = (bf16[288,1024]{1,0:T(8,128)(2,1)S(1)}, bf16[288,1024]{1,0:T(8,128)(2,1)S(1)}, u32[]{:S(2)}, u32[]{:S(2)}) collective-permute-start(bf16[288,1024]{1,0:T(8,128)(2,1)S(1)} %constant_dynamic-update-slice_fusion.5.far_own_ref), channel_id=1, source_target_pairs={{0,1},{1,0},{2,3},{3,2},{4,5},{5,4},{6,7},{7,6},{8,9},{9,8},{10,11... | collective-permute-start | bytes 1769480 | tf_op jit(solution)/shard_map/ppermute | solution.py:219

commit v8 on v7

--- a/solution.py
+++ b/solution.py
@@ -100,20 +100,27 @@
     slot_ref[...] = slot
     chosen = mm_nt(picker, coef_ref[...]).astype(BF16)
 
-    def build(t):
-        vx, cx, value, curve = weight_tables(cell_ref, frac_ref, slice(t * TILE, (t + 1) * TILE))
+    def build(start, w_ref):
+        vx, cx, value, curve = weight_tables(cell_ref, frac_ref, pl.ds(start, TILE))
         value = value.astype(BF16).reshape(GRID, GRID, TILE)
         curve = curve.astype(BF16).reshape(GRID, GRID, TILE)
         for g in range(GRID):
             x_value = jnp.broadcast_to(vx[g:g + 1, :], (GRID, TILE)).astype(BF16)[None]
             x_curve = jnp.broadcast_to(cx[g:g + 1, :], (GRID, TILE)).astype(BF16)[None]
-            w_refs[t % 2][g * PLANE:(g + 1) * PLANE, :] = (x_curve * value + x_value * curve).reshape(PLANE, TILE)
-
-    build(0)
-    for t in range(electrons // TILE):
-        if (t + 1) * TILE < electrons:
-            build(t + 1)
-        lapt_ref[:, t * TILE:(t + 1) * TILE] = mm(chosen, w_refs[t % 2][...]).astype(BF16)
+            w_ref[g * PLANE:(g + 1) * PLANE, :] = (x_curve * value + x_value * curve).reshape(PLANE, TILE)
+
+    chosen_ref, *w_refs = w_refs
+    chosen_ref[...] = chosen
+
+    def step(i, carry):
+        starts = [pl.multiple_of((i * len(w_refs) + k) * TILE, TILE) for k in range(len(w_refs))]
+        for start, w_ref in zip(starts, w_refs):
+            build(start, w_ref)
+        for start, w_ref in zip(starts, w_refs):
+            lapt_ref[:, pl.ds(start, TILE)] = mm(chosen_ref[...], w_ref[...]).astype(BF16)
+        return carry
+
+    lax.fori_loop(0, electrons // (TILE * len(w_refs)), step, 0)
 
 
 def eval_kernel(coef_ref, cell_ref, frac_ref, val_ref, lap_ref, *w_refs, first):
@@ -275,7 +282,7 @@
         out_shape=[out((slots, electrons), BF16), out((1, electrons), jnp.int32)],
         in_specs=[VMEM] * 5,
         out_specs=[VMEM] * 2,
-        scratch_shapes=[pltpu.VMEM((cells, TILE), BF16)] * 2,
+        scratch_shapes=[pltpu.VMEM((slots, cells), BF16)] + [pltpu.VMEM((cells, TILE), BF16)] * 2,
         compiler_params=params(32),
         cost_estimate=cost(slots * cells * electrons),
         name="early",

time: 61.6 us -> 61.2 us (level)
  blocking collectives: 16.3 us -> 15.5 us
    ppermute x2, starting transfers between devices: 4.7 us -> 3.61 us  [ring_swap(): return lax.ppermute(piece, 'xh', [(0, 1), (1, 0)])]
    ppermute x9, starting transfers between devices: 15 us -> 15.8 us  [ring_pass(): lax.ppermute(piece, 'z', [(i, (i + shift) % count) for i in range(count)])]
    all_to_all x1, blocking collectives: 16.3 us -> 15.5 us  [gradient(): lax.all_to_all(partial.reshape(count, electrons // count, width), walkers...]
  transfers between devices with their start and end apart: 15 -> 15, of which waited for: 6 -> 6; matrix products, arithmetic and copies ran while one was open for 0% -> 0% of each run, Pallas kernels for 17% -> 18%
where the time goes in v8:
time: 61.2 us; the launch traced here: 60.8 us
  starting transfers between devices  20.3 us (33%)
  blocking collectives  15.5 us (25%)
  Pallas kernels  12.7 us (21%)
  waiting for transfers between devices  9.92 us (16%)
  between operations  1.49 us (2%)
  other arithmetic  0.76 us (1%)
    ppermute x9, starting transfers between devices, ring_pass(): lax.ppermute(piece, 'z', [(i, (i + shift) % count) for i in range(count)])  15.8 us
    all_to_all x1, blocking collectives, gradient(): lax.all_to_all(partial.reshape(count, electrons // count, width), walkers...  15.5 us
    ppermute x9, waiting for transfers between devices, ring_pass(): lax.ppermute(piece, 'z', [(i, (i + shift) % count) for i in range(count)])  7.95 us
    pallas_call x2, Pallas kernels, evaluate(): pl.pallas_call(functools.partial(eval_kernel, first=h * part), out_shape=...  5.31 us
    pallas_call x1, Pallas kernels, gradient(): pl.pallas_call(functools.partial(early_kernel, shards=shards), out_shape=...  3.68 us
    ppermute x2, starting transfers between devices, ring_swap(): return lax.ppermute(piece, 'xh', [(0, 1), (1, 0)])  3.61 us
    ppermute x2, waiting for transfers between devices, ring_swap(): return lax.ppermute(piece, 'xh', [(0, 1), (1, 0)])  1.96 us
    pallas_call x1, Pallas kernels, gradient(): pl.pallas_call(functools.partial(finish_kernel, z_count=z_count, size=row...  1.93 us
  transfers between devices with their start and end apart: 15, of which 6 were waited for; matrix products, arithmetic and copies ran while one was open for 0% of the time, Pallas kernels for 18%

profile of v8, /device:TPU:0, one launch (start us, length us, event | category | flops | bytes accessed | tf_op | source)
XLA Modules:
  0.0 60.8 jit_solution(8226915263805326242)
XLA Ops:
  0.0 2.1 %collective-permute-start.10 = (bf16[64,1024]{1,0:T(8,128)(2,1)}, bf16[64,1024]{1,0:T(8,128)(2,1)S(1)}, u32[]{:S(2)}, u32[]{:S(2)}) collective-permute-start(bf16[64,1024]{1,0:T(8,128)(2,1)} %bitcast.13), channel_id=1, source_target_pairs={{0,2},{2,4},{4,6},{6,0},{1,3},{3,5},{5,7},{7,1},{8,10},{10,12},{12... | collective-permute-start | bytes 393224 | tf_op jit(solution)/shard_map/ppermute | solution.py:222
  2.1 2.2 %collective-permute-start.11 = (bf16[64,1024]{1,0:T(8,128)(2,1)}, bf16[64,1024]{1,0:T(8,128)(2,1)S(1)}, u32[]{:S(2)}, u32[]{:S(2)}) collective-permute-start(bf16[64,1024]{1,0:T(8,128)(2,1)} %bitcast.14), channel_id=1, source_target_pairs={{0,6},{2,0},{4,2},{6,4},{1,7},{3,1},{5,3},{7,5},{8,14},{10,8},{12,... | collective-permute-start | bytes 393224 | tf_op jit(solution)/shard_map/ppermute | solution.py:222
  4.3 1.8 %collective-permute-start.9 = (bf16[64,1024]{1,0:T(8,128)(2,1)}, bf16[64,1024]{1,0:T(8,128)(2,1)S(1)}, u32[]{:S(2)}, u32[]{:S(2)}) collective-permute-start(bf16[64,1024]{1,0:T(8,128)(2,1)} %bitcast.15), channel_id=1, source_target_pairs={{0,4},{2,6},{4,0},{6,2},{1,5},{3,7},{5,1},{7,3},{8,12},{10,14},{12... | collective-permute-start | bytes 393224 | tf_op jit(solution)/shard_map/ppermute | solution.py:222
  6.1 3.7 %early.1 = (bf16[96,1024]{1,0:T(8,128)(2,1)S(1)}, s32[1,1024]{1,0:T(1,128)S(1)}) custom-call(f32[8,128]{1,0:T(8,128)S(1)} %first.1.flag_ref, bf16[4096,256]{1,0:T(8,128)(2,1)S(1)} %copy-done, s32[3,1,1024]{2,1,0:T(1,128)S(1)} %bitcast.6, f32[3,1,1024]{2,1,0:T(1,128)S(1)} %bitcast.9, s32[1,1024]{1,0:T(1,128)S(1)} %bitcast.12), custom_call_target="tpu_custom_call" | custom-call | flops 805306368 | bytes 2097152 | tf_op jit(solution)/shard_map/early/pallas_call | solution.py:280
  9.8 1.8 %collective-permute-start = (bf16[96,1024]{1,0:T(8,128)(2,1)S(1)}, bf16[96,1024]{1,0:T(8,128)(2,1)S(1)}, u32[]{:S(2)}, u32[]{:S(2)}) collective-permute-start(bf16[96,1024]{1,0:T(8,128)(2,1)S(1)} %get-tuple-element.12), channel_id=1, source_target_pairs={{0,4},{2,6},{4,0},{6,2},{1,5},{3,7},{5,1},{7,3},{8,12},{10,14},{12... | collective-permute-start | bytes 589832 | tf_op jit(solution)/shard_map/ppermute | solution.py:222
  11.6 3.0 %collective-permute-start.3 = (bf16[96,1024]{1,0:T(8,128)(2,1)S(1)}, bf16[96,1024]{1,0:T(8,128)(2,1)S(1)}, u32[]{:S(2)}, u32[]{:S(2)}) collective-permute-start(bf16[96,1024]{1,0:T(8,128)(2,1)S(1)} %get-tuple-element.12), channel_id=1, source_target_pairs={{0,8},{8,0},{1,9},{9,1},{2,10},{10,2},{3,11},{11,3},{4,12},{12,4},... | collective-permute-start | bytes 589832 | tf_op jit(solution)/shard_map/ppermute | solution.py:217
  14.8 3.2 %collective-permute-start.2 = (bf16[96,1024]{1,0:T(8,128)(2,1)S(1)}, bf16[96,1024]{1,0:T(8,128)(2,1)S(1)}, u32[]{:S(2)}, u32[]{:S(2)}) collective-permute-start(bf16[96,1024]{1,0:T(8,128)(2,1)S(1)} %get-tuple-element.12), channel_id=1, source_target_pairs={{0,6},{2,0},{4,2},{6,4},{1,7},{3,1},{5,3},{7,5},{8,14},{10,8},{12,... | collective-permute-start | bytes 589832 | tf_op jit(solution)/shard_map/ppermute | solution.py:222
  18.1 0.6 collective-permute-start.12
  18.6 0.4 collective-permute-done.3
  19.1 2.7 %collective-permute-start.4 = (bf16[96,1024]{1,0:T(8,128)(2,1)S(1)}, bf16[96,1024]{1,0:T(8,128)(2,1)S(1)}, u32[]{:S(2)}, u32[]{:S(2)}) collective-permute-start(bf16[96,1024]{1,0:T(8,128)(2,1)S(1)} %collective-permute-done.3), channel_id=1, source_target_pairs={{0,4},{2,6},{4,0},{6,2},{1,5},{3,7},{5,1},{7,3},{8,12},{10,14},{12... | collective-permute-start | bytes 589832 | tf_op jit(solution)/shard_map/ppermute | solution.py:222
  21.8 1.0 %collective-permute-start.5 = (bf16[96,1024]{1,0:T(8,128)(2,1)S(1)}, bf16[96,1024]{1,0:T(8,128)(2,1)S(1)}, u32[]{:S(2)}, u32[]{:S(2)}) collective-permute-start(bf16[96,1024]{1,0:T(8,128)(2,1)S(1)} %collective-permute-done.3), channel_id=1, source_target_pairs={{0,2},{2,4},{4,6},{6,0},{1,3},{3,5},{5,7},{7,1},{8,10},{10,12},{12... | collective-permute-start | bytes 589832 | tf_op jit(solution)/shard_map/ppermute | solution.py:222
  22.8 0.3 collective-permute-done.2
  23.3 0.5 collective-permute-start.13
  23.8 4.4 %collective-permute-done.4 = bf16[96,1024]{1,0:T(8,128)(2,1)S(1)} collective-permute-done((bf16[96,1024]{1,0:T(8,128)(2,1)S(1)}, bf16[96,1024]{1,0:T(8,128)(2,1)S(1)}, u32[]{:S(2)}, u32[]{:S(2)}) %collective-permute-start.4) | collective-permute-done | bytes 196640 | tf_op jit(solution)/shard_map/ppermute | solution.py:222
  28.2 0.9 %collective-permute-start.6 = (bf16[96,1024]{1,0:T(8,128)(2,1)S(1)}, bf16[96,1024]{1,0:T(8,128)(2,1)S(1)}, u32[]{:S(2)}, u32[]{:S(2)}) collective-permute-start(bf16[96,1024]{1,0:T(8,128)(2,1)S(1)} %collective-permute-done.3), channel_id=1, source_target_pairs={{0,6},{2,0},{4,2},{6,4},{1,7},{3,1},{5,3},{7,5},{8,14},{10,8},{12,... | collective-permute-start | bytes 589832 | tf_op jit(solution)/shard_map/ppermute | solution.py:222
  29.1 1.0 %collective-permute-done.5 = bf16[96,1024]{1,0:T(8,128)(2,1)S(1)} collective-permute-done((bf16[96,1024]{1,0:T(8,128)(2,1)S(1)}, bf16[96,1024]{1,0:T(8,128)(2,1)S(1)}, u32[]{:S(2)}, u32[]{:S(2)}) %collective-permute-start.5) | collective-permute-done | bytes 196640 | tf_op jit(solution)/shard_map/ppermute | solution.py:222
  30.1 1.5 %collective-permute-done.12.refs_1_ = bf16[256,1024]{1,0:T(8,128)(2,1)S(1)} collective-permute-done((bf16[256,1024]{1,0:T(8,128)(2,1)S(1)}, bf16[256,1024]{1,0:T(8,128)(2,1)S(1)}, u32[]{:S(2)}, u32[]{:S(2)}) %collective-permute-start.12) | collective-permute-done | bytes 524320 | tf_op jit(solution)/shard_map/ppermute | solution.py:217
  31.6 2.2 %collective-permute-done.6 = bf16[96,1024]{1,0:T(8,128)(2,1)S(1)} collective-permute-done((bf16[96,1024]{1,0:T(8,128)(2,1)S(1)}, bf16[96,1024]{1,0:T(8,128)(2,1)S(1)}, u32[]{:S(2)}, u32[]{:S(2)}) %collective-permute-start.6) | collective-permute-done | bytes 196640 | tf_op jit(solution)/shard_map/ppermute | solution.py:222
  35.5 2.7 %evaluate.2 = (bf16[256,512]{1,0:T(8,128)(2,1)S(1)}, bf16[256,512]{1,0:T(8,128)(2,1)S(1)}, bf16[256,4096]{1,0:T(8,128)(2,1)S(1)}) custom-call(bf16[4096,256]{1,0:T(8,128)(2,1)S(1)} %copy-done, s32[3,1,1024]{2,1,0:T(1,128)S(1)} %bitcast.7, f32[3,1,1024]{2,1,0:T(1,128)S(1)} %bitcast.10), custom_call_target="tpu_custom_call" | custom-call | flops 2147483648 | bytes 2097152 | tf_op jit(solution)/shard_map/evaluate/pallas_call | solution.py:249
  38.1 2.6 %evaluate.3 = (bf16[256,512]{1,0:T(8,128)(2,1)S(1)}, bf16[256,512]{1,0:T(8,128)(2,1)S(1)}) custom-call(bf16[256,4096]{1,0:T(8,128)(2,1)S(1)} %get-tuple-element.14.coef_ref, s32[3,1,1024]{2,1,0:T(1,128)S(1)} %bitcast.8, f32[3,1,1024]{2,1,0:T(1,128)S(1)} %bitcast.11), custom_call_target="tpu_custom_call" | custom-call | flops 2147483648 | bytes 2097152 | tf_op jit(solution)/shard_map/evaluate/pallas_call | solution.py:249
  40.8 1.7 %ratio.1.rows_ref = bf16[1536,256]{1,0:T(8,128)(2,1)S(1)} custom-call(bf16[256,1024]{1,0:T(8,128)(2,1)S(1)} %pad_maximum_fusion.refs_0_, bf16[256,1024]{1,0:T(8,128)(2,1)S(1)} %collective-permute-done.12.refs_1_, bf16[256,1024]{1,0:T(8,128)(2,1)S(1)} %collective-permute-done.13.refs_2_, bf16[256,1024]{1,0:T(8,128)(2,1)S(1)} %collective-permute-done.14.refs_3_, ...), custom_call_target="tpu_custom_call" | custom-call | flops 1610612736 | bytes 2097152 | tf_op jit(solution)/shard_map/ratio/pallas_call | solution.py:306
  42.6 1.9 %finish.1 = bf16[1024,256]{1,0:T(8,128)(2,1)S(1)} custom-call(f32[2,128]{1,0:T(2,128)S(1)} %scale.1.scale_ref, bf16[480,1024]{1,0:T(8,128)(2,1)S(1)} %constant_dynamic-update-slice_fusion.near_own_ref, bf16[288,1024]{1,0:T(8,128)(2,1)S(1)} %constant_dynamic-update-slice_fusion.5.far_own_ref, bf16[480,1024]{1,0:T(8,128)(2,1)S(1)} %collective-permute-done.7.near_other_ref, ...), custom_call_target="tpu_custom_call" | custom-call | flops 1610612736 | bytes 2097152 | tf_op jit(solution)/shard_map/finish/pallas_call | solution.py:325
  44.5 15.5 %all_to_all.5 = bf16[8,128,256]{2,1,0:T(8,128)(2,1)S(1)} all-to-all(bf16[8,128,256]{2,1,0:T(8,128)(2,1)S(1)} %bitcast.5), channel_id=1, replica_groups=mesh['y'=4,'xl'=2,'xh'=2,'z'=4,'core'=2] {'y','xl'}, dimensions={0} | all-to-all | bytes 1048576 | tf_op jit(solution)/shard_map/all_to_all | solution.py:337
  60.1 0.7 %convert_reduce_fusion = f32[128,256]{1,0:T(8,128)} fusion(bf16[8,128,256]{2,1,0:T(8,128)(2,1)S(1)} %all_to_all.5), kind=kLoop, calls=%fused_computation | loop fusion | flops 491520 | bytes 655360 | tf_op jit(solution)/shard_map/reduce_sum | solution.py:338
  (34 shorter events, 0.6 us)
Async XLA Ops:
  0.0 6.1 %copy-start = (bf16[4096,256]{1,0:T(8,128)(2,1)S(1)}, bf16[4096,256]{1,0:T(8,128)(2,1)}, u32[]{:S(2)}) copy-start(bf16[4096,256]{1,0:T(8,128)(2,1)} %coef_ref.3) | copy-start | bytes 6291460
  0.0 6.1 %copy-start.1 = (s32[1,3,1024]{2,0,1:T(1,128)S(1)}, s32[1,3,1024]{2,0,1:T(1,128)}, u32[]{:S(2)}) copy-start(s32[1,3,1024]{2,0,1:T(1,128)} %param.9) | copy-start | bytes 36868
  0.0 6.1 %copy-start.2 = (f32[1,3,1024]{2,0,1:T(1,128)S(1)}, f32[1,3,1024]{2,0,1:T(1,128)}, u32[]{:S(2)}) copy-start(f32[1,3,1024]{2,0,1:T(1,128)} %param.10) | copy-start | bytes 36868
  0.0 6.1 %copy-start.3 = (s32[1024]{0:T(1024)S(1)}, s32[1024]{0:T(1024)}, u32[]{:S(2)}) copy-start(s32[1024]{0:T(1024)} %param.13) | copy-start | bytes 12292
  0.0 14.7 %collective-permute-start.10 = (bf16[64,1024]{1,0:T(8,128)(2,1)}, bf16[64,1024]{1,0:T(8,128)(2,1)S(1)}, u32[]{:S(2)}, u32[]{:S(2)}) collective-permute-start(bf16[64,1024]{1,0:T(8,128)(2,1)} %bitcast.13), channel_id=1, source_target_pairs={{0,2},{2,4},{4,6},{6,0},{1,3},{3,5},{5,7},{7,1},{8,10},{10,12},{12... | collective-permute-start | bytes 393224 | tf_op jit(solution)/shard_map/ppermute | solution.py:222
  2.1 12.7 %collective-permute-start.11 = (bf16[64,1024]{1,0:T(8,128)(2,1)}, bf16[64,1024]{1,0:T(8,128)(2,1)S(1)}, u32[]{:S(2)}, u32[]{:S(2)}) collective-permute-start(bf16[64,1024]{1,0:T(8,128)(2,1)} %bitcast.14), channel_id=1, source_target_pairs={{0,6},{2,0},{4,2},{6,4},{1,7},{3,1},{5,3},{7,5},{8,14},{10,8},{12,... | collective-permute-start | bytes 393224 | tf_op jit(solution)/shard_map/ppermute | solution.py:222
  4.3 13.7 %collective-permute-start.9 = (bf16[64,1024]{1,0:T(8,128)(2,1)}, bf16[64,1024]{1,0:T(8,128)(2,1)S(1)}, u32[]{:S(2)}, u32[]{:S(2)}) collective-permute-start(bf16[64,1024]{1,0:T(8,128)(2,1)} %bitcast.15), channel_id=1, source_target_pairs={{0,4},{2,6},{4,0},{6,2},{1,5},{3,7},{5,1},{7,3},{8,12},{10,14},{12... | collective-permute-start | bytes 393224 | tf_op jit(solution)/shard_map/ppermute | solution.py:222
  6.1 11.9 %copy-start.4 = (bf16[1,64,1024]{2,1,0:T(8,128)(2,1)S(1)}, bf16[1,64,1024]{2,1,0:T(8,128)(2,1)}, u32[]{:S(2)}) copy-start(bf16[1,64,1024]{2,1,0:T(8,128)(2,1)} %param.8) | copy-start | bytes 393220
  9.8 11.9 %collective-permute-start = (bf16[96,1024]{1,0:T(8,128)(2,1)S(1)}, bf16[96,1024]{1,0:T(8,128)(2,1)S(1)}, u32[]{:S(2)}, u32[]{:S(2)}) collective-permute-start(bf16[96,1024]{1,0:T(8,128)(2,1)S(1)} %get-tuple-element.12), channel_id=1, source_target_pairs={{0,4},{2,6},{4,0},{6,2},{1,5},{3,7},{5,1},{7,3},{8,12},{10,14},{12... | collective-permute-start | bytes 589832 | tf_op jit(solution)/shard_map/ppermute | solution.py:222
  11.6 7.4 %collective-permute-start.3 = (bf16[96,1024]{1,0:T(8,128)(2,1)S(1)}, bf16[96,1024]{1,0:T(8,128)(2,1)S(1)}, u32[]{:S(2)}, u32[]{:S(2)}) collective-permute-start(bf16[96,1024]{1,0:T(8,128)(2,1)S(1)} %get-tuple-element.12), channel_id=1, source_target_pairs={{0,8},{8,0},{1,9},{9,1},{2,10},{10,2},{3,11},{11,3},{4,12},{12,4},... | collective-permute-start | bytes 589832 | tf_op jit(solution)/shard_map/ppermute | solution.py:217
  14.7 8.1 %collective-permute-start.1 = (bf16[96,1024]{1,0:T(8,128)(2,1)S(1)}, bf16[96,1024]{1,0:T(8,128)(2,1)S(1)}, u32[]{:S(2)}, u32[]{:S(2)}) collective-permute-start(bf16[96,1024]{1,0:T(8,128)(2,1)S(1)} %get-tuple-element.12), channel_id=1, source_target_pairs={{0,2},{2,4},{4,6},{6,0},{1,3},{3,5},{5,7},{7,1},{8,10},{10,12},{12... | collective-permute-start | bytes 589832 | tf_op jit(solution)/shard_map/ppermute | solution.py:222
  14.8 8.3 %collective-permute-start.2 = (bf16[96,1024]{1,0:T(8,128)(2,1)S(1)}, bf16[96,1024]{1,0:T(8,128)(2,1)S(1)}, u32[]{:S(2)}, u32[]{:S(2)}) collective-permute-start(bf16[96,1024]{1,0:T(8,128)(2,1)S(1)} %get-tuple-element.12), channel_id=1, source_target_pairs={{0,6},{2,0},{4,2},{6,4},{1,7},{3,1},{5,3},{7,5},{8,14},{10,8},{12,... | collective-permute-start | bytes 589832 | tf_op jit(solution)/shard_map/ppermute | solution.py:222
  18.1 13.6 %collective-permute-start.12 = (bf16[256,1024]{1,0:T(8,128)(2,1)S(1)}, bf16[256,1024]{1,0:T(8,128)(2,1)S(1)}, u32[]{:S(2)}, u32[]{:S(2)}) collective-permute-start(bf16[256,1024]{1,0:T(8,128)(2,1)S(1)} %pad_maximum_fusion.refs_0_), channel_id=1, source_target_pairs={{0,8},{8,0},{1,9},{9,1},{2,10},{10,2},{3,11},{11,3},{4,12},{12,4},... | collective-permute-start | bytes 1572872 | tf_op jit(solution)/shard_map/ppermute | solution.py:217
  19.1 9.1 %collective-permute-start.4 = (bf16[96,1024]{1,0:T(8,128)(2,1)S(1)}, bf16[96,1024]{1,0:T(8,128)(2,1)S(1)}, u32[]{:S(2)}, u32[]{:S(2)}) collective-permute-start(bf16[96,1024]{1,0:T(8,128)(2,1)S(1)} %collective-permute-done.3), channel_id=1, source_target_pairs={{0,4},{2,6},{4,0},{6,2},{1,5},{3,7},{5,1},{7,3},{8,12},{10,14},{12... | collective-permute-start | bytes 589832 | tf_op jit(solution)/shard_map/ppermute | solution.py:222
  21.8 8.3 %collective-permute-start.5 = (bf16[96,1024]{1,0:T(8,128)(2,1)S(1)}, bf16[96,1024]{1,0:T(8,128)(2,1)S(1)}, u32[]{:S(2)}, u32[]{:S(2)}) collective-permute-start(bf16[96,1024]{1,0:T(8,128)(2,1)S(1)} %collective-permute-done.3), channel_id=1, source_target_pairs={{0,2},{2,4},{4,6},{6,0},{1,3},{3,5},{5,7},{7,1},{8,10},{10,12},{12... | collective-permute-start | bytes 589832 | tf_op jit(solution)/shard_map/ppermute | solution.py:222
  23.2 19.4 %collective-permute-start.7 = (bf16[480,1024]{1,0:T(8,128)(2,1)S(1)}, bf16[480,1024]{1,0:T(8,128)(2,1)S(1)}, u32[]{:S(2)}, u32[]{:S(2)}) collective-permute-start(bf16[480,1024]{1,0:T(8,128)(2,1)S(1)} %constant_dynamic-update-slice_fusion.near_own_ref), channel_id=1, source_target_pairs={{0,1},{1,0},{2,3},{3,2},{4,5},{5,4},{6,7},{7,6},{8,9},{9,8},{10,11... | collective-permute-start | bytes 2949128 | tf_op jit(solution)/shard_map/ppermute | solution.py:226
  23.3 17.5 %collective-permute-start.13 = (bf16[256,1024]{1,0:T(8,128)(2,1)S(1)}, bf16[256,1024]{1,0:T(8,128)(2,1)S(1)}, u32[]{:S(2)}, u32[]{:S(2)}) collective-permute-start(bf16[256,1024]{1,0:T(8,128)(2,1)S(1)} %pad_maximum_fusion.refs_0_), channel_id=1, source_target_pairs={{0,1},{1,0},{2,3},{3,2},{4,5},{5,4},{6,7},{7,6},{8,9},{9,8},{10,11... | collective-permute-start | bytes 1572872 | tf_op jit(solution)/shard_map/ppermute | solution.py:226
  28.2 5.7 %collective-permute-start.6 = (bf16[96,1024]{1,0:T(8,128)(2,1)S(1)}, bf16[96,1024]{1,0:T(8,128)(2,1)S(1)}, u32[]{:S(2)}, u32[]{:S(2)}) collective-permute-start(bf16[96,1024]{1,0:T(8,128)(2,1)S(1)} %collective-permute-done.3), channel_id=1, source_target_pairs={{0,6},{2,0},{4,2},{6,4},{1,7},{3,1},{5,3},{7,5},{8,14},{10,8},{12,... | collective-permute-start | bytes 589832 | tf_op jit(solution)/shard_map/ppermute | solution.py:222
  31.6 9.2 %collective-permute-start.14 = (bf16[256,1024]{1,0:T(8,128)(2,1)S(1)}, bf16[256,1024]{1,0:T(8,128)(2,1)S(1)}, u32[]{:S(2)}, u32[]{:S(2)}) collective-permute-start(bf16[256,1024]{1,0:T(8,128)(2,1)S(1)} %collective-permute-done.12.refs_1_), channel_id=1, source_target_pairs={{0,1},{1,0},{2,3},{3,2},{4,5},{5,4},{6,7},{7,6},{8,9},{9,8},{10,11... | collective-permute-start | bytes 1572872 | tf_op jit(solution)/shard_map/ppermute | solution.py:226
  33.9 8.7 %collective-permute-start.8 = (bf16[288,1024]{1,0:T(8,128)(2,1)S(1)}, bf16[288,1024]{1,0:T(8,128)(2,1)S(1)}, u32[]{:S(2)}, u32[]{:S(2)}) collective-permute-start(bf16[288,1024]{1,0:T(8,128)(2,1)S(1)} %constant_dynamic-update-slice_fusion.5.far_own_ref), channel_id=1, source_target_pairs={{0,1},{1,0},{2,3},{3,2},{4,5},{5,4},{6,7},{7,6},{8,9},{9,8},{10,11... | collective-permute-start | bytes 1769480 | tf_op jit(solution)/shard_map/ppermute | solution.py:226
